TPU v7x, 256 devices: a whole 4x4x8 slice. The times are simulated.
256 devices in a mesh: dp: 64 (over z, x, core), tensor: 4 (over y).
Axes of the slice: x: 4, y: 4, z: 8, core: 2. Of those that a mesh axis runs over, the one named last changes fastest.
Arguments:
- grads: bfloat16 [64, 160, 28672], P('dp', None, 'tensor'), may hold values from -336000 to 336000, as said below
- error: bfloat16 [64, 160, 28672], P('dp', None, 'tensor'), may hold values from -0.8984375 to 0.8984375
- q_init: float32 [28672, 64], P('tensor'), may hold values from -6 to 6
Outputs:
- p_factor: float32 [160, 64], replicated
- q_factor: float32 [28672, 64], P('tensor')
- new_error: float32 [64, 160, 28672], P('dp', None, 'tensor')
Inputs may be any that keep to these rules, and one draw needn't show every extreme that they name: `grads`: entries of the gradients; each replica's gradient has its own overall scale.
All inputs are finite; a program needn't handle non-finite values.
Results may differ from a plain program's by a relative error of at most 0.0025.
The roundings to bfloat16 on the way count: a program that leaves them out, or rounds other values in their place, can miss the bound.
Values may be sent and summed in bfloat16 or wider, within the bound.
No kernel may reach another device: no remote copies, remote signals or barrier semaphores. Data moves between devices by JAX's collectives and lax.ppermute only.
A program may use at most 64 MiB of HBM per device.

v0:
```python
import jax
import jax.numpy as jnp
from jax import lax
from jax.sharding import Mesh
from jax.sharding import PartitionSpec as P

ROWS = 160
COLS = 28672
ITERS = 2
DP = ("dp_0", "dp_1", "dp_2")


epsilon = 1e-06
clip_ratio = 0.5


def rows_for(lines, devices):
    spare = -len(lines) % devices
    return jnp.pad(lines, [(0, spare)] + [(0, 0)] * (lines.ndim - 1))


def from_everyone(shard, axis):
    devices = lax.axis_size(axis)
    return lax.all_to_all(
        jnp.broadcast_to(shard[None], (devices, *shard.shape)), axis, 0, 0, tiled=True
    )


def joined_along(blocks, dim):
    shape = list(blocks.shape[1:])
    shape[dim] *= blocks.shape[0]
    return jnp.moveaxis(blocks, 0, dim).reshape(shape)


def gather_axes(shard, axes, dim):
    far, near = axes
    blocks = from_everyone(from_everyone(shard, far), near)
    return joined_along(blocks.swapaxes(0, 1).reshape(-1, *shard.shape), dim)


def split_up(shard, dim, devices):
    before, after = (shard.shape[:dim], shard.shape[dim + 1 :])
    return jnp.moveaxis(shard.reshape(*before, devices, -1, *after), dim, 0)


def sent_and_summed(shard, axis, dim):
    blocks = split_up(shard, dim, lax.axis_size(axis))
    arrived = lax.all_to_all(blocks, axis, split_axis=0, concat_axis=0, tiled=True)
    return arrived.sum(axis=0)


def summed_rows(shard, axes, dim):
    far, near = axes
    own = sent_and_summed(split_up(shard, dim, lax.axis_size(far)), near, dim + 1)
    return jnp.sum(lax.all_to_all(own, far, 0, 0, tiled=True), axis=0)


def nested_sum(shard, axes):
    padded = rows_for(shard, lax.axis_size(axes[0]) * lax.axis_size(axes[1]))
    whole = gather_axes(summed_rows(padded, axes, 0), axes, 0)
    return lax.slice_in_dim(whole, 0, len(shard)).reshape(shard.shape)


def in_one(arrays, axis):
    flat, at, done = (jnp.concatenate([a.reshape(-1) for a in arrays]), 0, [])
    subtotal = nested_sum(flat, axis)
    for a in arrays:
        done.append(subtotal[at : at + a.size].reshape(a.shape))
        at += a.size
    return tuple(done)


def collect(shard, axis, dim):
    blocks = from_everyone(shard, axis)
    return joined_along(blocks, dim)


def orthonormal(matrix):
    rank_width = matrix.shape[1]
    columns = lax.broadcasted_iota(jnp.int32, (1, rank_width), 1)

    def sweep_col(position, vectors):
        position = position.astype(jnp.int32)
        column = lax.dynamic_slice_in_dim(vectors, position, 1, 1)
        column = column * lax.rsqrt(jnp.sum(column * column) + epsilon)
        vectors = lax.dynamic_update_slice_in_dim(vectors, column, position, 1)
        coeffs = jnp.dot(column.T, vectors, precision=lax.Precision.HIGHEST)
        coeffs = jnp.where(columns > position, coeffs, jnp.zeros_like(coeffs))
        return vectors - jnp.dot(column, coeffs, precision=lax.Precision.HIGHEST)

    return lax.fori_loop(jnp.int32(0), jnp.int32(rank_width), sweep_col, matrix)


def replica_sum(statistic, blocks):
    return in_one((statistic, blocks), (("dp_0", "dp_1"), ("dp_2", "tensor")))


def shrink_of(sum_squares, replicas):
    scaled = clip_ratio * jnp.sqrt(jnp.float32(ROWS * COLS))
    return jnp.minimum(1.0, scaled * lax.rsqrt(sum_squares / replicas + epsilon))


def local(grads, error, q_init):
    gradient = grads[0]
    residue = error[0]
    replicas = lax.axis_size(DP)
    local_squares = jnp.sum(jnp.square(gradient.astype(jnp.float32)))
    q_half = q_init.astype(jnp.bfloat16)
    first_left = None
    grad_term = jnp.dot(gradient, q_half, preferred_element_type=jnp.float32)
    error_term = jnp.dot(residue, q_half, preferred_element_type=jnp.float32)
    sum_squares, partials = replica_sum(local_squares, jnp.stack([grad_term, error_term]))
    shrink = shrink_of(sum_squares, replicas)
    first_left = shrink * partials[0] + partials[1]
    merged = shrink * gradient.astype(jnp.float32) + residue.astype(jnp.float32)
    q_full = q_init
    p_hat = None
    for sweep in range(ITERS):
        if sweep == 0 and first_left is not None:
            left_sum = first_left
        else:
            partial_value = jnp.dot(
                merged, q_half.astype(jnp.float32), precision=lax.Precision.HIGHEST
            )
            unused, stacked = replica_sum(jnp.zeros((), jnp.float32), partial_value[None])
            left_sum = stacked[0]
        p_hat = orthonormal(left_sum)
        p_wide = p_hat.astype(jnp.bfloat16).astype(jnp.float32)
        q_partial = lax.dot_general(
            merged, p_wide, (((0,), (0,)), ((), ())), precision=lax.Precision.HIGHEST
        )
        share = summed_rows(q_partial, (("dp_0", "dp_1"), "dp_2"), 0) / replicas
        if sweep + 1 < ITERS:
            q_half = collect(share.astype(jnp.bfloat16), DP, 0)
        else:
            q_full = gather_axes(share, (("dp_0", "dp_1"), "dp_2"), 0)
            q_half = q_full.astype(jnp.bfloat16)
    p_half = p_hat.astype(jnp.bfloat16)
    approx = lax.dot_general(
        p_half, q_half, (((1,), (1,)), ((), ())), preferred_element_type=jnp.float32
    )
    new_error = merged - approx
    return (p_hat, q_full, new_error[None])


def solution(mesh):
    finer = Mesh(
        mesh.devices.reshape(8, 4, 2, mesh.shape["tensor"]), ("dp_0", "dp_1", "dp_2", "tensor")
    )
    return jax.shard_map(
        local,
        mesh=finer,
        in_specs=(P(DP, None, "tensor"), P(DP, None, "tensor"), P("tensor", None)),
        out_specs=(P(), P("tensor", None), P(DP, None, "tensor")),
        check_vma=False,
    )
```

profile of v0, /device:TPU:1, one launch (start us, length us, event | category | flops | bytes accessed | tf_op | source)
XLA Modules:
  0.0 537.5 jit_solution(9836133322419507810)
XLA Ops:
  0.6 3.6 fusion.11
  4.2 2.5 fusion.31
  7.0 0.9 fusion.34
  8.1 0.7 select_maximum_fusion
  9.1 10.9 %all_to_all.85 = f32[8,32,81]{2,1,0:T(8,128)S(1)} all-to-all(f32[8,32,81]{2,1,0:T(8,128)S(1)} %copy.33), channel_id=1, replica_groups=mesh['dp_0'=8,'dp_1'=4,'dp_2'=2,'tensor'=4] {'dp_2','tensor'}, dimensions={0} | all-to-all | bytes 165888 | tf_op jit(solution)/shard_map/all_to_all | solution.py:48
  20.0 19.4 %all_to_all.86 = f32[32,1,81]{2,1,0:T(1,128)S(1)} all-to-all(f32[32,1,81]{2,1,0:T(1,128)S(1)} %bitcast.103), channel_id=1, replica_groups=mesh['dp_0'=8,'dp_1'=4,'dp_2'=2,'tensor'=4] {'dp_0','dp_1'}, dimensions={0} | all-to-all | bytes 20736 | tf_op jit(solution)/shard_map/all_to_all | solution.py:55
  39.5 11.6 %all_to_all.87 = f32[32,1,81]{2,1,0:T(1,128)S(1)} all-to-all(f32[32,1,81]{2,1,0:T(1,128)S(1)} %broadcast_in_dim.20), channel_id=1, replica_groups=mesh['dp_0'=8,'dp_1'=4,'dp_2'=2,'tensor'=4] {'dp_0','dp_1'}, dimensions={0} | all-to-all | bytes 20736 | tf_op jit(solution)/shard_map/all_to_all | solution.py:24
  51.1 0.7 broadcast_in_dim.22
  51.8 6.3 %all-to-all-start.3 = ((f32[8,32,81]{2,1,0:T(8,128)}), f32[8,32,81]{2,1,0:T(8,128)S(1)}, u32[]{:S(2)}, u32[]{:S(2)}) async-start(f32[8,32,81]{2,1,0:T(8,128)} %broadcast_in_dim.22), calls=%async_computation.3 | async-start | bytes 262144 | tf_op jit(solution)/shard_map/all_to_all | solution.py:24
  58.1 5.2 all-to-all-done.3
  64.8 4.5 fusion.19
  69.5 105.3 %while.22 = (s32[]{:T(128)}, f32[160,64]{0,1:T(8,128)S(1)}, s32[]{:T(128)}, f32[]{:T(128)}, s32[]{:T(128)}) while((s32[]{:T(128)}, f32[160,64]{0,1:T(8,128)S(1)}, s32[]{:T(128)}, f32[]{:T(128)}, s32[]{:T(128)}) %tuple.48), condition=%wide.region_5.6_spmd.clone, body=%wide.region_3.5_spmd.clone.sunk | while | flops 143970 | bytes 127985 | solution.py:91
  69.5 0.6 multiply_reduce_fusion.4
  71.1 0.6 multiply_reduce_fusion.4
  72.8 0.6 multiply_reduce_fusion.4
  74.4 0.6 multiply_reduce_fusion.4
  76.1 0.6 multiply_reduce_fusion.4
  77.7 0.6 multiply_reduce_fusion.4
  79.4 0.6 multiply_reduce_fusion.4
  81.0 0.6 multiply_reduce_fusion.4
  82.6 0.6 multiply_reduce_fusion.4
  84.3 0.6 multiply_reduce_fusion.4
  85.9 0.6 multiply_reduce_fusion.4
  87.6 0.6 multiply_reduce_fusion.4
  89.2 0.6 multiply_reduce_fusion.4
  90.9 0.6 multiply_reduce_fusion.4
  92.5 0.6 multiply_reduce_fusion.4
  94.2 0.6 multiply_reduce_fusion.4
  95.8 0.6 multiply_reduce_fusion.4
  97.4 0.6 multiply_reduce_fusion.4
  112.2 0.6 multiply_reduce_fusion.4
  143.5 0.6 multiply_reduce_fusion.4
  174.7 13.5 %dot_general.45 = f32[32,2,112,160]{2,1,0,3:T(2,128)} reshape(f32[7168,160]{0,1:T(8,128)} %fusion.19) | data formatting | bytes 9175040 | tf_op jit(solution)/shard_map/dot_general | solution.py:129
  188.2 7.3 %fusion.25 = f32[2,32,112,64]{2,3,0,1:T(8,128)S(1)} fusion(f32[32,2,112,160]{2,1,0,3:T(2,128)} %dot_general.45, f32[160,64]{0,1:T(8,128)S(1)} %get-tuple-element.37), kind=kOutput, calls=%fused_computation.34 | convolution fusion | flops 880814080 | bytes 6463488 | tf_op jit(solution)/shard_map/dot_general | solution.py:129
  195.7 6.4 %all_to_all.88 = f32[2,32,112,64]{2,3,1,0:T(8,128)} all-to-all(f32[2,32,112,64]{2,3,1,0:T(8,128)S(1)} %copy.37), channel_id=1, replica_groups=mesh['dp_0'=8,'dp_1'=4,'dp_2'=2,'tensor'=4] {'dp_2'}, dimensions={0} | all-to-all | bytes 3670016 | tf_op jit(solution)/shard_map/all_to_all | solution.py:48
  202.0 2.0 reduce_sum.102
  204.0 31.0 %all_to_all.89 = f32[32,112,64]{1,2,0:T(8,128)} all-to-all(f32[32,112,64]{1,2,0:T(8,128)S(1)} %reduce_sum.102), channel_id=1, replica_groups=mesh['dp_0'=8,'dp_1'=4,'dp_2'=2,'tensor'=4] {'dp_0','dp_1'}, dimensions={0} | all-to-all | bytes 1835008 | tf_op jit(solution)/shard_map/all_to_all | solution.py:55
  235.0 1.3 reduce_sum.103
  236.6 35.5 %all_to_all.90 = bf16[64,112,64]{1,2,0:T(8,128)(2,1)S(1)} all-to-all(bf16[64,112,64]{1,2,0:T(8,128)(2,1)S(1)} %broadcast_in_dim.23), channel_id=1, replica_groups=mesh['dp_0'=8,'dp_1'=4,'dp_2'=2,'tensor'=4] {'dp_0','dp_1','dp_2'}, dimensions={0} | all-to-all | bytes 1835008 | tf_op jit(solution)/shard_map/all_to_all | solution.py:24
  272.1 0.7 copy.39
  272.8 3.2 reshape.94
  276.0 4.5 fusion.13
  281.1 8.8 %all_to_all.91 = f32[8,1,1312]{2,1,0:T(1,128)S(1)} all-to-all(f32[8,1,1312]{2,1,0:T(1,128)S(1)} %reshape.105), channel_id=1, replica_groups=mesh['dp_0'=8,'dp_1'=4,'dp_2'=2,'tensor'=4] {'dp_2','tensor'}, dimensions={0} | all-to-all | bytes 83968 | tf_op jit(solution)/shard_map/all_to_all | solution.py:48
  290.5 0.7 reduce.2
  291.4 13.1 %all_to_all.92 = f32[32,1,41]{2,1,0:T(1,128)S(1)} all-to-all(f32[32,1,41]{2,1,0:T(1,128)S(1)} %bitcast.105), channel_id=1, replica_groups=mesh['dp_0'=8,'dp_1'=4,'dp_2'=2,'tensor'=4] {'dp_0','dp_1'}, dimensions={0} | all-to-all | bytes 10496 | tf_op jit(solution)/shard_map/all_to_all | solution.py:55
  304.6 11.6 %all_to_all.93 = f32[32,1,41]{2,1,0:T(1,128)S(1)} all-to-all(f32[32,1,41]{2,1,0:T(1,128)S(1)} %broadcast_in_dim.24), channel_id=1, replica_groups=mesh['dp_0'=8,'dp_1'=4,'dp_2'=2,'tensor'=4] {'dp_0','dp_1'}, dimensions={0} | all-to-all | bytes 10496 | tf_op jit(solution)/shard_map/all_to_all | solution.py:24
  316.2 0.8 reshape.107
  317.0 6.2 %all-to-all-start.10 = ((f32[8,1,1312]{2,1,0:T(1,128)}), f32[8,1,1312]{2,1,0:T(1,128)S(1)}, u32[]{:S(2)}, u32[]{:S(2)}) async-start(f32[8,1,1312]{2,1,0:T(1,128)} %reshape.107), calls=%async_computation.10 | async-start | bytes 90112 | tf_op jit(solution)/shard_map/all_to_all | solution.py:24
  323.2 4.9 all-to-all-done.10
  328.1 0.7 reduce.3
  329.6 105.3 %while.23 = (s32[]{:T(128)}, f32[160,64]{0,1:T(8,128)S(1)}, s32[]{:T(128)}, f32[]{:T(128)}, s32[]{:T(128)}) while((s32[]{:T(128)}, f32[160,64]{0,1:T(8,128)S(1)}, s32[]{:T(128)}, f32[]{:T(128)}, s32[]{:T(128)}) %tuple.51), condition=%wide.region_12.13_spmd.clone, body=%wide.region_10.12_spmd.clone.sunk | while | flops 143970 | bytes 127985 | solution.py:91
  352.6 0.6 multiply_reduce_fusion.5
  383.9 0.6 multiply_reduce_fusion.5
  415.1 0.6 multiply_reduce_fusion.5
  434.9 7.3 %fusion.28 = f32[2,32,112,64]{2,3,0,1:T(8,128)S(1)} fusion(f32[32,2,112,160]{2,1,0,3:T(2,128)} %dot_general.45, f32[160,64]{0,1:T(8,128)S(1)} %get-tuple-element.51), kind=kOutput, calls=%fused_computation.35 | convolution fusion | flops 880814080 | bytes 6463488 | tf_op jit(solution)/shard_map/dot_general | solution.py:129
  442.4 6.3 %all_to_all.94 = f32[2,32,112,64]{2,3,1,0:T(8,128)} all-to-all(f32[2,32,112,64]{2,3,1,0:T(8,128)S(1)} %copy.45), channel_id=1, replica_groups=mesh['dp_0'=8,'dp_1'=4,'dp_2'=2,'tensor'=4] {'dp_2'}, dimensions={0} | all-to-all | bytes 3670016 | tf_op jit(solution)/shard_map/all_to_all | solution.py:48
  448.7 2.9 reduce_sum.106
  451.6 31.1 %all_to_all.95 = f32[32,112,64]{1,2,0:T(8,128)S(1)} all-to-all(f32[32,112,64]{1,2,0:T(8,128)} %reduce_sum.106), channel_id=1, replica_groups=mesh['dp_0'=8,'dp_1'=4,'dp_2'=2,'tensor'=4] {'dp_0','dp_1'}, dimensions={0} | all-to-all | bytes 1835008 | tf_op jit(solution)/shard_map/all_to_all | solution.py:55
  483.0 31.4 %all_to_all.96 = f32[32,112,64]{1,2,0:T(8,128)S(1)} all-to-all(f32[32,112,64]{1,2,0:T(8,128)S(1)} %broadcast_in_dim.27), channel_id=1, replica_groups=mesh['dp_0'=8,'dp_1'=4,'dp_2'=2,'tensor'=4] {'dp_0','dp_1'}, dimensions={0} | all-to-all | bytes 1835008 | tf_op jit(solution)/shard_map/all_to_all | solution.py:24
  514.4 0.6 copy.47
  515.3 8.3 %all_to_all.97 = f32[2,32,112,64]{2,1,3,0:T(8,128)S(1)} all-to-all(f32[2,32,112,64]{2,1,3,0:T(8,128)S(1)} %broadcast_in_dim.28), channel_id=1, replica_groups=mesh['dp_0'=8,'dp_1'=4,'dp_2'=2,'tensor'=4] {'dp_2'}, dimensions={0} | all-to-all | bytes 3670016 | tf_op jit(solution)/shard_map/all_to_all | solution.py:24
  523.6 3.2 copy.48
  526.9 5.3 reshape_reshape.21
  532.2 5.3 fusion.6
  (664 shorter events, 108.2 us)
Async XLA Ops:
  0.6 3.6 copy-start
  4.2 2.5 copy-start.1
  4.2 2.7 copy-start.3
  51.8 11.5 %all-to-all-start.3 = ((f32[8,32,81]{2,1,0:T(8,128)}), f32[8,32,81]{2,1,0:T(8,128)S(1)}, u32[]{:S(2)}, u32[]{:S(2)}) async-start(f32[8,32,81]{2,1,0:T(8,128)} %broadcast_in_dim.22), calls=%async_computation.3 | async-start | bytes 262144 | tf_op jit(solution)/shard_map/all_to_all | solution.py:24
  317.0 11.2 %all-to-all-start.10 = ((f32[8,1,1312]{2,1,0:T(1,128)}), f32[8,1,1312]{2,1,0:T(1,128)S(1)}, u32[]{:S(2)}, u32[]{:S(2)}) async-start(f32[8,1,1312]{2,1,0:T(1,128)} %reshape.107), calls=%async_computation.10 | async-start | bytes 90112 | tf_op jit(solution)/shard_map/all_to_all | solution.py:24
  434.9 97.3 %copy-start.2 = (f32[160,64]{0,1:T(8,128)}, f32[160,64]{0,1:T(8,128)S(1)}, u32[]{:S(2)}) copy-start(f32[160,64]{0,1:T(8,128)S(1)} %get-tuple-element.51) | copy-start | bytes 122884
where the time goes:
time: 541 us; the launch traced here: 537 us
  blocking collectives  226 us (42%)
  other arithmetic  111 us (21%)
  loops' own time  93.1 us (17%)
  matrix products  46 us (9%)
  local copies, waits for them, and re-layouts  37.8 us (7%)
  starting transfers between devices  12.5 us (2%)
  waiting for transfers between devices  10.1 us (2%)
    all_to_all x5, blocking collectives, from_everyone(): lax.all_to_all(jnp.broadcast_to(shard[None], (devices, *shard.shape)), ax...  98.4 us
    all_to_all x4, blocking collectives, summed_rows(): return jnp.sum(lax.all_to_all(own, far, 0, 0, tiled=True), axis=0)  94.7 us
    another operation x2, loops' own time, orthonormal(): return lax.fori_loop(jnp.int32(0), jnp.int32(rank_width), sweep_col, matrix)  93.1 us
    reduce_sum x128, other arithmetic, sweep_col(): column = column * lax.rsqrt(jnp.sum(column * column) + epsilon)  77.9 us
    all_to_all x4, blocking collectives, sent_and_summed(): lax.all_to_all(blocks, axis, split_axis=0, concat_axis=0, tiled=True)  32.5 us
    dot_general x128, matrix products, sweep_col(): coeffs = jnp.dot(column.T, vectors, precision=lax.Precision.HIGHEST)  18.1 us
    dot_general x2, matrix products, local(): lax.dot_general(merged, p_wide, (((0,), (0,)), ((), ())), precision=lax.P...  14.6 us
    sub x128, other arithmetic, sweep_col(): return vectors - jnp.dot(column, coeffs, precision=lax.Precision.HIGHEST)  14.3 us
  transfers between devices with their start and end apart: 2, of which 2 were waited for; matrix products, arithmetic and copies ran while one was open for 0% of the time, Pallas kernels for 0%

commit v1 on v0

v1 whole, which is shorter than its diff:
```python
import functools

import jax
import jax.numpy as jnp
from jax import lax
from jax.experimental import pallas as pl
from jax.experimental.pallas import tpu as pltpu
from jax.sharding import Mesh
from jax.sharding import PartitionSpec as P

ROWS = 160
COLS = 28672
RANK = 64
LOCAL = 7168
HALF = LOCAL // 2
QUARTER = HALF // 4
LANES = 128
BLOCKS = QUARTER // LANES
TAIL = ROWS - LANES
REPLICAS = 64
EPS = 1e-06
CLIP = 0.5

f32 = jnp.float32
bf16 = jnp.bfloat16
HIGHEST = lax.Precision.HIGHEST
VMEM = pltpu.VMEM


def whole():
    return pl.BlockSpec(memory_space=VMEM)


def shrink_of(squares):
    rows = jnp.sum(squares, axis=0)
    total = jnp.sum(jnp.sum(rows, axis=1, keepdims=True), axis=0, keepdims=True)
    scaled = CLIP * jnp.sqrt(f32(ROWS * COLS))
    return jnp.minimum(1.0, scaled * lax.rsqrt(total / REPLICAS + EPS))


def prep_kernel(at, g, e, send, squares):
    step = pl.program_id(0)

    @pl.when(step == 0)
    def _():
        squares[...] = jnp.zeros_like(squares)

    def rows(i, total):
        block = g[0, pl.ds(i * 16, 16), :].astype(f32)
        block = block * block
        part = block[:8] + block[8:]
        for lane in range(0, part.shape[1], LANES):
            total = total + part[:, lane : lane + LANES]
        return total

    squares[...] += lax.fori_loop(0, ROWS // 16, rows, jnp.zeros((8, LANES), f32))

    @pl.when(step < 2)
    def _():
        send[0:ROWS, :] = g[0]
        send[ROWS:, :] = e[0]


def prep(at, grads, error):
    width = HALF // 2
    mine = lambda i, at: (0, 0, jnp.where(i < 2, (1 - at[0]) * 2 + i, at[0] * 2 + i - 2))
    theirs = lambda i, at: (0, 0, (1 - at[0]) * 2 + jnp.minimum(i, 1))
    return pl.pallas_call(
        prep_kernel,
        grid_spec=pltpu.PrefetchScalarGridSpec(
            num_scalar_prefetch=1,
            grid=(4,),
            in_specs=[pl.BlockSpec((1, ROWS, width), mine), pl.BlockSpec((1, ROWS, width), theirs)],
            out_specs=[
                pl.BlockSpec((2 * ROWS, width), lambda i, at: (0, jnp.minimum(i, 1))),
                pl.BlockSpec((8, LANES), lambda i, at: (0, 0)),
            ],
        ),
        out_shape=[
            jax.ShapeDtypeStruct((2 * ROWS, HALF), bf16),
            jax.ShapeDtypeStruct((8, LANES), f32),
        ],
        name="prep",
    )(at, grads, error)


def merge_kernel(at, g, e, got, squares, *outs):
    shrink = shrink_of(squares[...])
    for j, out in enumerate(outs):
        first = pl.multiple_of(lax.rem(at[1] + j, 4) * QUARTER, LANES)

        def rows(i, carry, out=out, first=first):
            here, cols = pl.ds(i * 16, 16), pl.ds(first, QUARTER)
            gradient = g[0, here, cols].astype(f32) + got[here, cols].astype(f32)
            residue = e[0, here, cols].astype(f32) + got[pl.ds(ROWS + i * 16, 16), cols].astype(f32)
            out[here, :] = shrink * gradient + residue
            return carry

        lax.fori_loop(0, ROWS // 16, rows, 0)


def merge(at, grads, error, got, squares):
    own = pl.BlockSpec((1, ROWS, HALF), lambda i, at: (0, 0, at[0]))
    return pl.pallas_call(
        merge_kernel,
        grid_spec=pltpu.PrefetchScalarGridSpec(
            num_scalar_prefetch=1,
            grid=(1,),
            in_specs=[
                own,
                own,
                pl.BlockSpec((2 * ROWS, HALF), lambda i, at: (0, 0)),
                pl.BlockSpec((8, 8, LANES), lambda i, at: (0, 0, 0)),
            ],
            out_specs=[pl.BlockSpec((ROWS, QUARTER), lambda i, at: (0, 0))] * 4,
        ),
        out_shape=[jax.ShapeDtypeStruct((ROWS, QUARTER), f32)] * 4,
        name="merge",
    )(at, grads, error, got, squares)


def fold_kernel(a, b, c, d, out):
    for k in range(BLOCKS):
        cols = slice(k * LANES, (k + 1) * LANES)
        out[k] = (a[:, cols] + c[:, cols]) + (b[:, cols] + d[:, cols])
    out[BLOCKS] = jnp.zeros((ROWS, LANES), f32)


def fold(parts):
    return pl.pallas_call(
        fold_kernel,
        in_specs=[whole()] * 4,
        out_specs=whole(),
        out_shape=jax.ShapeDtypeStruct((BLOCKS + 1, ROWS, LANES), f32),
        name="fold",
    )(*parts)


def dot(a, b):
    return jnp.dot(a, b, precision=HIGHEST, preferred_element_type=f32)


def dot_t(a, b):
    return lax.dot_general(
        a, b, (((1,), (1,)), ((), ())), precision=HIGHEST, preferred_element_type=f32
    )


def terms_kernel(at, pieces, q, total, pack):
    s = pieces[0]
    for k in range(1, BLOCKS + 1):
        s = s + pieces[k]
    total[...] = s
    head = s[:LANES]
    tail = s[LANES:]
    tail_full = jnp.concatenate([tail, jnp.zeros((LANES - TAIL, LANES), f32)], axis=0)
    q_half = q[...].astype(bf16).astype(f32)
    left_tail = dot_t(q_half, tail_full)
    corner = dot_t(tail, tail_full)
    packed_left = left_tail[0:16]
    packed_corner = corner[0:8]
    for j in range(1, 4):
        packed_left = packed_left + pltpu.roll(left_tail[16 * j : 16 * j + 16], 32 * j, 1)
        packed_corner = packed_corner + pltpu.roll(corner[8 * j : 8 * j + 8], 32 * j, 1)
    flat = jnp.concatenate(
        [
            dot_t(q_half, head),
            dot_t(head, head),
            dot_t(tail, head),
            packed_left,
            packed_corner,
            jnp.zeros((8, LANES), f32),
        ],
        axis=0,
    )
    for k in range(8):
        pack[k] = flat[32 * k : 32 * k + 32]


def terms(at, pieces, q_t):
    column = lambda i, at: (0, at[0] * 4 * BLOCKS + at[1] * BLOCKS + jnp.minimum(at[2], BLOCKS - 1))
    return pl.pallas_call(
        terms_kernel,
        grid_spec=pltpu.PrefetchScalarGridSpec(
            num_scalar_prefetch=1,
            grid=(1,),
            in_specs=[
                pl.BlockSpec((BLOCKS + 1, ROWS, LANES), lambda i, at: (0, 0, 0)),
                pl.BlockSpec((RANK, LANES), column),
            ],
            out_specs=[
                pl.BlockSpec((ROWS, LANES), lambda i, at: (0, 0)),
                pl.BlockSpec((8, 32, LANES), lambda i, at: (0, 0, 0)),
            ],
        ),
        out_shape=[
            jax.ShapeDtypeStruct((ROWS, LANES), f32),
            jax.ShapeDtypeStruct((8, 32, LANES), f32),
        ],
        name="terms",
    )(at, pieces, q_t)


def orthonormal(a, b):
    groups = RANK // 8
    a = [a[8 * i : 8 * i + 8] for i in range(groups)]
    b = [b[8 * i : 8 * i + 8] for i in range(groups)]
    place = lax.broadcasted_iota(jnp.int32, (8, 1), 0)
    for k in range(RANK):
        g, r = divmod(k, 8)
        row_a, row_b = a[g][r : r + 1], b[g][r : r + 1]
        dots = [
            jnp.sum(a[i] * row_a + b[i] * row_b, axis=1, keepdims=True) for i in range(g, groups)
        ]
        inverse = 1.0 / (dots[0][r : r + 1] + EPS)
        for i in range(g, groups):
            coeff = dots[i - g] * inverse
            if i == g:
                coeff = jnp.where(place > r, coeff, 0.0)
            a[i] = a[i] - coeff * row_a
            b[i] = b[i] - coeff * row_b
    for i in range(groups):
        scale = lax.rsqrt(jnp.sum(a[i] * a[i] + b[i] * b[i], axis=1, keepdims=True) + EPS)
        a[i] = a[i] * scale
        b[i] = b[i] * scale
    return jnp.concatenate(a, axis=0), jnp.concatenate(b, axis=0)


def factor_kernel(pack, s, p_t, p_half, q):
    lane = lax.broadcasted_iota(jnp.int32, (1, LANES), 1)
    keep = lane < TAIL

    def unpack(rows):
        parts = [jnp.where(keep, rows, 0.0)]
        for j in range(1, 4):
            parts.append(jnp.where(keep, pltpu.roll(rows, LANES - 32 * j, 1), 0.0))
        return jnp.concatenate(parts, axis=0)

    flat = jnp.concatenate([pack[k] for k in range(8)], axis=0)
    empty = jnp.zeros((LANES - TAIL, LANES), f32)
    first_a = flat[0:64]
    gram = flat[64 : 64 + LANES]
    gram_side = jnp.concatenate([flat[64 + LANES : 64 + ROWS], empty], axis=0)
    first_b = unpack(flat[224:240])
    gram_corner = jnp.concatenate([unpack(flat[240:248]), empty], axis=0)

    a, b = orthonormal(first_a, first_b)
    a = a.astype(bf16).astype(f32)
    b = b.astype(bf16).astype(f32)
    second_a = (dot(a, gram) + dot(b, gram_side)) * (1.0 / REPLICAS)
    second_b = (dot_t(a, gram_side) + dot(b, gram_corner)) * (1.0 / REPLICAS)
    a, b = orthonormal(second_a, second_b)
    p_t[:, 0:LANES] = a
    p_t[:, LANES:ROWS] = b[:, 0:TAIL]
    a = a.astype(bf16).astype(f32)
    b = b.astype(bf16).astype(f32)
    p_half[0:LANES, :] = a.T.astype(bf16)
    p_half[LANES:ROWS, :] = b.T[0:TAIL].astype(bf16)
    tail_full = jnp.concatenate([s[LANES:ROWS], empty], axis=0)
    q[...] = ((dot(a, s[0:LANES]) + dot(b, tail_full)) * (1.0 / REPLICAS)).astype(q.dtype)


def factor(pack, s):
    return pl.pallas_call(
        factor_kernel,
        in_specs=[whole()] * 2,
        out_specs=[whole()] * 3,
        out_shape=[
            jax.ShapeDtypeStruct((RANK, ROWS), f32),
            jax.ShapeDtypeStruct((ROWS, RANK), bf16),
            jax.ShapeDtypeStruct((RANK, LANES), bf16),
        ],
        name="factor",
    )(pack, s)


def finish_kernel(at, g, e, squares, p_half, *refs):
    parts, (out, q_t) = refs[:8], refs[8:]
    shrink = shrink_of(squares[...])
    for k in range(8):

        @pl.when(pl.program_id(0) == k)
        def _(part=parts[k]):
            for block in range(BLOCKS):
                cols = slice(block * LANES, (block + 1) * LANES)
                q = part[block]
                approx = jnp.dot(p_half[...], q, preferred_element_type=f32)
                merged = shrink * g[0, :, cols].astype(f32) + e[0, :, cols].astype(f32)
                out[0, :, cols] = merged - approx
                q_t[:, cols] = q.astype(f32)


def finish(at, grads, error, squares, p_half, parts):
    def column(i, at):
        core = jnp.where(i < 4, at[0], 1 - at[0])
        return core * 4 + lax.rem(at[1] + i, 4)

    tile = pl.BlockSpec((1, ROWS, QUARTER), lambda i, at: (0, 0, column(i, at)))
    return pl.pallas_call(
        finish_kernel,
        grid_spec=pltpu.PrefetchScalarGridSpec(
            num_scalar_prefetch=1,
            grid=(8,),
            in_specs=[
                tile,
                tile,
                pl.BlockSpec((8, 8, LANES), lambda i, at: (0, 0, 0)),
                pl.BlockSpec((ROWS, RANK), lambda i, at: (0, 0)),
            ]
            + [pl.BlockSpec((8, RANK, LANES), lambda i, at: (0, 0, 0))] * 8,
            out_specs=[tile, pl.BlockSpec((RANK, QUARTER), lambda i, at: (0, column(i, at)))],
        ),
        out_shape=[
            jax.ShapeDtypeStruct((1, ROWS, LOCAL), f32),
            jax.ShapeDtypeStruct((RANK, LOCAL), f32),
        ],
        name="finish",
    )(at, grads, error, squares, p_half, *parts)


def shifted(value, axis, by):
    n = lax.axis_size(axis)
    return lax.ppermute(value, axis, [(i, (i - by) % n) for i in range(n)])


def swap(value, axis):
    return lax.ppermute(value, axis, [(0, 1), (1, 0)])


def from_ring(value, axis):
    return [value] + [shifted(value, axis, j) for j in range(1, 4)]


def ring_sum(value, axis):
    a, b, c, d = from_ring(value, axis)
    return (a + c) + (b + d)


def exchange(blocks, axis):
    return lax.all_to_all(blocks, axis, 0, 0, tiled=True)


def everyone(value, axis, n):
    return exchange(jnp.broadcast_to(value[None], (n, *value.shape)), axis)


def local(grads, error, q_init):
    at = jnp.stack([lax.axis_index("c"), lax.axis_index("x"), lax.axis_index("z")]).astype(jnp.int32)
    send, squares = prep(at, grads, error)
    got = swap(send, "c")
    squares = squares + swap(squares, "c")
    squares = ring_sum(ring_sum(squares, "x"), "y")
    squares = everyone(squares, "z", 8)

    pieces = merge(at, grads, error, got, squares)
    pieces = [pieces[0]] + [shifted(pieces[j], "x", -j) for j in range(1, 4)]
    pieces = exchange(fold(pieces), "z")
    s, pack = terms(at, pieces, q_init.T)

    piece = jnp.sum(exchange(pack, ("c", "y")), axis=0)
    piece = ring_sum(piece, "x")
    piece = jnp.sum(everyone(piece, "z", 8), axis=0)
    pack = everyone(piece, ("c", "y"), 8)

    p_t, p_half, q = factor(pack, s)
    parts = from_ring(everyone(q, "z", 8), "x")
    parts = parts + [swap(part, "c") for part in parts]
    new_error, q_t = finish(at, grads, error, squares, p_half, parts)
    return p_t.T, q_t.T, new_error


def solution(mesh):
    finer = Mesh(
        mesh.devices.reshape(8, 4, 2, mesh.shape["tensor"]), ("z", "x", "c", "y")
    )
    replicas = ("z", "x", "c")
    return jax.shard_map(
        local,
        mesh=finer,
        in_specs=(P(replicas, None, "y"), P(replicas, None, "y"), P("y", None)),
        out_specs=(P(), P("y", None), P(replicas, None, "y")),
        check_vma=False,
    )
```

time: 541 us -> 194 us (0.36)
  blocking collectives: 226 us -> 79.5 us
  other arithmetic: 111 us -> 1.39 us
  loops' own time: 93.1 us -> 0 us
  matrix products: 46 us -> 0 us
  Pallas kernels: 0 us -> 39.7 us
  local copies, waits for them, and re-layouts: 37.8 us -> 3.61 us
  waiting for transfers between devices: 10.1 us -> 40.8 us
  starting transfers between devices: 12.5 us -> 27.2 us
    all_to_all x13 -> x6, blocking collectives: 226 us -> 79.5 us  [exchange(): return lax.all_to_all(blocks, axis, 0, 0, tiled=True)]
    another operation x2 -> x0, loops' own time: 93.1 us -> none  [orthonormal(): return lax.fori_loop(jnp.int32(0), jnp.int32(rank_width), sweep_col, matrix)]
    reduce_sum x137 -> x2, other arithmetic: 87.9 us -> 0.03 us  [the longest x1 0.01 us: local(): piece = jnp.sum(exchange(pack, ('c', 'y')), axis=0)]
    dot_general x134 -> x0, matrix products: 46 us -> none  [the longest x128 18.1 us: sweep_col(): coeffs = jnp.dot(column.T, vectors, precision=lax.Precision.HIGHEST)]
    ppermute x0 -> x21, waiting for transfers between devices: none -> 40.8 us  [the longest x15 35.5 us: shifted(): return lax.ppermute(value, axis, [(i, (i - by) % n) for i in range(n)])]
    pallas_call x0 -> x6, Pallas kernels: none -> 39.7 us  [the longest x1 14.3 us: factor(): pl.pallas_call(factor_kernel, in_specs=[whole()] * 2, out_specs=[whole()]...]
    ppermute x0 -> x21, starting transfers between devices: none -> 27.2 us  [the longest x15 16.7 us: shifted(): return lax.ppermute(value, axis, [(i, (i - by) % n) for i in range(n)])]
    sub x128 -> x0, other arithmetic: 14.3 us -> none  [sweep_col(): return vectors - jnp.dot(column, coeffs, precision=lax.Precision.HIGHEST)]
  transfers between devices with their start and end apart: 2 -> 21, of which waited for: 2 -> 12; matrix products, arithmetic and copies ran while one was open for 0% -> 0% of each run, Pallas kernels for 0% -> 0%
where the time goes in v1:
time: 194 us; the launch traced here: 193 us
  blocking collectives  79.5 us (41%)
  waiting for transfers between devices  40.8 us (21%)
  Pallas kernels  39.7 us (20%)
  starting transfers between devices  27.2 us (14%)
  local copies, waits for them, and re-layouts  3.61 us (2%)
    all_to_all x6, blocking collectives, exchange(): return lax.all_to_all(blocks, axis, 0, 0, tiled=True)  79.5 us
    ppermute x15, waiting for transfers between devices, shifted(): return lax.ppermute(value, axis, [(i, (i - by) % n) for i in range(n)])  35.5 us
    ppermute x15, starting transfers between devices, shifted(): return lax.ppermute(value, axis, [(i, (i - by) % n) for i in range(n)])  16.7 us
    pallas_call x1, Pallas kernels, factor(): pl.pallas_call(factor_kernel, in_specs=[whole()] * 2, out_specs=[whole()]...  14.3 us
    ppermute x6, starting transfers between devices, swap(): return lax.ppermute(value, axis, [(0, 1), (1, 0)])  10.5 us
    pallas_call x1, Pallas kernels, finish(): pl.pallas_call(finish_kernel, grid_spec=pltpu.PrefetchScalarGridSpec(num_...  9.12 us
    pallas_call x1, Pallas kernels, prep(): pl.pallas_call(prep_kernel, grid_spec=pltpu.PrefetchScalarGridSpec(num_sc...  5.49 us
    pallas_call x1, Pallas kernels, merge(): pl.pallas_call(merge_kernel, grid_spec=pltpu.PrefetchScalarGridSpec(num_s...  5.36 us
  transfers between devices with their start and end apart: 21, of which 12 were waited for; matrix products, arithmetic and copies ran while one was open for 0% of the time, Pallas kernels for 0%

profile of v1, /device:TPU:1, one launch (start us, length us, event | category | flops | bytes accessed | tf_op | source)
XLA Modules:
  0.0 193.0 jit_solution(3248677942694638543)
XLA Ops:
  0.6 0.7 pad_add_fusion.at
  1.3 5.5 %prep.1 = (bf16[320,3584]{1,0:T(8,128)(2,1)}, f32[8,128]{1,0:T(8,128)}) custom-call(s32[3]{0:T(128)} %pad_add_fusion.at, bf16[1,160,7168]{2,1,0:T(8,128)(2,1)} %g.5, bf16[1,160,7168]{2,1,0:T(8,128)(2,1)} %e.5), custom_call_target="tpu_custom_call" | custom-call | tf_op jit(solution)/shard_map/prep/pallas_call | solution.py:68
  6.8 3.2 %collective-permute-start = (bf16[320,3584]{1,0:T(8,128)(2,1)}, bf16[320,3584]{1,0:T(8,128)(2,1)S(1)}, u32[]{:S(2)}, u32[]{:S(2)}) collective-permute-start(bf16[320,3584]{1,0:T(8,128)(2,1)} %get-tuple-element.16), channel_id=1, source_target_pairs={{0,4},{4,0},{1,5},{5,1},{2,6},{6,2},{3,7},{7,3},{8,12},{12,8},{9,1... | collective-permute-start | bytes 6881288 | tf_op jit(solution)/shard_map/ppermute | solution.py:327
  10.0 0.0 collective-permute-start.1
  10.0 4.3 %collective-permute-done.1 = f32[8,128]{1,0:T(8,128)S(1)} collective-permute-done((f32[8,128]{1,0:T(8,128)}, f32[8,128]{1,0:T(8,128)S(1)}, u32[]{:S(2)}, u32[]{:S(2)}) %collective-permute-start.1) | collective-permute-done | bytes 4128 | tf_op jit(solution)/shard_map/ppermute | solution.py:327
  14.3 0.7 add.30
  15.0 0.0 collective-permute-start.4
  15.0 2.7 %collective-permute-start.3 = (f32[8,128]{1,0:T(8,128)S(1)}, f32[8,128]{1,0:T(8,128)S(1)}, u32[]{:S(2)}, u32[]{:S(2)}) collective-permute-start(f32[8,128]{1,0:T(8,128)S(1)} %add.30), channel_id=1, source_target_pairs={{0,24},{8,0},{16,8},{24,16},{1,25},{9,1},{17,9},{25,17},{2,26},{10... | collective-permute-start | bytes 12296 | tf_op jit(solution)/shard_map/ppermute | solution.py:323
  17.6 0.0 collective-permute-start.2
  17.6 1.0 collective-permute-done.4
  18.6 0.0 collective-permute-done.3
  18.6 3.0 %collective-permute-done.2 = f32[8,128]{1,0:T(8,128)S(1)} collective-permute-done((f32[8,128]{1,0:T(8,128)S(1)}, f32[8,128]{1,0:T(8,128)S(1)}, u32[]{:S(2)}, u32[]{:S(2)}) %collective-permute-start.2) | collective-permute-done | bytes 4128 | tf_op jit(solution)/shard_map/ppermute | solution.py:323
  21.6 0.0 collective-permute-start.7
  21.6 2.7 %collective-permute-start.6 = (f32[8,128]{1,0:T(8,128)S(1)}, f32[8,128]{1,0:T(8,128)S(1)}, u32[]{:S(2)}, u32[]{:S(2)}) collective-permute-start(f32[8,128]{1,0:T(8,128)S(1)} %add_add_fusion.2), channel_id=1, source_target_pairs={{0,3},{1,0},{2,1},{3,2},{4,7},{5,4},{6,5},{7,6},{8,11},{9,8},{10,9... | collective-permute-start | bytes 12296 | tf_op jit(solution)/shard_map/ppermute | solution.py:323
  24.3 0.0 collective-permute-start.5
  24.3 1.0 collective-permute-done.7
  25.3 0.0 collective-permute-done.6
  25.3 3.0 %collective-permute-done.5 = f32[8,128]{1,0:T(8,128)S(1)} collective-permute-done((f32[8,128]{1,0:T(8,128)S(1)}, f32[8,128]{1,0:T(8,128)S(1)}, u32[]{:S(2)}, u32[]{:S(2)}) %collective-permute-start.5) | collective-permute-done | bytes 4128 | tf_op jit(solution)/shard_map/ppermute | solution.py:323
  28.3 13.4 %all_to_all.30.squares = f32[8,8,128]{2,1,0:T(8,128)} all-to-all(f32[8,8,128]{2,1,0:T(8,128)S(1)} %broadcast_in_dim.8), channel_id=1, replica_groups=mesh['z'=8,'x'=4,'c'=2,'y'=4] {'z'}, dimensions={0} | all-to-all | bytes 65536 | tf_op jit(solution)/shard_map/all_to_all | solution.py:340
  41.7 0.0 collective-permute-done.got
  41.7 1.4 copy-done
  43.0 5.4 %merge.1 = (f32[160,896]{1,0:T(8,128)}, f32[160,896]{1,0:T(8,128)}, f32[160,896]{1,0:T(8,128)}, f32[160,896]{1,0:T(8,128)}) custom-call(s32[3]{0:T(128)} %pad_add_fusion.at, bf16[1,160,7168]{2,1,0:T(8,128)(2,1)} %g.5, bf16[1,160,7168]{2,1,0:T(8,128)(2,1)} %e.5, bf16[320,3584]{1,0:T(8,128)(2,1)} %copy-done, f32[8,8,128]{2,1,0:T(8,128)} %all_to_all.30.squares), custom_call_target="tpu_custom_call" | custom-call | tf_op jit(solution)/shard_map/merge/pallas_call | solution.py:104
  48.4 0.0 collective-permute-start.8
  48.4 2.4 %collective-permute-start.9 = (f32[160,896]{1,0:T(8,128)}, f32[160,896]{1,0:T(8,128)S(1)}, u32[]{:S(2)}, u32[]{:S(2)}) collective-permute-start(f32[160,896]{1,0:T(8,128)} %get-tuple-element.20), channel_id=1, source_target_pairs={{0,16},{8,24},{16,0},{24,8},{1,17},{9,25},{17,1},{25,9},{2,18},{10... | collective-permute-start | bytes 1720328 | tf_op jit(solution)/shard_map/ppermute | solution.py:323
  50.9 1.2 collective-permute-start.10
  52.0 7.5 %collective-permute-done.8.b = f32[160,896]{1,0:T(8,128)S(1)} collective-permute-done((f32[160,896]{1,0:T(8,128)}, f32[160,896]{1,0:T(8,128)S(1)}, u32[]{:S(2)}, u32[]{:S(2)}) %collective-permute-start.8) | collective-permute-done | bytes 573472 | tf_op jit(solution)/shard_map/ppermute | solution.py:323
  59.5 11.9 %collective-permute-done.9.c = f32[160,896]{1,0:T(8,128)S(1)} collective-permute-done((f32[160,896]{1,0:T(8,128)}, f32[160,896]{1,0:T(8,128)S(1)}, u32[]{:S(2)}, u32[]{:S(2)}) %collective-permute-start.9) | collective-permute-done | bytes 573472 | tf_op jit(solution)/shard_map/ppermute | solution.py:323
  71.4 5.3 %collective-permute-done.10.d = f32[160,896]{1,0:T(8,128)S(1)} collective-permute-done((f32[160,896]{1,0:T(8,128)}, f32[160,896]{1,0:T(8,128)S(1)}, u32[]{:S(2)}, u32[]{:S(2)}) %collective-permute-start.10) | collective-permute-done | bytes 573472 | tf_op jit(solution)/shard_map/ppermute | solution.py:323
  76.6 0.8 copy-done.3
  77.5 2.5 %fold.1 = f32[8,160,128]{2,1,0:T(8,128)} custom-call(f32[160,896]{1,0:T(8,128)} %get-tuple-element.18.a, f32[160,896]{1,0:T(8,128)} %copy-done.1, f32[160,896]{1,0:T(8,128)} %copy-done.2, f32[160,896]{1,0:T(8,128)} %copy-done.3), custom_call_target="tpu_custom_call" | custom-call | tf_op jit(solution)/shard_map/fold/pallas_call | solution.py:130
  80.0 23.1 %all_to_all.31.pieces = f32[8,160,128]{2,1,0:T(8,128)} all-to-all(f32[8,160,128]{2,1,0:T(8,128)} %fold.1), channel_id=1, replica_groups=mesh['z'=8,'x'=4,'c'=2,'y'=4] {'z'}, dimensions={0} | all-to-all | bytes 1310720 | tf_op jit(solution)/shard_map/all_to_all | solution.py:340
  103.1 2.9 %terms.1 = (f32[160,128]{1,0:T(8,128)}, f32[8,32,128]{2,1,0:T(8,128)}) custom-call(s32[3]{0:T(128)} %pad_add_fusion.at, f32[8,160,128]{2,1,0:T(8,128)} %all_to_all.31.pieces, f32[64,7168]{1,0:T(8,128)} %bitcast.6), custom_call_target="tpu_custom_call" | custom-call | tf_op jit(solution)/shard_map/terms/pallas_call | solution.py:182
  106.0 10.8 %all_to_all.32 = f32[8,32,128]{2,1,0:T(8,128)S(1)} all-to-all(f32[8,32,128]{2,1,0:T(8,128)} %get-tuple-element.22), channel_id=1, replica_groups=mesh['z'=8,'x'=4,'c'=2,'y'=4] {'c','y'}, dimensions={0} | all-to-all | bytes 262144 | tf_op jit(solution)/shard_map/all_to_all | solution.py:340
  116.8 2.0 %collective-permute-start.13 = (f32[32,128]{1,0:T(8,128)S(1)}, f32[32,128]{1,0:T(8,128)S(1)}, u32[]{:S(2)}, u32[]{:S(2)}) collective-permute-start(f32[32,128]{1,0:T(8,128)S(1)} %reduce_sum.18), channel_id=1, source_target_pairs={{0,8},{8,16},{16,24},{24,0},{1,9},{9,17},{17,25},{25,1},{2,10},{10... | collective-permute-start | bytes 49160 | tf_op jit(solution)/shard_map/ppermute | solution.py:323
  118.8 1.5 collective-permute-start.12
  120.3 1.1 collective-permute-start.11
  121.4 0.0 collective-permute-done.13
  121.4 0.3 collective-permute-done.12
  121.7 2.7 %collective-permute-done.11 = f32[32,128]{1,0:T(8,128)S(1)} collective-permute-done((f32[32,128]{1,0:T(8,128)S(1)}, f32[32,128]{1,0:T(8,128)S(1)}, u32[]{:S(2)}, u32[]{:S(2)}) %collective-permute-start.11) | collective-permute-done | bytes 16416 | tf_op jit(solution)/shard_map/ppermute | solution.py:323
  124.4 10.3 %all_to_all.33 = f32[8,32,128]{2,1,0:T(8,128)S(1)} all-to-all(f32[8,32,128]{2,1,0:T(8,128)S(1)} %broadcast_in_dim.9), channel_id=1, replica_groups=mesh['z'=8,'x'=4,'c'=2,'y'=4] {'z'}, dimensions={0} | all-to-all | bytes 262144 | tf_op jit(solution)/shard_map/all_to_all | solution.py:340
  134.8 11.2 %all_to_all.34.pack = f32[8,32,128]{2,1,0:T(8,128)} all-to-all(f32[8,32,128]{2,1,0:T(8,128)S(1)} %broadcast_in_dim.10), channel_id=1, replica_groups=mesh['z'=8,'x'=4,'c'=2,'y'=4] {'c','y'}, dimensions={0} | all-to-all | bytes 262144 | tf_op jit(solution)/shard_map/all_to_all | solution.py:340
  146.0 14.3 %factor.1 = (f32[64,160]{1,0:T(8,128)}, bf16[160,64]{1,0:T(8,128)(2,1)}, bf16[64,128]{1,0:T(8,128)(2,1)}) custom-call(f32[8,32,128]{2,1,0:T(8,128)} %all_to_all.34.pack, f32[160,128]{1,0:T(8,128)} %get-tuple-element.23.s), custom_call_target="tpu_custom_call" | custom-call | tf_op jit(solution)/shard_map/factor/pallas_call | solution.py:264
  160.3 0.7 broadcast_in_dim.11
  161.0 10.7 %all_to_all.35.refs_0_ = bf16[8,64,128]{2,1,0:T(8,128)(2,1)S(1)} all-to-all(bf16[8,64,128]{2,1,0:T(8,128)(2,1)S(1)} %broadcast_in_dim.11), channel_id=1, replica_groups=mesh['z'=8,'x'=4,'c'=2,'y'=4] {'z'}, dimensions={0} | all-to-all | bytes 262144 | tf_op jit(solution)/shard_map/all_to_all | solution.py:340
  171.7 0.2 collective-permute-start.16
  172.0 2.6 %collective-permute-start.15 = (bf16[8,64,128]{2,1,0:T(8,128)(2,1)S(1)}, bf16[8,64,128]{2,1,0:T(8,128)(2,1)S(1)}, u32[]{:S(2)}, u32[]{:S(2)}) collective-permute-start(bf16[8,64,128]{2,1,0:T(8,128)(2,1)S(1)} %all_to_all.35.refs_0_), channel_id=1, source_target_pairs={{0,16},{8,24},{16,0},{24,8},{1,17},{9,25},{17,1},{25,9},{2,18},{10... | collective-permute-start | bytes 393224 | tf_op jit(solution)/shard_map/ppermute | solution.py:323
  174.6 0.3 collective-permute-start.14
  174.9 2.5 %collective-permute-start.17 = (bf16[8,64,128]{2,1,0:T(8,128)(2,1)S(1)}, bf16[8,64,128]{2,1,0:T(8,128)(2,1)S(1)}, u32[]{:S(2)}, u32[]{:S(2)}) collective-permute-start(bf16[8,64,128]{2,1,0:T(8,128)(2,1)S(1)} %all_to_all.35.refs_0_), channel_id=1, source_target_pairs={{0,4},{4,0},{1,5},{5,1},{2,6},{6,2},{3,7},{7,3},{8,12},{12,8},{9,1... | collective-permute-start | bytes 393224 | tf_op jit(solution)/shard_map/ppermute | solution.py:327
  177.4 0.0 collective-permute-done.16.refs_3_
  177.4 3.0 %collective-permute-start.20 = (bf16[8,64,128]{2,1,0:T(8,128)(2,1)S(1)}, bf16[8,64,128]{2,1,0:T(8,128)(2,1)S(1)}, u32[]{:S(2)}, u32[]{:S(2)}) collective-permute-start(bf16[8,64,128]{2,1,0:T(8,128)(2,1)S(1)} %collective-permute-done.16.refs_3_), channel_id=1, source_target_pairs={{0,4},{4,0},{1,5},{5,1},{2,6},{6,2},{3,7},{7,3},{8,12},{12,8},{9,1... | collective-permute-start | bytes 393224 | tf_op jit(solution)/shard_map/ppermute | solution.py:327
  180.4 0.0 collective-permute-done.15.refs_2_
  180.4 1.4 collective-permute-start.19
  181.8 0.0 collective-permute-done.14.refs_1_
  181.8 0.4 collective-permute-start.18
  182.2 0.0 collective-permute-done.17.refs_4_
  182.2 0.0 collective-permute-done.20.refs_7_
  182.2 0.0 copy-start.9
  182.2 0.6 collective-permute-done.19.refs_6_
  182.8 0.4 collective-permute-done.18.refs_5_
  183.2 0.0 copy-done.6
  183.2 0.0 copy-done.7
  183.3 0.2 copy-done.10
  183.5 0.4 copy-done.11
  183.9 9.1 %finish.1 = (f32[1,160,7168]{2,1,0:T(8,128)}, f32[64,7168]{1,0:T(8,128)}) custom-call(s32[3]{0:T(128)} %pad_add_fusion.at, bf16[1,160,7168]{2,1,0:T(8,128)(2,1)} %g.5, bf16[1,160,7168]{2,1,0:T(8,128)(2,1)} %e.5, f32[8,8,128]{2,1,0:T(8,128)} %all_to_all.30.squares, bf16[160,64]{1,0:T(8,128)(2,1)} %get-tuple-element.25.p_half, bf16[8,64,128]{2,1,0:T(8,128)(2,1)} %copy-done.4, ...), custom_call_target="tpu_custom_call" | custom-call | tf_op jit(solution)/shard_map/finish/pallas_call | solution.py:299
  (25 shorter events, 0.1 us)
Async XLA Ops:
  6.8 34.9 %collective-permute-start = (bf16[320,3584]{1,0:T(8,128)(2,1)}, bf16[320,3584]{1,0:T(8,128)(2,1)S(1)}, u32[]{:S(2)}, u32[]{:S(2)}) collective-permute-start(bf16[320,3584]{1,0:T(8,128)(2,1)} %get-tuple-element.16), channel_id=1, source_target_pairs={{0,4},{4,0},{1,5},{5,1},{2,6},{6,2},{3,7},{7,3},{8,12},{12,8},{9,1... | collective-permute-start | bytes 6881288 | tf_op jit(solution)/shard_map/ppermute | solution.py:327
  10.0 4.3 %collective-permute-start.1 = (f32[8,128]{1,0:T(8,128)}, f32[8,128]{1,0:T(8,128)S(1)}, u32[]{:S(2)}, u32[]{:S(2)}) collective-permute-start(f32[8,128]{1,0:T(8,128)} %get-tuple-element.17), channel_id=1, source_target_pairs={{0,4},{4,0},{1,5},{5,1},{2,6},{6,2},{3,7},{7,3},{8,12},{12,8},{9,1... | collective-permute-start | bytes 12296 | tf_op jit(solution)/shard_map/ppermute | solution.py:327
  15.0 3.7 %collective-permute-start.4 = (f32[8,128]{1,0:T(8,128)S(1)}, f32[8,128]{1,0:T(8,128)S(1)}, u32[]{:S(2)}, u32[]{:S(2)}) collective-permute-start(f32[8,128]{1,0:T(8,128)S(1)} %add.30), channel_id=1, source_target_pairs={{0,8},{8,16},{16,24},{24,0},{1,9},{9,17},{17,25},{25,1},{2,10},{10... | collective-permute-start | bytes 12296 | tf_op jit(solution)/shard_map/ppermute | solution.py:323
  15.0 3.7 %collective-permute-start.3 = (f32[8,128]{1,0:T(8,128)S(1)}, f32[8,128]{1,0:T(8,128)S(1)}, u32[]{:S(2)}, u32[]{:S(2)}) collective-permute-start(f32[8,128]{1,0:T(8,128)S(1)} %add.30), channel_id=1, source_target_pairs={{0,24},{8,0},{16,8},{24,16},{1,25},{9,1},{17,9},{25,17},{2,26},{10... | collective-permute-start | bytes 12296 | tf_op jit(solution)/shard_map/ppermute | solution.py:323
  17.6 4.0 %collective-permute-start.2 = (f32[8,128]{1,0:T(8,128)S(1)}, f32[8,128]{1,0:T(8,128)S(1)}, u32[]{:S(2)}, u32[]{:S(2)}) collective-permute-start(f32[8,128]{1,0:T(8,128)S(1)} %add.30), channel_id=1, source_target_pairs={{0,16},{8,24},{16,0},{24,8},{1,17},{9,25},{17,1},{25,9},{2,18},{10... | collective-permute-start | bytes 12296 | tf_op jit(solution)/shard_map/ppermute | solution.py:323
  21.6 3.7 %collective-permute-start.7 = (f32[8,128]{1,0:T(8,128)S(1)}, f32[8,128]{1,0:T(8,128)S(1)}, u32[]{:S(2)}, u32[]{:S(2)}) collective-permute-start(f32[8,128]{1,0:T(8,128)S(1)} %add_add_fusion.2), channel_id=1, source_target_pairs={{0,1},{1,2},{2,3},{3,0},{4,5},{5,6},{6,7},{7,4},{8,9},{9,10},{10,1... | collective-permute-start | bytes 12296 | tf_op jit(solution)/shard_map/ppermute | solution.py:323
  21.6 3.7 %collective-permute-start.6 = (f32[8,128]{1,0:T(8,128)S(1)}, f32[8,128]{1,0:T(8,128)S(1)}, u32[]{:S(2)}, u32[]{:S(2)}) collective-permute-start(f32[8,128]{1,0:T(8,128)S(1)} %add_add_fusion.2), channel_id=1, source_target_pairs={{0,3},{1,0},{2,1},{3,2},{4,7},{5,4},{6,5},{7,6},{8,11},{9,8},{10,9... | collective-permute-start | bytes 12296 | tf_op jit(solution)/shard_map/ppermute | solution.py:323
  24.3 4.0 %collective-permute-start.5 = (f32[8,128]{1,0:T(8,128)S(1)}, f32[8,128]{1,0:T(8,128)S(1)}, u32[]{:S(2)}, u32[]{:S(2)}) collective-permute-start(f32[8,128]{1,0:T(8,128)S(1)} %add_add_fusion.2), channel_id=1, source_target_pairs={{0,2},{1,3},{2,0},{3,1},{4,6},{5,7},{6,4},{7,5},{8,10},{9,11},{10,... | collective-permute-start | bytes 12296 | tf_op jit(solution)/shard_map/ppermute | solution.py:323
  41.7 1.4 copy-start
  48.4 11.1 %collective-permute-start.8 = (f32[160,896]{1,0:T(8,128)}, f32[160,896]{1,0:T(8,128)S(1)}, u32[]{:S(2)}, u32[]{:S(2)}) collective-permute-start(f32[160,896]{1,0:T(8,128)} %get-tuple-element.19), channel_id=1, source_target_pairs={{0,8},{8,16},{16,24},{24,0},{1,9},{9,17},{17,25},{25,1},{2,10},{10... | collective-permute-start | bytes 1720328 | tf_op jit(solution)/shard_map/ppermute | solution.py:323
  48.4 22.9 %collective-permute-start.9 = (f32[160,896]{1,0:T(8,128)}, f32[160,896]{1,0:T(8,128)S(1)}, u32[]{:S(2)}, u32[]{:S(2)}) collective-permute-start(f32[160,896]{1,0:T(8,128)} %get-tuple-element.20), channel_id=1, source_target_pairs={{0,16},{8,24},{16,0},{24,8},{1,17},{9,25},{17,1},{25,9},{2,18},{10... | collective-permute-start | bytes 1720328 | tf_op jit(solution)/shard_map/ppermute | solution.py:323
  50.9 25.8 %collective-permute-start.10 = (f32[160,896]{1,0:T(8,128)}, f32[160,896]{1,0:T(8,128)S(1)}, u32[]{:S(2)}, u32[]{:S(2)}) collective-permute-start(f32[160,896]{1,0:T(8,128)} %get-tuple-element.21), channel_id=1, source_target_pairs={{0,24},{8,0},{16,8},{24,16},{1,25},{9,1},{17,9},{25,17},{2,26},{10... | collective-permute-start | bytes 1720328 | tf_op jit(solution)/shard_map/ppermute | solution.py:323
  59.5 17.1 %copy-start.1 = (f32[160,896]{1,0:T(8,128)}, f32[160,896]{1,0:T(8,128)S(1)}, u32[]{:S(2)}) copy-start(f32[160,896]{1,0:T(8,128)S(1)} %collective-permute-done.8.b) | copy-start | bytes 1720324
  71.4 5.3 %copy-start.2 = (f32[160,896]{1,0:T(8,128)}, f32[160,896]{1,0:T(8,128)S(1)}, u32[]{:S(2)}) copy-start(f32[160,896]{1,0:T(8,128)S(1)} %collective-permute-done.9.c) | copy-start | bytes 1720324
  76.6 0.8 copy-start.3
  116.8 4.6 %collective-permute-start.13 = (f32[32,128]{1,0:T(8,128)S(1)}, f32[32,128]{1,0:T(8,128)S(1)}, u32[]{:S(2)}, u32[]{:S(2)}) collective-permute-start(f32[32,128]{1,0:T(8,128)S(1)} %reduce_sum.18), channel_id=1, source_target_pairs={{0,8},{8,16},{16,24},{24,0},{1,9},{9,17},{17,25},{25,1},{2,10},{10... | collective-permute-start | bytes 49160 | tf_op jit(solution)/shard_map/ppermute | solution.py:323
  118.8 2.9 %collective-permute-start.12 = (f32[32,128]{1,0:T(8,128)S(1)}, f32[32,128]{1,0:T(8,128)S(1)}, u32[]{:S(2)}, u32[]{:S(2)}) collective-permute-start(f32[32,128]{1,0:T(8,128)S(1)} %reduce_sum.18), channel_id=1, source_target_pairs={{0,24},{8,0},{16,8},{24,16},{1,25},{9,1},{17,9},{25,17},{2,26},{10... | collective-permute-start | bytes 49160 | tf_op jit(solution)/shard_map/ppermute | solution.py:323
  120.3 4.1 %collective-permute-start.11 = (f32[32,128]{1,0:T(8,128)S(1)}, f32[32,128]{1,0:T(8,128)S(1)}, u32[]{:S(2)}, u32[]{:S(2)}) collective-permute-start(f32[32,128]{1,0:T(8,128)S(1)} %reduce_sum.18), channel_id=1, source_target_pairs={{0,16},{8,24},{16,0},{24,8},{1,17},{9,25},{17,1},{25,9},{2,18},{10... | collective-permute-start | bytes 49160 | tf_op jit(solution)/shard_map/ppermute | solution.py:323
  171.7 11.5 %copy-start.4 = (bf16[8,64,128]{2,1,0:T(8,128)(2,1)}, bf16[8,64,128]{2,1,0:T(8,128)(2,1)S(1)}, u32[]{:S(2)}) copy-start(bf16[8,64,128]{2,1,0:T(8,128)(2,1)S(1)} %all_to_all.35.refs_0_) | copy-start | bytes 393220
  171.7 5.7 %collective-permute-start.16 = (bf16[8,64,128]{2,1,0:T(8,128)(2,1)S(1)}, bf16[8,64,128]{2,1,0:T(8,128)(2,1)S(1)}, u32[]{:S(2)}, u32[]{:S(2)}) collective-permute-start(bf16[8,64,128]{2,1,0:T(8,128)(2,1)S(1)} %all_to_all.35.refs_0_), channel_id=1, source_target_pairs={{0,8},{8,16},{16,24},{24,0},{1,9},{9,17},{17,25},{25,1},{2,10},{10... | collective-permute-start | bytes 393224 | tf_op jit(solution)/shard_map/ppermute | solution.py:323
  172.0 8.5 %collective-permute-start.15 = (bf16[8,64,128]{2,1,0:T(8,128)(2,1)S(1)}, bf16[8,64,128]{2,1,0:T(8,128)(2,1)S(1)}, u32[]{:S(2)}, u32[]{:S(2)}) collective-permute-start(bf16[8,64,128]{2,1,0:T(8,128)(2,1)S(1)} %all_to_all.35.refs_0_), channel_id=1, source_target_pairs={{0,16},{8,24},{16,0},{24,8},{1,17},{9,25},{17,1},{25,9},{2,18},{10... | collective-permute-start | bytes 393224 | tf_op jit(solution)/shard_map/ppermute | solution.py:323
  174.6 7.3 %collective-permute-start.14 = (bf16[8,64,128]{2,1,0:T(8,128)(2,1)S(1)}, bf16[8,64,128]{2,1,0:T(8,128)(2,1)S(1)}, u32[]{:S(2)}, u32[]{:S(2)}) collective-permute-start(bf16[8,64,128]{2,1,0:T(8,128)(2,1)S(1)} %all_to_all.35.refs_0_), channel_id=1, source_target_pairs={{0,24},{8,0},{16,8},{24,16},{1,25},{9,1},{17,9},{25,17},{2,26},{10... | collective-permute-start | bytes 393224 | tf_op jit(solution)/shard_map/ppermute | solution.py:323
  174.9 7.3 %collective-permute-start.17 = (bf16[8,64,128]{2,1,0:T(8,128)(2,1)S(1)}, bf16[8,64,128]{2,1,0:T(8,128)(2,1)S(1)}, u32[]{:S(2)}, u32[]{:S(2)}) collective-permute-start(bf16[8,64,128]{2,1,0:T(8,128)(2,1)S(1)} %all_to_all.35.refs_0_), channel_id=1, source_target_pairs={{0,4},{4,0},{1,5},{5,1},{2,6},{6,2},{3,7},{7,3},{8,12},{12,8},{9,1... | collective-permute-start | bytes 393224 | tf_op jit(solution)/shard_map/ppermute | solution.py:327
  177.4 5.8 %copy-start.5 = (bf16[8,64,128]{2,1,0:T(8,128)(2,1)}, bf16[8,64,128]{2,1,0:T(8,128)(2,1)S(1)}, u32[]{:S(2)}) copy-start(bf16[8,64,128]{2,1,0:T(8,128)(2,1)S(1)} %collective-permute-done.16.refs_3_) | copy-start | bytes 393220
  177.4 4.8 %collective-permute-start.20 = (bf16[8,64,128]{2,1,0:T(8,128)(2,1)S(1)}, bf16[8,64,128]{2,1,0:T(8,128)(2,1)S(1)}, u32[]{:S(2)}, u32[]{:S(2)}) collective-permute-start(bf16[8,64,128]{2,1,0:T(8,128)(2,1)S(1)} %collective-permute-done.16.refs_3_), channel_id=1, source_target_pairs={{0,4},{4,0},{1,5},{5,1},{2,6},{6,2},{3,7},{7,3},{8,12},{12,8},{9,1... | collective-permute-start | bytes 393224 | tf_op jit(solution)/shard_map/ppermute | solution.py:327
  180.4 2.8 %copy-start.6 = (bf16[8,64,128]{2,1,0:T(8,128)(2,1)}, bf16[8,64,128]{2,1,0:T(8,128)(2,1)S(1)}, u32[]{:S(2)}) copy-start(bf16[8,64,128]{2,1,0:T(8,128)(2,1)S(1)} %collective-permute-done.15.refs_2_) | copy-start | bytes 393220
  180.4 2.4 %collective-permute-start.19 = (bf16[8,64,128]{2,1,0:T(8,128)(2,1)S(1)}, bf16[8,64,128]{2,1,0:T(8,128)(2,1)S(1)}, u32[]{:S(2)}, u32[]{:S(2)}) collective-permute-start(bf16[8,64,128]{2,1,0:T(8,128)(2,1)S(1)} %collective-permute-done.15.refs_2_), channel_id=1, source_target_pairs={{0,4},{4,0},{1,5},{5,1},{2,6},{6,2},{3,7},{7,3},{8,12},{12,8},{9,1... | collective-permute-start | bytes 393224 | tf_op jit(solution)/shard_map/ppermute | solution.py:327
  181.8 1.4 copy-start.7
  181.8 1.4 collective-permute-start.18
  182.2 1.0 copy-start.8
  182.2 1.0 copy-start.9
  182.8 0.7 copy-start.10
  183.2 0.7 copy-start.11

commit v2 on v1

v2 whole, which is shorter than its diff:
```python
import functools

import jax
import jax.numpy as jnp
from jax import lax
from jax.experimental import pallas as pl
from jax.experimental.pallas import tpu as pltpu
from jax.sharding import Mesh
from jax.sharding import PartitionSpec as P


ROWS = 160
COLS = 28672
RANK = 64
LOCAL = 7168
HALF = LOCAL // 2
QUARTER = HALF // 4
LANES = 128
BLOCKS = QUARTER // LANES
TAIL = ROWS - LANES
EARLY = 48
LATE = ROWS - EARLY
SPREAD = 32
REPLICAS = 64
EPS = 1e-06
CLIP = 0.5

f32 = jnp.float32
bf16 = jnp.bfloat16
HIGHEST = lax.Precision.HIGHEST
VMEM = pltpu.VMEM


def whole():
    return pl.BlockSpec(memory_space=VMEM)


def room(mib, flops=10**6):
    return dict(
        compiler_params=pltpu.CompilerParams(vmem_limit_bytes=mib * 2**20),
        cost_estimate=pl.CostEstimate(flops=flops, bytes_accessed=2**20, transcendentals=0),
    )


def shrink_of(squares):
    rows = jnp.sum(squares, axis=0)
    total = jnp.sum(jnp.sum(rows, axis=1, keepdims=True), axis=0, keepdims=True)
    scaled = CLIP * jnp.sqrt(f32(ROWS * COLS))
    return jnp.minimum(1.0, scaled * lax.rsqrt(total / REPLICAS + EPS))


def prep_kernel(at, g, e, q_all, send, squares, q, own, sems):
    def piece(ref, core, out, sem):
        cols = pl.ds(pl.multiple_of(core * HALF, LANES), HALF)
        return pltpu.make_async_copy(ref.at[0, :, cols], out, sems.at[sem])

    copies = [
        piece(g, 1 - at[0], send.at[0:ROWS], 0),
        piece(g, at[0], own, 1),
        piece(e, 1 - at[0], send.at[ROWS : 2 * ROWS], 2),
    ]
    first = at[0] * 4 * BLOCKS + at[1] * BLOCKS + jnp.minimum(at[2], BLOCKS - 1)
    cols = pl.ds(pl.multiple_of(first * LANES, LANES), LANES)
    copies.append(pltpu.make_async_copy(q_all.at[:, cols], q, sems.at[3]))
    for copy in copies:
        copy.start()

    def rows_of(ref):
        def rows(i, acc):
            for lane in range(0, HALF, HALF // 4):
                block = ref[pl.ds(i * 16, 16), lane : lane + HALF // 4].astype(f32)
                block = block * block
                acc = acc + (block[:8] + block[8:])
            return acc

        return rows

    acc = jnp.zeros((8, HALF // 4), f32)
    copies[0].wait()
    acc = lax.fori_loop(0, ROWS // 16, rows_of(send), acc)
    copies[1].wait()
    acc = lax.fori_loop(0, ROWS // 16, rows_of(own), acc)
    part = acc[:, :LANES]
    for lane in range(LANES, HALF // 4, LANES):
        part = part + acc[:, lane : lane + LANES]
    for k in range(SPREAD):
        squares[k] = part
    copies[2].wait()
    copies[3].wait()


def prep(at, grads, error, q_t):
    hbm = pl.BlockSpec(memory_space=pltpu.HBM)
    return pl.pallas_call(
        prep_kernel,
        grid_spec=pltpu.PrefetchScalarGridSpec(
            num_scalar_prefetch=1,
            grid=(1,),
            in_specs=[hbm, hbm, hbm],
            out_specs=[
                pl.BlockSpec((2 * ROWS, HALF), lambda i, at: (0, 0)),
                pl.BlockSpec((SPREAD, 8, LANES), lambda i, at: (0, 0, 0)),
                pl.BlockSpec((RANK, LANES), lambda i, at: (0, 0)),
            ],
            scratch_shapes=[VMEM((ROWS, HALF), bf16), pltpu.SemaphoreType.DMA((4,))],
        ),
        out_shape=[
            jax.ShapeDtypeStruct((2 * ROWS, HALF), bf16),
            jax.ShapeDtypeStruct((SPREAD, 8, LANES), f32),
            jax.ShapeDtypeStruct((RANK, LANES), f32),
        ],
        name="prep",
        **room(58, 10**8),
    )(at, grads, error, q_t)


def both(g, e, got, row, cols):
    here = pl.ds(row, 16)
    gradient = g[0, here, cols].astype(f32) + got[here, cols].astype(f32)
    residue = e[0, here, cols].astype(f32) + got[pl.ds(ROWS + row, 16), cols].astype(f32)
    return gradient, residue


def early_kernel(at, g, e, got, squares, *outs):
    outs, spread = outs[:4], outs[4]
    for j, out in enumerate(outs):
        cols = pl.ds(pl.multiple_of(lax.rem(at[1] + j, 4) * QUARTER, LANES), QUARTER)

        def rows(i, carry, out=out, cols=cols):
            gradient, residue = both(g, e, got, i * 16, cols)
            out[pl.ds(i * 16, 16), :] = gradient
            out[pl.ds(EARLY + i * 16, 16), :] = residue
            return carry

        lax.fori_loop(0, EARLY // 16, rows, 0)
    total = jnp.sum(squares[...], axis=0)
    for k in range(8):
        spread[k] = total


def late_kernel(at, g, e, got, squares, *outs):
    outs, spread = outs[:4], outs[4]
    shrink = shrink_of(squares[...])
    spread[...] = jnp.broadcast_to(shrink, (8, LANES))
    for j, out in enumerate(outs):
        cols = pl.ds(pl.multiple_of(lax.rem(at[1] + j, 4) * QUARTER, LANES), QUARTER)

        def rows(i, carry, out=out, cols=cols):
            gradient, residue = both(g, e, got, EARLY + i * 16, cols)
            out[pl.ds(i * 16, 16), :] = shrink * gradient + residue
            return carry

        lax.fori_loop(0, LATE // 16, rows, 0)


def merge(kernel, at, grads, error, got, squares, rows, spread):
    own = pl.BlockSpec((1, ROWS, HALF), lambda i, at: (0, 0, at[0]))
    outs = [((rows, QUARTER), f32)] * 4
    outs = outs + [((*spread, 8, LANES), f32)]
    return pl.pallas_call(
        kernel,
        grid_spec=pltpu.PrefetchScalarGridSpec(
            num_scalar_prefetch=1,
            grid=(1,),
            in_specs=[
                own,
                own,
                pl.BlockSpec((2 * ROWS, HALF), lambda i, at: (0, 0)),
                pl.BlockSpec(squares.shape, lambda i, at: (0, 0, 0)),
            ],
            out_specs=[
                pl.BlockSpec(shape, lambda i, at, shape=shape: (0,) * len(shape))
                for shape, _ in outs
            ],
        ),
        out_shape=[jax.ShapeDtypeStruct(*out) for out in outs],
        **room(16, 10**9),
    )(at, grads, error, got, squares)


def fold_early_kernel(a, b, c, d, shrink, out):
    shrink = shrink[0:1, 0:1]
    top, low = slice(0, EARLY), slice(EARLY, 2 * EARLY)
    for k in range(BLOCKS):
        cols = slice(k * LANES, (k + 1) * LANES)
        gradient = (a[top, cols] + c[top, cols]) + (b[top, cols] + d[top, cols])
        residue = (a[low, cols] + c[low, cols]) + (b[low, cols] + d[low, cols])
        out[k] = shrink * gradient + residue
    out[BLOCKS] = jnp.zeros((EARLY, LANES), f32)


def fold_late_kernel(a, b, c, d, after, out):
    for k in range(BLOCKS):
        cols = slice(k * LANES, (k + 1) * LANES)
        out[k] = (a[:, cols] + c[:, cols]) + (b[:, cols] + d[:, cols])
    out[BLOCKS] = jnp.zeros((LATE, LANES), f32)


def fold(kernel, rows, *args):
    return pl.pallas_call(
        kernel,
        in_specs=[whole()] * len(args),
        out_specs=whole(),
        out_shape=jax.ShapeDtypeStruct((BLOCKS + 1, rows, LANES), f32),
        **room(8, 10**8),
    )(*args)


def dot(a, b):
    return jnp.dot(a, b, precision=HIGHEST, preferred_element_type=f32)


def dot_t(a, b):
    return lax.dot_general(
        a, b, (((1,), (1,)), ((), ())), precision=HIGHEST, preferred_element_type=f32
    )


def terms_kernel(early, late, q, total, pack):
    top, low = early[0], late[0]
    for k in range(1, BLOCKS + 1):
        top = top + early[k]
        low = low + late[k]
    s = jnp.concatenate([top, low], axis=0)
    total[...] = s
    head = s[:LANES]
    tail = s[LANES:]
    tail_full = jnp.concatenate([tail, jnp.zeros((LANES - TAIL, LANES), f32)], axis=0)
    q_half = q[...].astype(bf16).astype(f32)
    left_tail = dot_t(q_half, tail_full)
    corner = dot_t(tail, tail_full)
    packed_left = left_tail[0:16]
    packed_corner = corner[0:8]
    for j in range(1, 4):
        packed_left = packed_left + pltpu.roll(left_tail[16 * j : 16 * j + 16], 32 * j, 1)
        packed_corner = packed_corner + pltpu.roll(corner[8 * j : 8 * j + 8], 32 * j, 1)
    flat = jnp.concatenate(
        [
            dot_t(q_half, head),
            dot_t(head, head),
            dot_t(tail, head),
            packed_left,
            packed_corner,
            jnp.zeros((8, LANES), f32),
        ],
        axis=0,
    )
    for k in range(SPREAD):
        pack[k] = flat[8 * k : 8 * k + 8]


def terms(early, late, q):
    return pl.pallas_call(
        terms_kernel,
        in_specs=[whole()] * 3,
        out_specs=[whole()] * 2,
        out_shape=[
            jax.ShapeDtypeStruct((ROWS, LANES), f32),
            jax.ShapeDtypeStruct((SPREAD, 8, LANES), f32),
        ],
        name="terms",
        **room(8, 10**8),
    )(early, late, q)


def orthonormal(a, b):
    groups = RANK // 8
    a = [a[8 * i : 8 * i + 8] for i in range(groups)]
    b = [b[8 * i : 8 * i + 8] for i in range(groups)]
    place = lax.broadcasted_iota(jnp.int32, (8, 1), 0)
    for k in range(0, RANK, 2):
        g, r = divmod(k, 8)
        u_a, u_b = a[g][r : r + 1], b[g][r : r + 1]
        w_a, w_b = a[g][r + 1 : r + 2], b[g][r + 1 : r + 2]
        span = range(g, groups)
        by_u = [jnp.sum(a[i] * u_a + b[i] * u_b, axis=1, keepdims=True) for i in span]
        by_w = [jnp.sum(a[i] * w_a + b[i] * w_b, axis=1, keepdims=True) for i in span]
        uu, uw = by_u[0][r : r + 1], by_u[0][r + 1 : r + 2]
        ww = by_w[0][r + 1 : r + 2]
        over_u = 1.0 / (uu + EPS)
        along = uw * over_u
        rest = uw - along * uu
        over_w = 1.0 / (jnp.maximum(ww - along * (uw + rest), 0.0) + EPS)
        w_a = w_a - along * u_a
        w_b = w_b - along * u_b
        for i in span:
            coeff_u = by_u[i - g] * over_u
            coeff_w = (by_w[i - g] - along * by_u[i - g] - coeff_u * rest) * over_w
            if i == g:
                coeff_u = jnp.where(place > r, coeff_u, 0.0)
                coeff_w = jnp.where(place > r + 1, coeff_w, 0.0)
            a[i] = a[i] - coeff_u * u_a - coeff_w * w_a
            b[i] = b[i] - coeff_u * u_b - coeff_w * w_b
    for i in range(groups):
        scale = lax.rsqrt(jnp.sum(a[i] * a[i] + b[i] * b[i], axis=1, keepdims=True) + EPS)
        a[i] = a[i] * scale
        b[i] = b[i] * scale
    return jnp.concatenate(a, axis=0), jnp.concatenate(b, axis=0)


def factor_kernel(pack, s, p_t, p_half, q):
    lane = lax.broadcasted_iota(jnp.int32, (1, LANES), 1)
    keep = lane < TAIL

    def unpack(rows):
        parts = [jnp.where(keep, rows, 0.0)]
        for j in range(1, 4):
            parts.append(jnp.where(keep, pltpu.roll(rows, LANES - 32 * j, 1), 0.0))
        return jnp.concatenate(parts, axis=0)

    flat = jnp.concatenate([pack[k] for k in range(SPREAD)], axis=0)
    empty = jnp.zeros((LANES - TAIL, LANES), f32)
    first_a = flat[0:64]
    gram = flat[64 : 64 + LANES]
    gram_side = jnp.concatenate([flat[64 + LANES : 64 + ROWS], empty], axis=0)
    first_b = unpack(flat[224:240])
    gram_corner = jnp.concatenate([unpack(flat[240:248]), empty], axis=0)

    a, b = orthonormal(first_a, first_b)
    a = a.astype(bf16).astype(f32)
    b = b.astype(bf16).astype(f32)
    second_a = (dot(a, gram) + dot(b, gram_side)) * (1.0 / REPLICAS)
    second_b = (dot_t(a, gram_side) + dot(b, gram_corner)) * (1.0 / REPLICAS)
    a, b = orthonormal(second_a, second_b)
    p_t[:, 0:LANES] = a
    p_t[:, LANES:ROWS] = b[:, 0:TAIL]
    a = a.astype(bf16).astype(f32)
    b = b.astype(bf16).astype(f32)
    p_half[0:LANES, :] = a.T.astype(bf16)
    p_half[LANES:ROWS, :] = b.T[0:TAIL].astype(bf16)
    tail_full = jnp.concatenate([s[LANES:ROWS], empty], axis=0)
    columns = ((dot(a, s[0:LANES]) + dot(b, tail_full)) * (1.0 / REPLICAS)).astype(q.dtype)
    for k in range(8):
        q[k] = columns


def factor(pack, s):
    return pl.pallas_call(
        factor_kernel,
        in_specs=[whole()] * 2,
        out_specs=[whole()] * 3,
        out_shape=[
            jax.ShapeDtypeStruct((RANK, ROWS), f32),
            jax.ShapeDtypeStruct((ROWS, RANK), bf16),
            jax.ShapeDtypeStruct((8, RANK, LANES), bf16),
        ],
        name="factor",
        **room(8, 100000000),
    )(pack, s)


def finish_kernel(n, at, g, e, shrink, p_half, *refs):
    parts, (out, q_t) = refs[:n], refs[-2:]
    shrink = shrink[0:1, 0:1]
    for k in range(n):

        @pl.when(pl.program_id(0) == k)
        def _(part=parts[k]):
            for block in range(BLOCKS):
                cols = slice(block * LANES, (block + 1) * LANES)
                q = part[block]
                approx = jnp.dot(p_half[...], q, preferred_element_type=f32)
                merged = shrink * g[0, :, cols].astype(f32) + e[0, :, cols].astype(f32)
                out[0, :, cols] = merged - approx
                q_t[:, cols] = q.astype(f32)


def finish(at, which, grads, error, shrink, p_half, parts, before=()):
    n = len(parts)

    def column(i, at):
        place = 0
        for k, (other, ahead) in enumerate(which):
            core = 1 - at[0] if other else at[0]
            place = jnp.where(i == k, core * 4 + lax.rem(at[1] + ahead, 4), place)
        return place

    tile = pl.BlockSpec((1, ROWS, QUARTER), lambda i, at: (0, 0, column(i, at)))
    return pl.pallas_call(
        functools.partial(finish_kernel, n),
        grid_spec=pltpu.PrefetchScalarGridSpec(
            num_scalar_prefetch=1,
            grid=(n,),
            in_specs=[
                tile,
                tile,
                pl.BlockSpec((8, LANES), lambda i, at: (0, 0)),
                pl.BlockSpec((ROWS, RANK), lambda i, at: (0, 0)),
            ]
            + [pl.BlockSpec((8, RANK, LANES), lambda i, at: (0, 0, 0))] * n
            + [pl.BlockSpec(memory_space=pl.ANY)] * len(before),
            out_specs=[tile, pl.BlockSpec((RANK, QUARTER), lambda i, at: (0, column(i, at)))],
        ),
        out_shape=[
            jax.ShapeDtypeStruct((1, ROWS, LOCAL), f32),
            jax.ShapeDtypeStruct((RANK, LOCAL), f32),
        ],
        input_output_aliases={5 + n: 0, 6 + n: 1} if before else {},
        name="finish",
        **room(12, 10**9),
    )(at, grads, error, shrink, p_half, *parts, *before)


def respread_kernel(blocks, out):
    total = blocks[0]
    for k in range(1, blocks.shape[0]):
        total = total + blocks[k]
    for k in range(out.shape[0]):
        out[k] = total


def respread(blocks, n):
    return pl.pallas_call(
        respread_kernel,
        in_specs=[whole()],
        out_specs=whole(),
        out_shape=jax.ShapeDtypeStruct((n, *blocks.shape[1:]), f32),
        name="respread",
        **room(4, 1000000),
    )(blocks)


def shifted(value, axis, by):
    n = lax.axis_size(axis)
    return lax.ppermute(value, axis, [(i, (i - by) % n) for i in range(n)])


def swap(value, axis):
    return lax.ppermute(value, axis, [(0, 1), (1, 0)])


def exchange(blocks, axis):
    return lax.all_to_all(blocks, axis, 0, 0, tiled=True)


def from_ring(value, axis):
    return [value] + [shifted(value, axis, j) for j in range(1, 4)]


def to_ring(pieces, axis):
    return [pieces[0]] + [shifted(pieces[j], axis, -j) for j in range(1, 4)]


def step(grads, error, q_init):
    at = jnp.stack([lax.axis_index("c"), lax.axis_index("x"), lax.axis_index("z")]).astype(jnp.int32)
    chip = ("x", "c", "y")
    send, squares, q = prep(at, grads, error, q_init.T)
    got = swap(send, "c")
    squares = exchange(squares, chip)
    *early, squares = merge(early_kernel, at, grads, error, got, squares, 2 * EARLY, (8,))
    early = to_ring(early, "x")
    squares = exchange(squares, "z")
    *late, shrink = merge(late_kernel, at, grads, error, got, squares, LATE, ())
    late = to_ring(late, "x")
    early = fold(fold_early_kernel, EARLY, *early, shrink)
    early = exchange(early, "z")
    late = exchange(fold(fold_late_kernel, LATE, *late, early), "z")
    s, pack = terms(early, late, q)

    pack = respread(exchange(pack, chip), 8)
    pack = exchange(respread(exchange(pack, "z"), SPREAD), chip)

    p_t, p_half, q = factor(pack, s)
    parts = from_ring(exchange(q, "z"), "x")
    others = [swap(part, "c") for part in parts]
    args = (grads, error, shrink, p_half)
    outs = finish(at, [(0, 0), (1, 0)], *args, [parts[0], others[0]])
    outs = finish(at, [(0, 1), (0, 2), (0, 3)], *args, parts[1:], outs)
    new_error, q_t = finish(at, [(1, 1), (1, 2), (1, 3)], *args, others[1:], outs)
    return p_t.T, q_t.T, new_error


def solution(mesh):
    finer = Mesh(
        mesh.devices.reshape(8, 4, 2, mesh.shape["tensor"]), ("z", "x", "c", "y")
    )
    replicas = ("z", "x", "c")
    return jax.shard_map(
        step,
        mesh=finer,
        in_specs=(P(replicas, None, "y"), P(replicas, None, "y"), P("y", None)),
        out_specs=(P(), P("y", None), P(replicas, None, "y")),
        check_vma=False,
    )
```

time: 194 us -> 163 us (0.84)
  waiting for transfers between devices: 40.8 us -> 12.7 us
  blocking collectives: 79.5 us -> 92.3 us
  Pallas kernels: 39.7 us -> 32.3 us
  local copies, waits for them, and re-layouts: 3.61 us -> 0.02 us
  starting transfers between devices: 27.2 us -> 24.1 us
    ppermute x15 -> x9, waiting for transfers between devices: 35.5 us -> 12.7 us  [shifted(): return lax.ppermute(value, axis, [(i, (i - by) % n) for i in range(n)])]
    all_to_all x6 -> x7, blocking collectives: 79.5 us -> 92.3 us  [exchange(): return lax.all_to_all(blocks, axis, 0, 0, tiled=True)]
    ppermute x15 -> x9, starting transfers between devices: 16.7 us -> 11 us  [shifted(): return lax.ppermute(value, axis, [(i, (i - by) % n) for i in range(n)])]
    pallas_call x4 -> x10, Pallas kernels: 20 us -> 14.3 us  [the longest x3 8.2 us: finish(): pl.pallas_call(functools.partial(finish_kernel, n), grid_spec=pltpu.Prefe...]
    ppermute x6 -> x5, waiting for transfers between devices: 5.25 us -> 0.01 us  [swap(): return lax.ppermute(value, axis, [(0, 1), (1, 0)])]
    all_to_all x0 -> x1, starting transfers between devices: none -> 3.39 us  [exchange(): return lax.all_to_all(blocks, axis, 0, 0, tiled=True)]
    unnamed x24 -> x10, local copies, waits for them, and re-layouts: 2.84 us -> 0.02 us
    ppermute x6 -> x5, starting transfers between devices: 10.5 us -> 9.76 us  [swap(): return lax.ppermute(value, axis, [(0, 1), (1, 0)])]
  transfers between devices with their start and end apart: 21 -> 15, of which waited for: 12 -> 3; matrix products, arithmetic and copies ran while one was open for 0% -> 0% of each run, Pallas kernels for 0% -> 5%
where the time goes in v2:
time: 163 us
  blocking collectives  92.3 us (57%)
  Pallas kernels  32.3 us (20%)
  starting transfers between devices  24.1 us (15%)
  waiting for transfers between devices  12.7 us (8%)
    all_to_all x7, blocking collectives, exchange(): return lax.all_to_all(blocks, axis, 0, 0, tiled=True)  92.3 us
    pallas_call x1, Pallas kernels, factor(): pl.pallas_call(factor_kernel, in_specs=[whole()] * 2, out_specs=[whole()]...  13.4 us
    ppermute x9, waiting for transfers between devices, shifted(): return lax.ppermute(value, axis, [(i, (i - by) % n) for i in range(n)])  12.7 us
    ppermute x9, starting transfers between devices, shifted(): return lax.ppermute(value, axis, [(i, (i - by) % n) for i in range(n)])  11 us
    ppermute x5, starting transfers between devices, swap(): return lax.ppermute(value, axis, [(0, 1), (1, 0)])  9.76 us
    pallas_call x3, Pallas kernels, finish(): pl.pallas_call(functools.partial(finish_kernel, n), grid_spec=pltpu.Prefe...  8.2 us
    pallas_call x1, Pallas kernels, prep(): pl.pallas_call(prep_kernel, grid_spec=pltpu.PrefetchScalarGridSpec(num_sc...  4.6 us
    all_to_all x1, starting transfers between devices, exchange(): return lax.all_to_all(blocks, axis, 0, 0, tiled=True)  3.39 us
  transfers between devices with their start and end apart: 15, of which 3 were waited for; matrix products, arithmetic and copies ran while one was open for 0% of the time, Pallas kernels for 5%

profile of v2, /device:TPU:1, one launch (start us, length us, event | category | flops | bytes accessed | tf_op | source)
XLA Modules:
  0.0 162.8 jit_solution(238528625424823522)
XLA Ops:
  0.6 0.7 pad_add_fusion.at
  1.3 0.0 copy-start
  1.3 0.0 copy-start.1
  1.3 0.0 copy-start.4
  1.3 4.6 %prep.1 = (bf16[320,3584]{1,0:T(8,128)(2,1)}, f32[32,8,128]{2,1,0:T(8,128)}, f32[64,128]{1,0:T(8,128)}) custom-call(s32[3]{0:T(128)} %pad_add_fusion.at, bf16[1,160,7168]{2,1,0:T(8,128)(2,1)} %g.11, bf16[1,160,7168]{2,1,0:T(8,128)(2,1)} %e.11, f32[64,7168]{1,0:T(8,128)} %bitcast.7), custom_call_target="tpu_custom_call" | custom-call | flops 100000000 | bytes 1048576 | tf_op jit(solution)/shard_map/prep/pallas_call | solution.py:94
  5.9 3.3 %collective-permute-start = (bf16[320,3584]{1,0:T(8,128)(2,1)}, bf16[320,3584]{1,0:T(8,128)(2,1)S(1)}, u32[]{:S(2)}, u32[]{:S(2)}) collective-permute-start(bf16[320,3584]{1,0:T(8,128)(2,1)} %get-tuple-element.27), channel_id=1, source_target_pairs={{0,4},{4,0},{1,5},{5,1},{2,6},{6,2},{3,7},{7,3},{8,12},{12,8},{9,1... | collective-permute-start | bytes 6881288 | tf_op jit(solution)/shard_map/ppermute | solution.py:429
  9.2 13.1 %all_to_all.40.squares = f32[32,8,128]{2,1,0:T(8,128)S(1)} all-to-all(f32[32,8,128]{2,1,0:T(8,128)} %get-tuple-element.28), channel_id=1, replica_groups=mesh['z'=8,'x'=4,'c'=2,'y'=4] {'x','c','y'}, dimensions={0} | all-to-all | bytes 262144 | tf_op jit(solution)/shard_map/all_to_all | solution.py:433
  22.3 0.0 collective-permute-done.got
  22.3 0.0 copy-done
  22.3 0.0 copy-done.1
  22.3 0.0 copy-done.4
  22.3 1.0 shard_map.58
  23.3 0.5 collective-permute-start.1
  23.7 1.7 %collective-permute-start.2 = (f32[96,896]{1,0:T(8,128)S(1)}, f32[96,896]{1,0:T(8,128)S(1)}, u32[]{:S(2)}, u32[]{:S(2)}) collective-permute-start(f32[96,896]{1,0:T(8,128)S(1)} %get-tuple-element.31), channel_id=1, source_target_pairs={{0,16},{8,24},{16,0},{24,8},{1,17},{9,25},{17,1},{25,9},{2,18},{10... | collective-permute-start | bytes 1032200 | tf_op jit(solution)/shard_map/ppermute | solution.py:425
  25.4 1.0 collective-permute-start.3
  26.4 14.9 %all_to_all.41.squares = f32[8,8,128]{2,1,0:T(8,128)S(1)} all-to-all(f32[8,8,128]{2,1,0:T(8,128)S(1)} %get-tuple-element.33), channel_id=1, replica_groups=mesh['z'=8,'x'=4,'c'=2,'y'=4] {'z'}, dimensions={0} | all-to-all | bytes 65536 | tf_op jit(solution)/shard_map/all_to_all | solution.py:433
  41.4 2.3 %shard_map.59 = (f32[112,896]{1,0:T(8,128)S(1)}, f32[112,896]{1,0:T(8,128)}, f32[112,896]{1,0:T(8,128)}, f32[112,896]{1,0:T(8,128)}, f32[8,128]{1,0:T(8,128)S(1)}) custom-call(s32[3]{0:T(128)S(1)} %copy-done.4, bf16[1,160,7168]{2,1,0:T(8,128)(2,1)S(1)} %copy-done, bf16[1,160,7168]{2,1,0:T(8,128)(2,1)S(1)} %copy-done.1, ...), custom_call_target="tpu_custom_call" | custom-call | flops 1000000000 | bytes 1048576 | tf_op jit(solution)/shard_map/pallas_call | solution.py:160
  43.7 0.4 collective-permute-start.4
  44.1 1.6 collective-permute-start.5
  45.7 0.0 collective-permute-done.1.b
  45.7 2.1 %collective-permute-start.6 = (f32[112,896]{1,0:T(8,128)}, f32[112,896]{1,0:T(8,128)}, u32[]{:S(2)}, u32[]{:S(2)}) collective-permute-start(f32[112,896]{1,0:T(8,128)} %get-tuple-element.38), channel_id=1, source_target_pairs={{0,24},{8,0},{16,8},{24,16},{1,25},{9,1},{17,9},{25,17},{2,26},{10... | collective-permute-start | bytes 1204232 | tf_op jit(solution)/shard_map/ppermute | solution.py:425
  47.7 0.0 collective-permute-done.2.c
  47.8 0.0 collective-permute-done.3.d
  47.8 0.0 copy-start.3
  47.8 0.8 shard_map.60
  48.5 3.4 %all-to-all-start.2 = ((f32[8,48,128]{2,1,0:T(8,128)}), f32[8,48,128]{2,1,0:T(8,128)S(1)}, u32[]{:S(2)}, u32[]{:S(2)}) async-start(f32[8,48,128]{2,1,0:T(8,128)} %shard_map.60), calls=%async_computation.2 | async-start | bytes 393216 | tf_op jit(solution)/shard_map/all_to_all | solution.py:433
  51.9 1.9 %collective-permute-done.4.b = f32[112,896]{1,0:T(8,128)S(1)} collective-permute-done((f32[112,896]{1,0:T(8,128)}, f32[112,896]{1,0:T(8,128)S(1)}, u32[]{:S(2)}, u32[]{:S(2)}) %collective-permute-start.4) | collective-permute-done | bytes 401440 | tf_op jit(solution)/shard_map/ppermute | solution.py:425
  53.8 7.8 %collective-permute-done.5.c = f32[112,896]{1,0:T(8,128)} collective-permute-done((f32[112,896]{1,0:T(8,128)}, f32[112,896]{1,0:T(8,128)}, u32[]{:S(2)}, u32[]{:S(2)}) %collective-permute-start.5) | collective-permute-done | bytes 401440 | tf_op jit(solution)/shard_map/ppermute | solution.py:425
  61.6 3.0 %collective-permute-done.6.d = f32[112,896]{1,0:T(8,128)} collective-permute-done((f32[112,896]{1,0:T(8,128)}, f32[112,896]{1,0:T(8,128)}, u32[]{:S(2)}, u32[]{:S(2)}) %collective-permute-start.6) | collective-permute-done | bytes 401440 | tf_op jit(solution)/shard_map/ppermute | solution.py:425
  64.6 0.0 all-to-all-done.2.after.early
  64.6 0.0 copy-start.2
  64.6 1.4 shard_map.61
  66.0 16.6 %all_to_all.42.late = f32[8,112,128]{2,1,0:T(8,128)S(1)} all-to-all(f32[8,112,128]{2,1,0:T(8,128)S(1)} %shard_map.61), channel_id=1, replica_groups=mesh['z'=8,'x'=4,'c'=2,'y'=4] {'z'}, dimensions={0} | all-to-all | bytes 917504 | tf_op jit(solution)/shard_map/all_to_all | solution.py:433
  82.6 0.0 copy-done.3
  82.6 0.5 terms.1
  83.2 15.4 %all_to_all.43.blocks = f32[32,8,128]{2,1,0:T(8,128)S(1)} all-to-all(f32[32,8,128]{2,1,0:T(8,128)S(1)} %get-tuple-element.40), channel_id=1, replica_groups=mesh['z'=8,'x'=4,'c'=2,'y'=4] {'x','c','y'}, dimensions={0} | all-to-all | bytes 262144 | tf_op jit(solution)/shard_map/all_to_all | solution.py:433
  98.6 9.2 %all_to_all.44.blocks = f32[8,8,128]{2,1,0:T(8,128)S(1)} all-to-all(f32[8,8,128]{2,1,0:T(8,128)S(1)} %respread.2), channel_id=1, replica_groups=mesh['z'=8,'x'=4,'c'=2,'y'=4] {'z'}, dimensions={0} | all-to-all | bytes 65536 | tf_op jit(solution)/shard_map/all_to_all | solution.py:433
  107.9 12.5 %all_to_all.45.pack = f32[32,8,128]{2,1,0:T(8,128)S(1)} all-to-all(f32[32,8,128]{2,1,0:T(8,128)S(1)} %respread.3), channel_id=1, replica_groups=mesh['z'=8,'x'=4,'c'=2,'y'=4] {'x','c','y'}, dimensions={0} | all-to-all | bytes 262144 | tf_op jit(solution)/shard_map/all_to_all | solution.py:433
  120.4 13.4 %factor.1 = (f32[64,160]{1,0:T(8,128)}, bf16[160,64]{1,0:T(8,128)(2,1)S(1)}, bf16[8,64,128]{2,1,0:T(8,128)(2,1)S(1)}) custom-call(f32[32,8,128]{2,1,0:T(8,128)S(1)} %all_to_all.45.pack, f32[160,128]{1,0:T(8,128)S(1)} %get-tuple-element.41.s), custom_call_target="tpu_custom_call" | custom-call | flops 100000000 | bytes 1048576 | tf_op jit(solution)/shard_map/factor/pallas_call | solution.py:338
  133.8 10.5 %all_to_all.46.refs_0_ = bf16[8,64,128]{2,1,0:T(8,128)(2,1)S(1)} all-to-all(bf16[8,64,128]{2,1,0:T(8,128)(2,1)S(1)} %get-tuple-element.44), channel_id=1, replica_groups=mesh['z'=8,'x'=4,'c'=2,'y'=4] {'z'}, dimensions={0} | all-to-all | bytes 262144 | tf_op jit(solution)/shard_map/all_to_all | solution.py:433
  144.4 1.1 collective-permute-start.9
  145.4 0.6 collective-permute-start.11
  146.0 2.1 %collective-permute-start.7 = (bf16[8,64,128]{2,1,0:T(8,128)(2,1)S(1)}, bf16[8,64,128]{2,1,0:T(8,128)(2,1)S(1)}, u32[]{:S(2)}, u32[]{:S(2)}) collective-permute-start(bf16[8,64,128]{2,1,0:T(8,128)(2,1)S(1)} %all_to_all.46.refs_0_), channel_id=1, source_target_pairs={{0,24},{8,0},{16,8},{24,16},{1,25},{9,1},{17,9},{25,17},{2,26},{10... | collective-permute-start | bytes 393224 | tf_op jit(solution)/shard_map/ppermute | solution.py:425
  148.1 2.6 %collective-permute-start.13 = (bf16[8,64,128]{2,1,0:T(8,128)(2,1)S(1)}, bf16[8,64,128]{2,1,0:T(8,128)(2,1)S(1)}, u32[]{:S(2)}, u32[]{:S(2)}) collective-permute-start(bf16[8,64,128]{2,1,0:T(8,128)(2,1)S(1)} %all_to_all.46.refs_0_), channel_id=1, source_target_pairs={{0,4},{4,0},{1,5},{5,1},{2,6},{6,2},{3,7},{7,3},{8,12},{12,8},{9,1... | collective-permute-start | bytes 393224 | tf_op jit(solution)/shard_map/ppermute | solution.py:429
  150.8 0.0 collective-permute-done.9.refs_1_
  150.8 2.4 %collective-permute-start.10 = (bf16[8,64,128]{2,1,0:T(8,128)(2,1)S(1)}, bf16[8,64,128]{2,1,0:T(8,128)(2,1)S(1)}, u32[]{:S(2)}, u32[]{:S(2)}) collective-permute-start(bf16[8,64,128]{2,1,0:T(8,128)(2,1)S(1)} %collective-permute-done.9.refs_1_), channel_id=1, source_target_pairs={{0,4},{4,0},{1,5},{5,1},{2,6},{6,2},{3,7},{7,3},{8,12},{12,8},{9,1... | collective-permute-start | bytes 393224 | tf_op jit(solution)/shard_map/ppermute | solution.py:429
  153.2 0.0 collective-permute-done.11.refs_2_
  153.2 1.4 collective-permute-start.12
  154.6 0.0 collective-permute-done.7.refs_0_
  154.6 0.0 collective-permute-start.8
  154.6 0.0 collective-permute-done.13.refs_1_
  154.6 0.0 copy-done.2
  154.6 2.2 %finish.3 = (f32[1,160,7168]{2,1,0:T(8,128)}, f32[64,7168]{1,0:T(8,128)}) custom-call(s32[3]{0:T(128)S(1)} %copy-done.4, bf16[1,160,7168]{2,1,0:T(8,128)(2,1)S(1)} %copy-done, bf16[1,160,7168]{2,1,0:T(8,128)(2,1)S(1)} %copy-done.2, f32[8,128]{1,0:T(8,128)S(1)} %get-tuple-element.34.shrink, bf16[160,64]{1,0:T(8,128)(2,1)S(1)} %get-tuple-element.43.p_half, ...), custom_call_target="tpu_custom_call" | custom-call | flops 1000000000 | bytes 1048576 | tf_op jit(solution)/shard_map/finish/pallas_call | solution.py:379
  156.8 3.0 %finish.4 = (f32[1,160,7168]{2,1,0:T(8,128)}, f32[64,7168]{1,0:T(8,128)}) custom-call(s32[3]{0:T(128)S(1)} %copy-done.4, bf16[1,160,7168]{2,1,0:T(8,128)(2,1)S(1)} %copy-done, bf16[1,160,7168]{2,1,0:T(8,128)(2,1)S(1)} %copy-done.2, f32[8,128]{1,0:T(8,128)S(1)} %get-tuple-element.34.shrink, ...), custom_call_target="tpu_custom_call", output_to_operand_aliasing={{0}: (8, {}), {1}: (9, {})} | custom-call | flops 1000000000 | bytes 1048576 | tf_op jit(solution)/shard_map/finish/pallas_call | solution.py:379
  159.8 0.0 collective-permute-done.10.refs_1_
  159.8 0.0 collective-permute-done.12.refs_2_
  159.8 0.0 collective-permute-done.8.refs_0_
  159.8 3.0 %finish.5 = (f32[1,160,7168]{2,1,0:T(8,128)}, f32[64,7168]{1,0:T(8,128)}) custom-call(s32[3]{0:T(128)S(1)} %copy-done.4, bf16[1,160,7168]{2,1,0:T(8,128)(2,1)S(1)} %copy-done, bf16[1,160,7168]{2,1,0:T(8,128)(2,1)S(1)} %copy-done.2, f32[8,128]{1,0:T(8,128)S(1)} %get-tuple-element.34.shrink, ...), custom_call_target="tpu_custom_call", output_to_operand_aliasing={{0}: (8, {}), {1}: (9, {})} | custom-call | flops 1000000000 | bytes 1048576 | tf_op jit(solution)/shard_map/finish/pallas_call | solution.py:379
  (2 shorter events, 0.1 us)
Async XLA Ops:
  1.3 21.0 %copy-start = (bf16[1,160,7168]{2,1,0:T(8,128)(2,1)S(1)}, bf16[1,160,7168]{2,1,0:T(8,128)(2,1)}, u32[]{:S(2)}) copy-start(bf16[1,160,7168]{2,1,0:T(8,128)(2,1)} %g.11) | copy-start | bytes 6881284
  1.3 21.0 %copy-start.1 = (bf16[1,160,7168]{2,1,0:T(8,128)(2,1)S(1)}, bf16[1,160,7168]{2,1,0:T(8,128)(2,1)}, u32[]{:S(2)}) copy-start(bf16[1,160,7168]{2,1,0:T(8,128)(2,1)} %e.11) | copy-start | bytes 6881284
  1.3 21.0 %copy-start.4 = (s32[3]{0:T(128)S(1)}, s32[3]{0:T(128)}, u32[]{:S(2)}) copy-start(s32[3]{0:T(128)} %pad_add_fusion.at) | copy-start | bytes 40
  5.9 16.3 %collective-permute-start = (bf16[320,3584]{1,0:T(8,128)(2,1)}, bf16[320,3584]{1,0:T(8,128)(2,1)S(1)}, u32[]{:S(2)}, u32[]{:S(2)}) collective-permute-start(bf16[320,3584]{1,0:T(8,128)(2,1)} %get-tuple-element.27), channel_id=1, source_target_pairs={{0,4},{4,0},{1,5},{5,1},{2,6},{6,2},{3,7},{7,3},{8,12},{12,8},{9,1... | collective-permute-start | bytes 6881288 | tf_op jit(solution)/shard_map/ppermute | solution.py:429
  23.3 22.4 %collective-permute-start.1 = (f32[96,896]{1,0:T(8,128)S(1)}, f32[96,896]{1,0:T(8,128)S(1)}, u32[]{:S(2)}, u32[]{:S(2)}) collective-permute-start(f32[96,896]{1,0:T(8,128)S(1)} %get-tuple-element.30), channel_id=1, source_target_pairs={{0,8},{8,16},{16,24},{24,0},{1,9},{9,17},{17,25},{25,1},{2,10},{10... | collective-permute-start | bytes 1032200 | tf_op jit(solution)/shard_map/ppermute | solution.py:425
  23.7 24.0 %collective-permute-start.2 = (f32[96,896]{1,0:T(8,128)S(1)}, f32[96,896]{1,0:T(8,128)S(1)}, u32[]{:S(2)}, u32[]{:S(2)}) collective-permute-start(f32[96,896]{1,0:T(8,128)S(1)} %get-tuple-element.31), channel_id=1, source_target_pairs={{0,16},{8,24},{16,0},{24,8},{1,17},{9,25},{17,1},{25,9},{2,18},{10... | collective-permute-start | bytes 1032200 | tf_op jit(solution)/shard_map/ppermute | solution.py:425
  25.4 22.3 %collective-permute-start.3 = (f32[96,896]{1,0:T(8,128)S(1)}, f32[96,896]{1,0:T(8,128)S(1)}, u32[]{:S(2)}, u32[]{:S(2)}) collective-permute-start(f32[96,896]{1,0:T(8,128)S(1)} %get-tuple-element.32), channel_id=1, source_target_pairs={{0,24},{8,0},{16,8},{24,16},{1,25},{9,1},{17,9},{25,17},{2,26},{10... | collective-permute-start | bytes 1032200 | tf_op jit(solution)/shard_map/ppermute | solution.py:425
  43.7 10.1 %collective-permute-start.4 = (f32[112,896]{1,0:T(8,128)}, f32[112,896]{1,0:T(8,128)S(1)}, u32[]{:S(2)}, u32[]{:S(2)}) collective-permute-start(f32[112,896]{1,0:T(8,128)} %get-tuple-element.36), channel_id=1, source_target_pairs={{0,8},{8,16},{16,24},{24,0},{1,9},{9,17},{17,25},{25,1},{2,10},{10... | collective-permute-start | bytes 1204232 | tf_op jit(solution)/shard_map/ppermute | solution.py:425
  44.1 17.5 %collective-permute-start.5 = (f32[112,896]{1,0:T(8,128)}, f32[112,896]{1,0:T(8,128)}, u32[]{:S(2)}, u32[]{:S(2)}) collective-permute-start(f32[112,896]{1,0:T(8,128)} %get-tuple-element.37), channel_id=1, source_target_pairs={{0,16},{8,24},{16,0},{24,8},{1,17},{9,25},{17,1},{25,9},{2,18},{10... | collective-permute-start | bytes 1204232 | tf_op jit(solution)/shard_map/ppermute | solution.py:425
  45.7 18.9 %collective-permute-start.6 = (f32[112,896]{1,0:T(8,128)}, f32[112,896]{1,0:T(8,128)}, u32[]{:S(2)}, u32[]{:S(2)}) collective-permute-start(f32[112,896]{1,0:T(8,128)} %get-tuple-element.38), channel_id=1, source_target_pairs={{0,24},{8,0},{16,8},{24,16},{1,25},{9,1},{17,9},{25,17},{2,26},{10... | collective-permute-start | bytes 1204232 | tf_op jit(solution)/shard_map/ppermute | solution.py:425
  47.8 34.9 %copy-start.3 = (f32[64,128]{1,0:T(8,128)S(1)}, f32[64,128]{1,0:T(8,128)}, u32[]{:S(2)}) copy-start(f32[64,128]{1,0:T(8,128)} %get-tuple-element.39.q) | copy-start | bytes 98308
  48.5 16.1 %all-to-all-start.2 = ((f32[8,48,128]{2,1,0:T(8,128)}), f32[8,48,128]{2,1,0:T(8,128)S(1)}, u32[]{:S(2)}, u32[]{:S(2)}) async-start(f32[8,48,128]{2,1,0:T(8,128)} %shard_map.60), calls=%async_computation.2 | async-start | bytes 393216 | tf_op jit(solution)/shard_map/all_to_all | solution.py:433
  64.6 90.0 %copy-start.2 = (bf16[1,160,7168]{2,1,0:T(8,128)(2,1)S(1)}, bf16[1,160,7168]{2,1,0:T(8,128)(2,1)}, u32[]{:S(2)}) copy-start(bf16[1,160,7168]{2,1,0:T(8,128)(2,1)} %e.11) | copy-start | bytes 6881284
  144.4 6.4 %collective-permute-start.9 = (bf16[8,64,128]{2,1,0:T(8,128)(2,1)S(1)}, bf16[8,64,128]{2,1,0:T(8,128)(2,1)S(1)}, u32[]{:S(2)}, u32[]{:S(2)}) collective-permute-start(bf16[8,64,128]{2,1,0:T(8,128)(2,1)S(1)} %all_to_all.46.refs_0_), channel_id=1, source_target_pairs={{0,16},{8,24},{16,0},{24,8},{1,17},{9,25},{17,1},{25,9},{2,18},{10... | collective-permute-start | bytes 393224 | tf_op jit(solution)/shard_map/ppermute | solution.py:425
  145.4 7.7 %collective-permute-start.11 = (bf16[8,64,128]{2,1,0:T(8,128)(2,1)S(1)}, bf16[8,64,128]{2,1,0:T(8,128)(2,1)S(1)}, u32[]{:S(2)}, u32[]{:S(2)}) collective-permute-start(bf16[8,64,128]{2,1,0:T(8,128)(2,1)S(1)} %all_to_all.46.refs_0_), channel_id=1, source_target_pairs={{0,8},{8,16},{16,24},{24,0},{1,9},{9,17},{17,25},{25,1},{2,10},{10... | collective-permute-start | bytes 393224 | tf_op jit(solution)/shard_map/ppermute | solution.py:425
  146.0 8.6 %collective-permute-start.7 = (bf16[8,64,128]{2,1,0:T(8,128)(2,1)S(1)}, bf16[8,64,128]{2,1,0:T(8,128)(2,1)S(1)}, u32[]{:S(2)}, u32[]{:S(2)}) collective-permute-start(bf16[8,64,128]{2,1,0:T(8,128)(2,1)S(1)} %all_to_all.46.refs_0_), channel_id=1, source_target_pairs={{0,24},{8,0},{16,8},{24,16},{1,25},{9,1},{17,9},{25,17},{2,26},{10... | collective-permute-start | bytes 393224 | tf_op jit(solution)/shard_map/ppermute | solution.py:425
  148.1 6.5 %collective-permute-start.13 = (bf16[8,64,128]{2,1,0:T(8,128)(2,1)S(1)}, bf16[8,64,128]{2,1,0:T(8,128)(2,1)S(1)}, u32[]{:S(2)}, u32[]{:S(2)}) collective-permute-start(bf16[8,64,128]{2,1,0:T(8,128)(2,1)S(1)} %all_to_all.46.refs_0_), channel_id=1, source_target_pairs={{0,4},{4,0},{1,5},{5,1},{2,6},{6,2},{3,7},{7,3},{8,12},{12,8},{9,1... | collective-permute-start | bytes 393224 | tf_op jit(solution)/shard_map/ppermute | solution.py:429
  150.8 9.0 %collective-permute-start.10 = (bf16[8,64,128]{2,1,0:T(8,128)(2,1)S(1)}, bf16[8,64,128]{2,1,0:T(8,128)(2,1)S(1)}, u32[]{:S(2)}, u32[]{:S(2)}) collective-permute-start(bf16[8,64,128]{2,1,0:T(8,128)(2,1)S(1)} %collective-permute-done.9.refs_1_), channel_id=1, source_target_pairs={{0,4},{4,0},{1,5},{5,1},{2,6},{6,2},{3,7},{7,3},{8,12},{12,8},{9,1... | collective-permute-start | bytes 393224 | tf_op jit(solution)/shard_map/ppermute | solution.py:429
  153.2 6.6 %collective-permute-start.12 = (bf16[8,64,128]{2,1,0:T(8,128)(2,1)S(1)}, bf16[8,64,128]{2,1,0:T(8,128)(2,1)S(1)}, u32[]{:S(2)}, u32[]{:S(2)}) collective-permute-start(bf16[8,64,128]{2,1,0:T(8,128)(2,1)S(1)} %collective-permute-done.11.refs_2_), channel_id=1, source_target_pairs={{0,4},{4,0},{1,5},{5,1},{2,6},{6,2},{3,7},{7,3},{8,12},{12,8},{9,1... | collective-permute-start | bytes 393224 | tf_op jit(solution)/shard_map/ppermute | solution.py:429
  154.6 5.2 %collective-permute-start.8 = (bf16[8,64,128]{2,1,0:T(8,128)(2,1)S(1)}, bf16[8,64,128]{2,1,0:T(8,128)(2,1)S(1)}, u32[]{:S(2)}, u32[]{:S(2)}) collective-permute-start(bf16[8,64,128]{2,1,0:T(8,128)(2,1)S(1)} %collective-permute-done.7.refs_0_), channel_id=1, source_target_pairs={{0,4},{4,0},{1,5},{5,1},{2,6},{6,2},{3,7},{7,3},{8,12},{12,8},{9,1... | collective-permute-start | bytes 393224 | tf_op jit(solution)/shard_map/ppermute | solution.py:429

commit v3 on v2

--- a/solution.py
+++ b/solution.py
@@ -49,19 +49,27 @@
     return jnp.minimum(1.0, scaled * lax.rsqrt(total / REPLICAS + EPS))
 
 
-def prep_kernel(at, g, e, q_all, send, squares, q, own, sems):
+def prep_kernel(g, e, q_all, send, squares, q, at, other, own, sems):
+    core, x, z = (lax.axis_index(axis) for axis in ("c", "x", "z"))
+    at[0], at[1], at[2] = core, x, z
+
     def piece(ref, core, out, sem):
         cols = pl.ds(pl.multiple_of(core * HALF, LANES), HALF)
         return pltpu.make_async_copy(ref.at[0, :, cols], out, sems.at[sem])
 
+    top, low = slice(0, ROWS), slice(ROWS, 2 * ROWS)
+    first = core * 4 * BLOCKS + x * BLOCKS + jnp.minimum(z, BLOCKS - 1)
+    cols = pl.ds(pl.multiple_of(first * LANES, LANES), LANES)
     copies = [
-        piece(g, 1 - at[0], send.at[0:ROWS], 0),
-        piece(g, at[0], own, 1),
-        piece(e, 1 - at[0], send.at[ROWS : 2 * ROWS], 2),
+        piece(g, 1 - core, other.at[top], 0),
+        piece(g, core, own, 1),
+        piece(e, 1 - core, other.at[low], 2),
+        pltpu.make_async_copy(q_all.at[:, cols], q, sems.at[3]),
     ]
-    first = at[0] * 4 * BLOCKS + at[1] * BLOCKS + jnp.minimum(at[2], BLOCKS - 1)
-    cols = pl.ds(pl.multiple_of(first * LANES, LANES), LANES)
-    copies.append(pltpu.make_async_copy(q_all.at[:, cols], q, sems.at[3]))
+    out = [
+        pltpu.make_async_copy(other.at[part], send.at[part], sems.at[4 + k])
+        for k, part in enumerate((top, low))
+    ]
     for copy in copies:
         copy.start()
 
@@ -77,41 +85,42 @@
 
     acc = jnp.zeros((8, HALF // 4), f32)
     copies[0].wait()
-    acc = lax.fori_loop(0, ROWS // 16, rows_of(send), acc)
+    out[0].start()
+    acc = lax.fori_loop(0, ROWS // 16, rows_of(other), acc)
     copies[1].wait()
+    copies[2].wait()
+    out[1].start()
     acc = lax.fori_loop(0, ROWS // 16, rows_of(own), acc)
     part = acc[:, :LANES]
     for lane in range(LANES, HALF // 4, LANES):
         part = part + acc[:, lane : lane + LANES]
     for k in range(SPREAD):
         squares[k] = part
-    copies[2].wait()
     copies[3].wait()
-
-
-def prep(at, grads, error, q_t):
+    for copy in out:
+        copy.wait()
+
+
+def prep(grads, error, q_t):
     hbm = pl.BlockSpec(memory_space=pltpu.HBM)
     return pl.pallas_call(
         prep_kernel,
-        grid_spec=pltpu.PrefetchScalarGridSpec(
-            num_scalar_prefetch=1,
-            grid=(1,),
-            in_specs=[hbm, hbm, hbm],
-            out_specs=[
-                pl.BlockSpec((2 * ROWS, HALF), lambda i, at: (0, 0)),
-                pl.BlockSpec((SPREAD, 8, LANES), lambda i, at: (0, 0, 0)),
-                pl.BlockSpec((RANK, LANES), lambda i, at: (0, 0)),
-            ],
-            scratch_shapes=[VMEM((ROWS, HALF), bf16), pltpu.SemaphoreType.DMA((4,))],
-        ),
+        in_specs=[hbm, hbm, hbm],
+        out_specs=[hbm, whole(), whole(), pl.BlockSpec(memory_space=pltpu.SMEM)],
+        scratch_shapes=[
+            VMEM((2 * ROWS, HALF), bf16),
+            VMEM((ROWS, HALF), bf16),
+            pltpu.SemaphoreType.DMA((6,)),
+        ],
         out_shape=[
             jax.ShapeDtypeStruct((2 * ROWS, HALF), bf16),
             jax.ShapeDtypeStruct((SPREAD, 8, LANES), f32),
             jax.ShapeDtypeStruct((RANK, LANES), f32),
+            jax.ShapeDtypeStruct((3,), jnp.int32),
         ],
         name="prep",
         **room(58, 10**8),
-    )(at, grads, error, q_t)
+    )(grads, error, q_t)
 
 
 def both(g, e, got, row, cols):
@@ -263,18 +272,22 @@
     )(early, late, q)
 
 
+def across(value):
+    return jnp.broadcast_to(jnp.sum(value, axis=1, keepdims=True), value.shape)
+
+
 def orthonormal(a, b):
     groups = RANK // 8
     a = [a[8 * i : 8 * i + 8] for i in range(groups)]
     b = [b[8 * i : 8 * i + 8] for i in range(groups)]
-    place = lax.broadcasted_iota(jnp.int32, (8, 1), 0)
+    place = lax.broadcasted_iota(jnp.int32, (8, LANES), 0)
     for k in range(0, RANK, 2):
         g, r = divmod(k, 8)
         u_a, u_b = a[g][r : r + 1], b[g][r : r + 1]
         w_a, w_b = a[g][r + 1 : r + 2], b[g][r + 1 : r + 2]
         span = range(g, groups)
-        by_u = [jnp.sum(a[i] * u_a + b[i] * u_b, axis=1, keepdims=True) for i in span]
-        by_w = [jnp.sum(a[i] * w_a + b[i] * w_b, axis=1, keepdims=True) for i in span]
+        by_u = [across(a[i] * u_a + b[i] * u_b) for i in span]
+        by_w = [across(a[i] * w_a + b[i] * w_b) for i in span]
         uu, uw = by_u[0][r : r + 1], by_u[0][r + 1 : r + 2]
         ww = by_w[0][r + 1 : r + 2]
         over_u = 1.0 / (uu + EPS)
@@ -292,7 +305,7 @@
             a[i] = a[i] - coeff_u * u_a - coeff_w * w_a
             b[i] = b[i] - coeff_u * u_b - coeff_w * w_b
     for i in range(groups):
-        scale = lax.rsqrt(jnp.sum(a[i] * a[i] + b[i] * b[i], axis=1, keepdims=True) + EPS)
+        scale = lax.rsqrt(across(a[i] * a[i] + b[i] * b[i]) + EPS)
         a[i] = a[i] * scale
         b[i] = b[i] * scale
     return jnp.concatenate(a, axis=0), jnp.concatenate(b, axis=0)
@@ -349,47 +362,47 @@
     )(pack, s)
 
 
-def finish_kernel(n, at, g, e, shrink, p_half, *refs):
+def place_of(which, i, at):
+    place = 0
+    for k, (other, ahead) in enumerate(which):
+        core = 1 - at[0] if other else at[0]
+        place = jnp.where(i == k, core * 4 + lax.rem(at[1] + ahead, 4), place)
+    return place
+
+
+def finish_kernel(which, at, g, e, shrink, p_half, *refs):
+    n = len(which)
     parts, (out, q_t) = refs[:n], refs[-2:]
     shrink = shrink[0:1, 0:1]
+    step = pl.program_id(0)
+    first = place_of(which, step, at) * QUARTER
     for k in range(n):
 
-        @pl.when(pl.program_id(0) == k)
+        @pl.when(step == k)
         def _(part=parts[k]):
             for block in range(BLOCKS):
                 cols = slice(block * LANES, (block + 1) * LANES)
+                here = pl.ds(pl.multiple_of(first + block * LANES, LANES), LANES)
                 q = part[block]
                 approx = jnp.dot(p_half[...], q, preferred_element_type=f32)
-                merged = shrink * g[0, :, cols].astype(f32) + e[0, :, cols].astype(f32)
+                merged = shrink * g[0, :, here].astype(f32) + e[0, :, here].astype(f32)
                 out[0, :, cols] = merged - approx
                 q_t[:, cols] = q.astype(f32)
 
 
 def finish(at, which, grads, error, shrink, p_half, parts, before=()):
     n = len(parts)
-
-    def column(i, at):
-        place = 0
-        for k, (other, ahead) in enumerate(which):
-            core = 1 - at[0] if other else at[0]
-            place = jnp.where(i == k, core * 4 + lax.rem(at[1] + ahead, 4), place)
-        return place
-
-    tile = pl.BlockSpec((1, ROWS, QUARTER), lambda i, at: (0, 0, column(i, at)))
-    return pl.pallas_call(
-        functools.partial(finish_kernel, n),
+    column = functools.partial(place_of, which)
+    return pl.pallas_call(
+        functools.partial(finish_kernel, which),
         grid_spec=pltpu.PrefetchScalarGridSpec(
             num_scalar_prefetch=1,
             grid=(n,),
-            in_specs=[
-                tile,
-                tile,
-                pl.BlockSpec((8, LANES), lambda i, at: (0, 0)),
-                pl.BlockSpec((ROWS, RANK), lambda i, at: (0, 0)),
-            ]
-            + [pl.BlockSpec((8, RANK, LANES), lambda i, at: (0, 0, 0))] * n
-            + [pl.BlockSpec(memory_space=pl.ANY)] * len(before),
-            out_specs=[tile, pl.BlockSpec((RANK, QUARTER), lambda i, at: (0, column(i, at)))],
+            in_specs=[whole()] * (4 + n) + [pl.BlockSpec(memory_space=pl.ANY)] * len(before),
+            out_specs=[
+                pl.BlockSpec((1, ROWS, QUARTER), lambda i, at: (0, 0, column(i, at))),
+                pl.BlockSpec((RANK, QUARTER), lambda i, at: (0, column(i, at))),
+            ],
         ),
         out_shape=[
             jax.ShapeDtypeStruct((1, ROWS, LOCAL), f32),
@@ -442,9 +455,8 @@
 
 
 def step(grads, error, q_init):
-    at = jnp.stack([lax.axis_index("c"), lax.axis_index("x"), lax.axis_index("z")]).astype(jnp.int32)
     chip = ("x", "c", "y")
-    send, squares, q = prep(at, grads, error, q_init.T)
+    send, squares, q, at = prep(grads, error, q_init.T)
     got = swap(send, "c")
     squares = exchange(squares, chip)
     *early, squares = merge(early_kernel, at, grads, error, got, squares, 2 * EARLY, (8,))
@@ -461,7 +473,8 @@
     pack = exchange(respread(exchange(pack, "z"), SPREAD), chip)
 
     p_t, p_half, q = factor(pack, s)
-    parts = from_ring(exchange(q, "z"), "x")
+    q = exchange(q, "z")
+    parts = from_ring(q, "x")
     others = [swap(part, "c") for part in parts]
     args = (grads, error, shrink, p_half)
     outs = finish(at, [(0, 0), (1, 0)], *args, [parts[0], others[0]])

time: 163 us -> 157 us (0.963)
  Pallas kernels: 32.3 us -> 26.3 us
    pallas_call x1, Pallas kernels: 13.4 us -> 8.61 us  [factor(): pl.pallas_call(factor_kernel, in_specs=[whole()] * 2, out_specs=[whole()]...]
where the time goes in v3:
time: 157 us
  blocking collectives  92.3 us (59%)
  Pallas kernels  26.3 us (17%)
  starting transfers between devices  24.1 us (15%)
  waiting for transfers between devices  12.7 us (8%)
    all_to_all x7, blocking collectives, exchange(): return lax.all_to_all(blocks, axis, 0, 0, tiled=True)  92.3 us
    ppermute x9, waiting for transfers between devices, shifted(): return lax.ppermute(value, axis, [(i, (i - by) % n) for i in range(n)])  12.7 us
    ppermute x9, starting transfers between devices, shifted(): return lax.ppermute(value, axis, [(i, (i - by) % n) for i in range(n)])  11 us
    ppermute x5, starting transfers between devices, swap(): return lax.ppermute(value, axis, [(0, 1), (1, 0)])  9.76 us
    pallas_call x1, Pallas kernels, factor(): pl.pallas_call(factor_kernel, in_specs=[whole()] * 2, out_specs=[whole()]...  8.61 us
    pallas_call x3, Pallas kernels, finish(): pl.pallas_call(functools.partial(finish_kernel, which), grid_spec=pltpu.P...  7.78 us
    pallas_call x1, Pallas kernels, prep(): pl.pallas_call(prep_kernel, in_specs=[hbm, hbm, hbm], out_specs=[hbm, who...  3.83 us
    all_to_all x1, starting transfers between devices, exchange(): return lax.all_to_all(blocks, axis, 0, 0, tiled=True)  3.39 us
  transfers between devices with their start and end apart: 15, of which 3 were waited for; matrix products, arithmetic and copies ran while one was open for 0% of the time, Pallas kernels for 5%

profile of v3, /device:TPU:1, one launch (start us, length us, event | category | flops | bytes accessed | tf_op | source)
XLA Modules:
  0.0 156.8 jit_solution(3766821210279615958)
XLA Ops:
  0.6 0.0 copy-start
  0.6 0.0 copy-start.1
  0.7 3.8 %prep.1 = (bf16[320,3584]{1,0:T(8,128)(2,1)}, f32[32,8,128]{2,1,0:T(8,128)}, f32[64,128]{1,0:T(8,128)}, s32[3]{0:T(128)}) custom-call(bf16[1,160,7168]{2,1,0:T(8,128)(2,1)} %g.11, bf16[1,160,7168]{2,1,0:T(8,128)(2,1)} %e.11, f32[64,7168]{1,0:T(8,128)} %bitcast.4), custom_call_target="tpu_custom_call" | custom-call | flops 100000000 | bytes 1048576 | tf_op jit(solution)/shard_map/prep/pallas_call | solution.py:106
  4.5 3.3 %collective-permute-start = (bf16[320,3584]{1,0:T(8,128)(2,1)}, bf16[320,3584]{1,0:T(8,128)(2,1)S(1)}, u32[]{:S(2)}, u32[]{:S(2)}) collective-permute-start(bf16[320,3584]{1,0:T(8,128)(2,1)} %get-tuple-element.29), channel_id=1, source_target_pairs={{0,4},{4,0},{1,5},{5,1},{2,6},{6,2},{3,7},{7,3},{8,12},{12,8},{9,1... | collective-permute-start | bytes 6881288 | tf_op jit(solution)/shard_map/ppermute | solution.py:442
  7.8 13.1 %all_to_all.40.squares = f32[32,8,128]{2,1,0:T(8,128)S(1)} all-to-all(f32[32,8,128]{2,1,0:T(8,128)} %get-tuple-element.30), channel_id=1, replica_groups=mesh['z'=8,'x'=4,'c'=2,'y'=4] {'x','c','y'}, dimensions={0} | all-to-all | bytes 262144 | tf_op jit(solution)/shard_map/all_to_all | solution.py:446
  20.8 0.0 collective-permute-done.got
  20.8 0.0 copy-done
  20.8 0.0 copy-done.1
  20.8 0.0 copy-start.4
  20.9 0.6 copy-done.4
  21.4 1.0 shard_map.58
  22.4 0.5 collective-permute-start.1
  22.9 1.7 %collective-permute-start.2 = (f32[96,896]{1,0:T(8,128)S(1)}, f32[96,896]{1,0:T(8,128)S(1)}, u32[]{:S(2)}, u32[]{:S(2)}) collective-permute-start(f32[96,896]{1,0:T(8,128)S(1)} %get-tuple-element.33), channel_id=1, source_target_pairs={{0,16},{8,24},{16,0},{24,8},{1,17},{9,25},{17,1},{25,9},{2,18},{10... | collective-permute-start | bytes 1032200 | tf_op jit(solution)/shard_map/ppermute | solution.py:438
  24.6 1.0 collective-permute-start.3
  25.6 14.9 %all_to_all.41.squares = f32[8,8,128]{2,1,0:T(8,128)S(1)} all-to-all(f32[8,8,128]{2,1,0:T(8,128)S(1)} %get-tuple-element.35), channel_id=1, replica_groups=mesh['z'=8,'x'=4,'c'=2,'y'=4] {'z'}, dimensions={0} | all-to-all | bytes 65536 | tf_op jit(solution)/shard_map/all_to_all | solution.py:446
  40.5 2.3 %shard_map.59 = (f32[112,896]{1,0:T(8,128)S(1)}, f32[112,896]{1,0:T(8,128)}, f32[112,896]{1,0:T(8,128)}, f32[112,896]{1,0:T(8,128)}, f32[8,128]{1,0:T(8,128)S(1)}) custom-call(s32[3]{0:T(128)S(1)} %copy-done.4, bf16[1,160,7168]{2,1,0:T(8,128)(2,1)S(1)} %copy-done, bf16[1,160,7168]{2,1,0:T(8,128)(2,1)S(1)} %copy-done.1, ...), custom_call_target="tpu_custom_call" | custom-call | flops 1000000000 | bytes 1048576 | tf_op jit(solution)/shard_map/pallas_call | solution.py:169
  42.8 0.4 collective-permute-start.4
  43.3 1.6 collective-permute-start.5
  44.8 0.0 collective-permute-done.1.b
  44.8 2.1 %collective-permute-start.6 = (f32[112,896]{1,0:T(8,128)}, f32[112,896]{1,0:T(8,128)}, u32[]{:S(2)}, u32[]{:S(2)}) collective-permute-start(f32[112,896]{1,0:T(8,128)} %get-tuple-element.40), channel_id=1, source_target_pairs={{0,24},{8,0},{16,8},{24,16},{1,25},{9,1},{17,9},{25,17},{2,26},{10... | collective-permute-start | bytes 1204232 | tf_op jit(solution)/shard_map/ppermute | solution.py:438
  46.9 0.0 collective-permute-done.2.c
  46.9 0.0 collective-permute-done.3.d
  46.9 0.0 copy-start.3
  46.9 0.8 shard_map.60
  47.6 3.4 %all-to-all-start.2 = ((f32[8,48,128]{2,1,0:T(8,128)}), f32[8,48,128]{2,1,0:T(8,128)S(1)}, u32[]{:S(2)}, u32[]{:S(2)}) async-start(f32[8,48,128]{2,1,0:T(8,128)} %shard_map.60), calls=%async_computation.2 | async-start | bytes 393216 | tf_op jit(solution)/shard_map/all_to_all | solution.py:446
  51.0 1.9 %collective-permute-done.4.b = f32[112,896]{1,0:T(8,128)S(1)} collective-permute-done((f32[112,896]{1,0:T(8,128)}, f32[112,896]{1,0:T(8,128)S(1)}, u32[]{:S(2)}, u32[]{:S(2)}) %collective-permute-start.4) | collective-permute-done | bytes 401440 | tf_op jit(solution)/shard_map/ppermute | solution.py:438
  52.9 7.8 %collective-permute-done.5.c = f32[112,896]{1,0:T(8,128)} collective-permute-done((f32[112,896]{1,0:T(8,128)}, f32[112,896]{1,0:T(8,128)}, u32[]{:S(2)}, u32[]{:S(2)}) %collective-permute-start.5) | collective-permute-done | bytes 401440 | tf_op jit(solution)/shard_map/ppermute | solution.py:438
  60.8 3.0 %collective-permute-done.6.d = f32[112,896]{1,0:T(8,128)} collective-permute-done((f32[112,896]{1,0:T(8,128)}, f32[112,896]{1,0:T(8,128)}, u32[]{:S(2)}, u32[]{:S(2)}) %collective-permute-start.6) | collective-permute-done | bytes 401440 | tf_op jit(solution)/shard_map/ppermute | solution.py:438
  63.7 0.0 all-to-all-done.2.after.early
  63.8 0.0 copy-start.2
  63.8 0.0 copy-start.5
  63.8 1.4 shard_map.61
  65.1 16.6 %all_to_all.42.late = f32[8,112,128]{2,1,0:T(8,128)S(1)} all-to-all(f32[8,112,128]{2,1,0:T(8,128)S(1)} %shard_map.61), channel_id=1, replica_groups=mesh['z'=8,'x'=4,'c'=2,'y'=4] {'z'}, dimensions={0} | all-to-all | bytes 917504 | tf_op jit(solution)/shard_map/all_to_all | solution.py:446
  81.8 0.0 copy-done.3
  81.8 0.5 terms.1
  82.3 15.4 %all_to_all.43.blocks = f32[32,8,128]{2,1,0:T(8,128)S(1)} all-to-all(f32[32,8,128]{2,1,0:T(8,128)S(1)} %get-tuple-element.42), channel_id=1, replica_groups=mesh['z'=8,'x'=4,'c'=2,'y'=4] {'x','c','y'}, dimensions={0} | all-to-all | bytes 262144 | tf_op jit(solution)/shard_map/all_to_all | solution.py:446
  97.8 9.2 %all_to_all.44.blocks = f32[8,8,128]{2,1,0:T(8,128)S(1)} all-to-all(f32[8,8,128]{2,1,0:T(8,128)S(1)} %respread.2), channel_id=1, replica_groups=mesh['z'=8,'x'=4,'c'=2,'y'=4] {'z'}, dimensions={0} | all-to-all | bytes 65536 | tf_op jit(solution)/shard_map/all_to_all | solution.py:446
  107.0 12.5 %all_to_all.45.pack = f32[32,8,128]{2,1,0:T(8,128)S(1)} all-to-all(f32[32,8,128]{2,1,0:T(8,128)S(1)} %respread.3), channel_id=1, replica_groups=mesh['z'=8,'x'=4,'c'=2,'y'=4] {'x','c','y'}, dimensions={0} | all-to-all | bytes 262144 | tf_op jit(solution)/shard_map/all_to_all | solution.py:446
  119.6 8.6 %factor.1 = (f32[64,160]{1,0:T(8,128)}, bf16[160,64]{1,0:T(8,128)(2,1)S(1)}, bf16[8,64,128]{2,1,0:T(8,128)(2,1)S(1)}) custom-call(f32[32,8,128]{2,1,0:T(8,128)S(1)} %all_to_all.45.pack, f32[160,128]{1,0:T(8,128)S(1)} %get-tuple-element.43.s), custom_call_target="tpu_custom_call" | custom-call | flops 100000000 | bytes 1048576 | tf_op jit(solution)/shard_map/factor/pallas_call | solution.py:351
  128.2 10.5 %all_to_all.46.refs_0_ = bf16[8,64,128]{2,1,0:T(8,128)(2,1)S(1)} all-to-all(bf16[8,64,128]{2,1,0:T(8,128)(2,1)S(1)} %get-tuple-element.46), channel_id=1, replica_groups=mesh['z'=8,'x'=4,'c'=2,'y'=4] {'z'}, dimensions={0} | all-to-all | bytes 262144 | tf_op jit(solution)/shard_map/all_to_all | solution.py:446
  138.7 1.1 collective-permute-start.9
  139.8 0.6 collective-permute-start.11
  140.3 2.1 %collective-permute-start.7 = (bf16[8,64,128]{2,1,0:T(8,128)(2,1)S(1)}, bf16[8,64,128]{2,1,0:T(8,128)(2,1)S(1)}, u32[]{:S(2)}, u32[]{:S(2)}) collective-permute-start(bf16[8,64,128]{2,1,0:T(8,128)(2,1)S(1)} %all_to_all.46.refs_0_), channel_id=1, source_target_pairs={{0,24},{8,0},{16,8},{24,16},{1,25},{9,1},{17,9},{25,17},{2,26},{10... | collective-permute-start | bytes 393224 | tf_op jit(solution)/shard_map/ppermute | solution.py:438
  142.5 2.6 %collective-permute-start.13 = (bf16[8,64,128]{2,1,0:T(8,128)(2,1)S(1)}, bf16[8,64,128]{2,1,0:T(8,128)(2,1)S(1)}, u32[]{:S(2)}, u32[]{:S(2)}) collective-permute-start(bf16[8,64,128]{2,1,0:T(8,128)(2,1)S(1)} %all_to_all.46.refs_0_), channel_id=1, source_target_pairs={{0,4},{4,0},{1,5},{5,1},{2,6},{6,2},{3,7},{7,3},{8,12},{12,8},{9,1... | collective-permute-start | bytes 393224 | tf_op jit(solution)/shard_map/ppermute | solution.py:442
  145.1 0.0 collective-permute-done.9.refs_1_
  145.1 2.4 %collective-permute-start.10 = (bf16[8,64,128]{2,1,0:T(8,128)(2,1)S(1)}, bf16[8,64,128]{2,1,0:T(8,128)(2,1)S(1)}, u32[]{:S(2)}, u32[]{:S(2)}) collective-permute-start(bf16[8,64,128]{2,1,0:T(8,128)(2,1)S(1)} %collective-permute-done.9.refs_1_), channel_id=1, source_target_pairs={{0,4},{4,0},{1,5},{5,1},{2,6},{6,2},{3,7},{7,3},{8,12},{12,8},{9,1... | collective-permute-start | bytes 393224 | tf_op jit(solution)/shard_map/ppermute | solution.py:442
  147.5 0.0 collective-permute-done.11.refs_2_
  147.5 1.4 collective-permute-start.12
  148.9 0.0 collective-permute-done.7.refs_0_
  148.9 0.0 collective-permute-start.8
  148.9 0.0 collective-permute-done.13.refs_1_
  149.0 0.0 copy-done.2
  149.0 0.0 copy-done.5
  149.0 2.0 %finish.3 = (f32[1,160,7168]{2,1,0:T(8,128)}, f32[64,7168]{1,0:T(8,128)}) custom-call(s32[3]{0:T(128)S(1)} %copy-done.5, bf16[1,160,7168]{2,1,0:T(8,128)(2,1)S(1)} %copy-done, bf16[1,160,7168]{2,1,0:T(8,128)(2,1)S(1)} %copy-done.2, f32[8,128]{1,0:T(8,128)S(1)} %get-tuple-element.36.shrink, bf16[160,64]{1,0:T(8,128)(2,1)S(1)} %get-tuple-element.45.p_half, ...), custom_call_target="tpu_custom_call" | custom-call | flops 1000000000 | bytes 1048576 | tf_op jit(solution)/shard_map/finish/pallas_call | solution.py:396
  151.0 2.9 %finish.4 = (f32[1,160,7168]{2,1,0:T(8,128)}, f32[64,7168]{1,0:T(8,128)}) custom-call(s32[3]{0:T(128)S(1)} %copy-done.5, bf16[1,160,7168]{2,1,0:T(8,128)(2,1)S(1)} %copy-done, bf16[1,160,7168]{2,1,0:T(8,128)(2,1)S(1)} %copy-done.2, f32[8,128]{1,0:T(8,128)S(1)} %get-tuple-element.36.shrink, ...), custom_call_target="tpu_custom_call", output_to_operand_aliasing={{0}: (8, {}), {1}: (9, {})} | custom-call | flops 1000000000 | bytes 1048576 | tf_op jit(solution)/shard_map/finish/pallas_call | solution.py:396
  153.9 0.0 collective-permute-done.10.refs_1_
  153.9 0.0 collective-permute-done.12.refs_2_
  153.9 0.0 collective-permute-done.8.refs_0_
  153.9 2.9 %finish.5 = (f32[1,160,7168]{2,1,0:T(8,128)}, f32[64,7168]{1,0:T(8,128)}) custom-call(s32[3]{0:T(128)S(1)} %copy-done.5, bf16[1,160,7168]{2,1,0:T(8,128)(2,1)S(1)} %copy-done, bf16[1,160,7168]{2,1,0:T(8,128)(2,1)S(1)} %copy-done.2, f32[8,128]{1,0:T(8,128)S(1)} %get-tuple-element.36.shrink, ...), custom_call_target="tpu_custom_call", output_to_operand_aliasing={{0}: (8, {}), {1}: (9, {})} | custom-call | flops 1000000000 | bytes 1048576 | tf_op jit(solution)/shard_map/finish/pallas_call | solution.py:396
  (2 shorter events, 0.1 us)
Async XLA Ops:
  0.6 20.2 %copy-start = (bf16[1,160,7168]{2,1,0:T(8,128)(2,1)S(1)}, bf16[1,160,7168]{2,1,0:T(8,128)(2,1)}, u32[]{:S(2)}) copy-start(bf16[1,160,7168]{2,1,0:T(8,128)(2,1)} %g.11) | copy-start | bytes 6881284
  0.6 20.2 %copy-start.1 = (bf16[1,160,7168]{2,1,0:T(8,128)(2,1)S(1)}, bf16[1,160,7168]{2,1,0:T(8,128)(2,1)}, u32[]{:S(2)}) copy-start(bf16[1,160,7168]{2,1,0:T(8,128)(2,1)} %e.11) | copy-start | bytes 6881284
  4.5 16.3 %collective-permute-start = (bf16[320,3584]{1,0:T(8,128)(2,1)}, bf16[320,3584]{1,0:T(8,128)(2,1)S(1)}, u32[]{:S(2)}, u32[]{:S(2)}) collective-permute-start(bf16[320,3584]{1,0:T(8,128)(2,1)} %get-tuple-element.29), channel_id=1, source_target_pairs={{0,4},{4,0},{1,5},{5,1},{2,6},{6,2},{3,7},{7,3},{8,12},{12,8},{9,1... | collective-permute-start | bytes 6881288 | tf_op jit(solution)/shard_map/ppermute | solution.py:442
  20.8 0.6 copy-start.4
  22.4 22.4 %collective-permute-start.1 = (f32[96,896]{1,0:T(8,128)S(1)}, f32[96,896]{1,0:T(8,128)S(1)}, u32[]{:S(2)}, u32[]{:S(2)}) collective-permute-start(f32[96,896]{1,0:T(8,128)S(1)} %get-tuple-element.32), channel_id=1, source_target_pairs={{0,8},{8,16},{16,24},{24,0},{1,9},{9,17},{17,25},{25,1},{2,10},{10... | collective-permute-start | bytes 1032200 | tf_op jit(solution)/shard_map/ppermute | solution.py:438
  22.9 24.0 %collective-permute-start.2 = (f32[96,896]{1,0:T(8,128)S(1)}, f32[96,896]{1,0:T(8,128)S(1)}, u32[]{:S(2)}, u32[]{:S(2)}) collective-permute-start(f32[96,896]{1,0:T(8,128)S(1)} %get-tuple-element.33), channel_id=1, source_target_pairs={{0,16},{8,24},{16,0},{24,8},{1,17},{9,25},{17,1},{25,9},{2,18},{10... | collective-permute-start | bytes 1032200 | tf_op jit(solution)/shard_map/ppermute | solution.py:438
  24.6 22.3 %collective-permute-start.3 = (f32[96,896]{1,0:T(8,128)S(1)}, f32[96,896]{1,0:T(8,128)S(1)}, u32[]{:S(2)}, u32[]{:S(2)}) collective-permute-start(f32[96,896]{1,0:T(8,128)S(1)} %get-tuple-element.34), channel_id=1, source_target_pairs={{0,24},{8,0},{16,8},{24,16},{1,25},{9,1},{17,9},{25,17},{2,26},{10... | collective-permute-start | bytes 1032200 | tf_op jit(solution)/shard_map/ppermute | solution.py:438
  42.8 10.1 %collective-permute-start.4 = (f32[112,896]{1,0:T(8,128)}, f32[112,896]{1,0:T(8,128)S(1)}, u32[]{:S(2)}, u32[]{:S(2)}) collective-permute-start(f32[112,896]{1,0:T(8,128)} %get-tuple-element.38), channel_id=1, source_target_pairs={{0,8},{8,16},{16,24},{24,0},{1,9},{9,17},{17,25},{25,1},{2,10},{10... | collective-permute-start | bytes 1204232 | tf_op jit(solution)/shard_map/ppermute | solution.py:438
  43.3 17.5 %collective-permute-start.5 = (f32[112,896]{1,0:T(8,128)}, f32[112,896]{1,0:T(8,128)}, u32[]{:S(2)}, u32[]{:S(2)}) collective-permute-start(f32[112,896]{1,0:T(8,128)} %get-tuple-element.39), channel_id=1, source_target_pairs={{0,16},{8,24},{16,0},{24,8},{1,17},{9,25},{17,1},{25,9},{2,18},{10... | collective-permute-start | bytes 1204232 | tf_op jit(solution)/shard_map/ppermute | solution.py:438
  44.8 18.9 %collective-permute-start.6 = (f32[112,896]{1,0:T(8,128)}, f32[112,896]{1,0:T(8,128)}, u32[]{:S(2)}, u32[]{:S(2)}) collective-permute-start(f32[112,896]{1,0:T(8,128)} %get-tuple-element.40), channel_id=1, source_target_pairs={{0,24},{8,0},{16,8},{24,16},{1,25},{9,1},{17,9},{25,17},{2,26},{10... | collective-permute-start | bytes 1204232 | tf_op jit(solution)/shard_map/ppermute | solution.py:438
  46.9 34.9 %copy-start.3 = (f32[64,128]{1,0:T(8,128)S(1)}, f32[64,128]{1,0:T(8,128)}, u32[]{:S(2)}) copy-start(f32[64,128]{1,0:T(8,128)} %get-tuple-element.41.q) | copy-start | bytes 98308
  47.6 16.1 %all-to-all-start.2 = ((f32[8,48,128]{2,1,0:T(8,128)}), f32[8,48,128]{2,1,0:T(8,128)S(1)}, u32[]{:S(2)}, u32[]{:S(2)}) async-start(f32[8,48,128]{2,1,0:T(8,128)} %shard_map.60), calls=%async_computation.2 | async-start | bytes 393216 | tf_op jit(solution)/shard_map/all_to_all | solution.py:446
  63.8 85.2 %copy-start.2 = (bf16[1,160,7168]{2,1,0:T(8,128)(2,1)S(1)}, bf16[1,160,7168]{2,1,0:T(8,128)(2,1)}, u32[]{:S(2)}) copy-start(bf16[1,160,7168]{2,1,0:T(8,128)(2,1)} %e.11) | copy-start | bytes 6881284
  63.8 85.2 %copy-start.5 = (s32[3]{0:T(128)S(1)}, s32[3]{0:T(128)}, u32[]{:S(2)}) copy-start(s32[3]{0:T(128)} %get-tuple-element.28.at) | copy-start | bytes 40
  138.7 6.4 %collective-permute-start.9 = (bf16[8,64,128]{2,1,0:T(8,128)(2,1)S(1)}, bf16[8,64,128]{2,1,0:T(8,128)(2,1)S(1)}, u32[]{:S(2)}, u32[]{:S(2)}) collective-permute-start(bf16[8,64,128]{2,1,0:T(8,128)(2,1)S(1)} %all_to_all.46.refs_0_), channel_id=1, source_target_pairs={{0,16},{8,24},{16,0},{24,8},{1,17},{9,25},{17,1},{25,9},{2,18},{10... | collective-permute-start | bytes 393224 | tf_op jit(solution)/shard_map/ppermute | solution.py:438
  139.8 7.7 %collective-permute-start.11 = (bf16[8,64,128]{2,1,0:T(8,128)(2,1)S(1)}, bf16[8,64,128]{2,1,0:T(8,128)(2,1)S(1)}, u32[]{:S(2)}, u32[]{:S(2)}) collective-permute-start(bf16[8,64,128]{2,1,0:T(8,128)(2,1)S(1)} %all_to_all.46.refs_0_), channel_id=1, source_target_pairs={{0,8},{8,16},{16,24},{24,0},{1,9},{9,17},{17,25},{25,1},{2,10},{10... | collective-permute-start | bytes 393224 | tf_op jit(solution)/shard_map/ppermute | solution.py:438
  140.3 8.6 %collective-permute-start.7 = (bf16[8,64,128]{2,1,0:T(8,128)(2,1)S(1)}, bf16[8,64,128]{2,1,0:T(8,128)(2,1)S(1)}, u32[]{:S(2)}, u32[]{:S(2)}) collective-permute-start(bf16[8,64,128]{2,1,0:T(8,128)(2,1)S(1)} %all_to_all.46.refs_0_), channel_id=1, source_target_pairs={{0,24},{8,0},{16,8},{24,16},{1,25},{9,1},{17,9},{25,17},{2,26},{10... | collective-permute-start | bytes 393224 | tf_op jit(solution)/shard_map/ppermute | solution.py:438
  142.5 6.5 %collective-permute-start.13 = (bf16[8,64,128]{2,1,0:T(8,128)(2,1)S(1)}, bf16[8,64,128]{2,1,0:T(8,128)(2,1)S(1)}, u32[]{:S(2)}, u32[]{:S(2)}) collective-permute-start(bf16[8,64,128]{2,1,0:T(8,128)(2,1)S(1)} %all_to_all.46.refs_0_), channel_id=1, source_target_pairs={{0,4},{4,0},{1,5},{5,1},{2,6},{6,2},{3,7},{7,3},{8,12},{12,8},{9,1... | collective-permute-start | bytes 393224 | tf_op jit(solution)/shard_map/ppermute | solution.py:442
  145.1 8.7 %collective-permute-start.10 = (bf16[8,64,128]{2,1,0:T(8,128)(2,1)S(1)}, bf16[8,64,128]{2,1,0:T(8,128)(2,1)S(1)}, u32[]{:S(2)}, u32[]{:S(2)}) collective-permute-start(bf16[8,64,128]{2,1,0:T(8,128)(2,1)S(1)} %collective-permute-done.9.refs_1_), channel_id=1, source_target_pairs={{0,4},{4,0},{1,5},{5,1},{2,6},{6,2},{3,7},{7,3},{8,12},{12,8},{9,1... | collective-permute-start | bytes 393224 | tf_op jit(solution)/shard_map/ppermute | solution.py:442
  147.5 6.3 %collective-permute-start.12 = (bf16[8,64,128]{2,1,0:T(8,128)(2,1)S(1)}, bf16[8,64,128]{2,1,0:T(8,128)(2,1)S(1)}, u32[]{:S(2)}, u32[]{:S(2)}) collective-permute-start(bf16[8,64,128]{2,1,0:T(8,128)(2,1)S(1)} %collective-permute-done.11.refs_2_), channel_id=1, source_target_pairs={{0,4},{4,0},{1,5},{5,1},{2,6},{6,2},{3,7},{7,3},{8,12},{12,8},{9,1... | collective-permute-start | bytes 393224 | tf_op jit(solution)/shard_map/ppermute | solution.py:442
  148.9 4.9 %collective-permute-start.8 = (bf16[8,64,128]{2,1,0:T(8,128)(2,1)S(1)}, bf16[8,64,128]{2,1,0:T(8,128)(2,1)S(1)}, u32[]{:S(2)}, u32[]{:S(2)}) collective-permute-start(bf16[8,64,128]{2,1,0:T(8,128)(2,1)S(1)} %collective-permute-done.7.refs_0_), channel_id=1, source_target_pairs={{0,4},{4,0},{1,5},{5,1},{2,6},{6,2},{3,7},{7,3},{8,12},{12,8},{9,1... | collective-permute-start | bytes 393224 | tf_op jit(solution)/shard_map/ppermute | solution.py:442

commit v4 on v3

--- a/solution.py
+++ b/solution.py
@@ -49,9 +49,8 @@
     return jnp.minimum(1.0, scaled * lax.rsqrt(total / REPLICAS + EPS))
 
 
-def prep_kernel(g, e, q_all, send, squares, q, at, other, own, sems):
+def prep_kernel(g, e, q_all, send, squares, q, other, own, sems):
     core, x, z = (lax.axis_index(axis) for axis in ("c", "x", "z"))
-    at[0], at[1], at[2] = core, x, z
 
     def piece(ref, core, out, sem):
         cols = pl.ds(pl.multiple_of(core * HALF, LANES), HALF)
@@ -106,7 +105,7 @@
     return pl.pallas_call(
         prep_kernel,
         in_specs=[hbm, hbm, hbm],
-        out_specs=[hbm, whole(), whole(), pl.BlockSpec(memory_space=pltpu.SMEM)],
+        out_specs=[hbm, whole(), whole()],
         scratch_shapes=[
             VMEM((2 * ROWS, HALF), bf16),
             VMEM((ROWS, HALF), bf16),
@@ -116,27 +115,29 @@
             jax.ShapeDtypeStruct((2 * ROWS, HALF), bf16),
             jax.ShapeDtypeStruct((SPREAD, 8, LANES), f32),
             jax.ShapeDtypeStruct((RANK, LANES), f32),
-            jax.ShapeDtypeStruct((3,), jnp.int32),
         ],
         name="prep",
         **room(58, 10**8),
     )(grads, error, q_t)
 
 
-def both(g, e, got, row, cols):
+def both(g, e, got, row, core, place):
     here = pl.ds(row, 16)
-    gradient = g[0, here, cols].astype(f32) + got[here, cols].astype(f32)
-    residue = e[0, here, cols].astype(f32) + got[pl.ds(ROWS + row, 16), cols].astype(f32)
+    mine = pl.ds(pl.multiple_of(core * HALF + place * QUARTER, LANES), QUARTER)
+    cols = pl.ds(pl.multiple_of(place * QUARTER, LANES), QUARTER)
+    gradient = g[0, here, mine].astype(f32) + got[here, cols].astype(f32)
+    residue = e[0, here, mine].astype(f32) + got[pl.ds(ROWS + row, 16), cols].astype(f32)
     return gradient, residue
 
 
-def early_kernel(at, g, e, got, squares, *outs):
+def early_kernel(g, e, got, squares, *outs):
     outs, spread = outs[:4], outs[4]
+    core, x = lax.axis_index("c"), lax.axis_index("x")
     for j, out in enumerate(outs):
-        cols = pl.ds(pl.multiple_of(lax.rem(at[1] + j, 4) * QUARTER, LANES), QUARTER)
-
-        def rows(i, carry, out=out, cols=cols):
-            gradient, residue = both(g, e, got, i * 16, cols)
+        place = lax.rem(x + j, 4)
+
+        def rows(i, carry, out=out, place=place):
+            gradient, residue = both(g, e, got, i * 16, core, place)
             out[pl.ds(i * 16, 16), :] = gradient
             out[pl.ds(EARLY + i * 16, 16), :] = residue
             return carry
@@ -147,44 +148,31 @@
         spread[k] = total
 
 
-def late_kernel(at, g, e, got, squares, *outs):
+def late_kernel(g, e, got, squares, *outs):
     outs, spread = outs[:4], outs[4]
+    core, x = lax.axis_index("c"), lax.axis_index("x")
     shrink = shrink_of(squares[...])
     spread[...] = jnp.broadcast_to(shrink, (8, LANES))
     for j, out in enumerate(outs):
-        cols = pl.ds(pl.multiple_of(lax.rem(at[1] + j, 4) * QUARTER, LANES), QUARTER)
-
-        def rows(i, carry, out=out, cols=cols):
-            gradient, residue = both(g, e, got, EARLY + i * 16, cols)
+        place = lax.rem(x + j, 4)
+
+        def rows(i, carry, out=out, place=place):
+            gradient, residue = both(g, e, got, EARLY + i * 16, core, place)
             out[pl.ds(i * 16, 16), :] = shrink * gradient + residue
             return carry
 
         lax.fori_loop(0, LATE // 16, rows, 0)
 
 
-def merge(kernel, at, grads, error, got, squares, rows, spread):
-    own = pl.BlockSpec((1, ROWS, HALF), lambda i, at: (0, 0, at[0]))
-    outs = [((rows, QUARTER), f32)] * 4
-    outs = outs + [((*spread, 8, LANES), f32)]
+def merge(kernel, grads, error, got, squares, rows, spread):
+    outs = [(rows, QUARTER)] * 4 + [(*spread, 8, LANES)]
     return pl.pallas_call(
         kernel,
-        grid_spec=pltpu.PrefetchScalarGridSpec(
-            num_scalar_prefetch=1,
-            grid=(1,),
-            in_specs=[
-                own,
-                own,
-                pl.BlockSpec((2 * ROWS, HALF), lambda i, at: (0, 0)),
-                pl.BlockSpec(squares.shape, lambda i, at: (0, 0, 0)),
-            ],
-            out_specs=[
-                pl.BlockSpec(shape, lambda i, at, shape=shape: (0,) * len(shape))
-                for shape, _ in outs
-            ],
-        ),
-        out_shape=[jax.ShapeDtypeStruct(*out) for out in outs],
+        in_specs=[whole()] * 4,
+        out_specs=[whole()] * len(outs),
+        out_shape=[jax.ShapeDtypeStruct(shape, f32) for shape in outs],
         **room(16, 10**9),
-    )(at, grads, error, got, squares)
+    )(grads, error, got, squares)
 
 
 def fold_early_kernel(a, b, c, d, shrink, out):
@@ -362,56 +350,56 @@
     )(pack, s)
 
 
-def place_of(which, i, at):
-    place = 0
+def finish_kernel(which, g, e, shrink, p_half, *refs):
+    n = len(which)
+    parts = refs[:n]
+    out, q_t, new, right_part, sems = refs[-5:]
+    shrink = shrink[0:1, 0:1]
+    core, x = lax.axis_index("c"), lax.axis_index("x")
+    copies = []
     for k, (other, ahead) in enumerate(which):
-        core = 1 - at[0] if other else at[0]
-        place = jnp.where(i == k, core * 4 + lax.rem(at[1] + ahead, 4), place)
-    return place
-
-
-def finish_kernel(which, at, g, e, shrink, p_half, *refs):
-    n = len(which)
-    parts, (out, q_t) = refs[:n], refs[-2:]
-    shrink = shrink[0:1, 0:1]
-    step = pl.program_id(0)
-    first = place_of(which, step, at) * QUARTER
-    for k in range(n):
-
-        @pl.when(step == k)
-        def _(part=parts[k]):
-            for block in range(BLOCKS):
-                cols = slice(block * LANES, (block + 1) * LANES)
-                here = pl.ds(pl.multiple_of(first + block * LANES, LANES), LANES)
-                q = part[block]
-                approx = jnp.dot(p_half[...], q, preferred_element_type=f32)
-                merged = shrink * g[0, :, here].astype(f32) + e[0, :, here].astype(f32)
-                out[0, :, cols] = merged - approx
-                q_t[:, cols] = q.astype(f32)
-
-
-def finish(at, which, grads, error, shrink, p_half, parts, before=()):
+        place = (1 - core if other else core) * 4 + lax.rem(x + ahead, 4)
+        first = place * QUARTER
+        for block in range(BLOCKS):
+            cols = slice(block * LANES, (block + 1) * LANES)
+            here = pl.ds(pl.multiple_of(first + block * LANES, LANES), LANES)
+            q = parts[k][block]
+            approx = jnp.dot(p_half[...], q, preferred_element_type=f32)
+            merged = shrink * g[0, :, here].astype(f32) + e[0, :, here].astype(f32)
+            new[k, :, cols] = merged - approx
+            right_part[k, :, cols] = q.astype(f32)
+        cols = pl.ds(pl.multiple_of(first, LANES), QUARTER)
+        for j, rows in enumerate((slice(0, ROWS // 2), slice(ROWS // 2, ROWS))):
+            copies.append(
+                pltpu.make_async_copy(new.at[k, rows], out.at[0, rows, cols], sems.at[3 * k + j])
+            )
+        copies.append(pltpu.make_async_copy(right_part.at[k], q_t.at[:, cols], sems.at[3 * k + 2]))
+        for copy in copies[-3:]:
+            copy.start()
+    for copy in copies:
+        copy.wait()
+
+
+def finish(which, grads, error, shrink, p_half, parts, before=()):
     n = len(parts)
-    column = functools.partial(place_of, which)
+    hbm = pl.BlockSpec(memory_space=pltpu.HBM)
     return pl.pallas_call(
         functools.partial(finish_kernel, which),
-        grid_spec=pltpu.PrefetchScalarGridSpec(
-            num_scalar_prefetch=1,
-            grid=(n,),
-            in_specs=[whole()] * (4 + n) + [pl.BlockSpec(memory_space=pl.ANY)] * len(before),
-            out_specs=[
-                pl.BlockSpec((1, ROWS, QUARTER), lambda i, at: (0, 0, column(i, at))),
-                pl.BlockSpec((RANK, QUARTER), lambda i, at: (0, column(i, at))),
-            ],
-        ),
+        in_specs=[whole()] * (4 + n) + [hbm] * len(before),
+        out_specs=[hbm, hbm],
+        scratch_shapes=[
+            VMEM((n, ROWS, QUARTER), f32),
+            VMEM((n, RANK, QUARTER), f32),
+            pltpu.SemaphoreType.DMA((3 * n,)),
+        ],
         out_shape=[
             jax.ShapeDtypeStruct((1, ROWS, LOCAL), f32),
             jax.ShapeDtypeStruct((RANK, LOCAL), f32),
         ],
-        input_output_aliases={5 + n: 0, 6 + n: 1} if before else {},
+        input_output_aliases={4 + n: 0, 5 + n: 1} if before else {},
         name="finish",
         **room(12, 10**9),
-    )(at, grads, error, shrink, p_half, *parts, *before)
+    )(grads, error, shrink, p_half, *parts, *before)
 
 
 def respread_kernel(blocks, out):
@@ -456,13 +444,13 @@
 
 def step(grads, error, q_init):
     chip = ("x", "c", "y")
-    send, squares, q, at = prep(grads, error, q_init.T)
+    send, squares, q = prep(grads, error, q_init.T)
     got = swap(send, "c")
     squares = exchange(squares, chip)
-    *early, squares = merge(early_kernel, at, grads, error, got, squares, 2 * EARLY, (8,))
+    *early, squares = merge(early_kernel, grads, error, got, squares, 2 * EARLY, (8,))
     early = to_ring(early, "x")
     squares = exchange(squares, "z")
-    *late, shrink = merge(late_kernel, at, grads, error, got, squares, LATE, ())
+    *late, shrink = merge(late_kernel, grads, error, got, squares, LATE, ())
     late = to_ring(late, "x")
     early = fold(fold_early_kernel, EARLY, *early, shrink)
     early = exchange(early, "z")
@@ -477,9 +465,9 @@
     parts = from_ring(q, "x")
     others = [swap(part, "c") for part in parts]
     args = (grads, error, shrink, p_half)
-    outs = finish(at, [(0, 0), (1, 0)], *args, [parts[0], others[0]])
-    outs = finish(at, [(0, 1), (0, 2), (0, 3)], *args, parts[1:], outs)
-    new_error, q_t = finish(at, [(1, 1), (1, 2), (1, 3)], *args, others[1:], outs)
+    outs = finish([(0, 0), (1, 0)], *args, [parts[0], others[0]])
+    outs = finish([(0, 1), (0, 2), (0, 3)], *args, parts[1:], outs)
+    new_error, q_t = finish([(1, 1), (1, 2), (1, 3)], *args, others[1:], outs)
     return p_t.T, q_t.T, new_error
 
 

time: 157 us -> 154 us (0.981)
  Pallas kernels: 26.3 us -> 22.4 us
    pallas_call x5, Pallas kernels: 11.1 us -> 7.27 us  [the longest x3 5.21 us: finish(): pl.pallas_call(functools.partial(finish_kernel, which), in_specs=[whole()...]
  transfers between devices with their start and end apart: 15 -> 15, of which waited for: 3 -> 3; matrix products, arithmetic and copies ran while one was open for 0% -> 0% of each run, Pallas kernels for 5% -> 4%
where the time goes in v4:
time: 154 us; the launch traced here: 153 us
  blocking collectives  92.9 us (60%)
  starting transfers between devices  24.1 us (16%)
  Pallas kernels  22.4 us (15%)
  waiting for transfers between devices  12.7 us (8%)
    all_to_all x7, blocking collectives, exchange(): return lax.all_to_all(blocks, axis, 0, 0, tiled=True)  92.9 us
    ppermute x9, waiting for transfers between devices, shifted(): return lax.ppermute(value, axis, [(i, (i - by) % n) for i in range(n)])  12.7 us
    ppermute x9, starting transfers between devices, shifted(): return lax.ppermute(value, axis, [(i, (i - by) % n) for i in range(n)])  11 us
    ppermute x5, starting transfers between devices, swap(): return lax.ppermute(value, axis, [(0, 1), (1, 0)])  9.76 us
    pallas_call x1, Pallas kernels, factor(): pl.pallas_call(factor_kernel, in_specs=[whole()] * 2, out_specs=[whole()]...  8.61 us
    pallas_call x3, Pallas kernels, finish(): pl.pallas_call(functools.partial(finish_kernel, which), in_specs=[whole()...  5.21 us
    pallas_call x1, Pallas kernels, prep(): pl.pallas_call(prep_kernel, in_specs=[hbm, hbm, hbm], out_specs=[hbm, who...  3.83 us
    all_to_all x1, starting transfers between devices, exchange(): return lax.all_to_all(blocks, axis, 0, 0, tiled=True)  3.39 us
  transfers between devices with their start and end apart: 15, of which 3 were waited for; matrix products, arithmetic and copies ran while one was open for 0% of the time, Pallas kernels for 4%

profile of v4, /device:TPU:1, one launch (start us, length us, event | category | flops | bytes accessed | tf_op | source)
XLA Modules:
  0.0 153.1 jit_solution(14806006086425887311)
XLA Ops:
  0.6 0.0 copy-start
  0.6 0.0 copy-start.1
  0.7 3.8 %prep.1 = (bf16[320,3584]{1,0:T(8,128)(2,1)}, f32[32,8,128]{2,1,0:T(8,128)}, f32[64,128]{1,0:T(8,128)}) custom-call(bf16[1,160,7168]{2,1,0:T(8,128)(2,1)} %g.11, bf16[1,160,7168]{2,1,0:T(8,128)(2,1)} %e.11, f32[64,7168]{1,0:T(8,128)} %bitcast.4), custom_call_target="tpu_custom_call" | custom-call | flops 100000000 | bytes 1048576 | tf_op jit(solution)/shard_map/prep/pallas_call | solution.py:105
  4.5 3.3 %collective-permute-start = (bf16[320,3584]{1,0:T(8,128)(2,1)}, bf16[320,3584]{1,0:T(8,128)(2,1)S(1)}, u32[]{:S(2)}, u32[]{:S(2)}) collective-permute-start(bf16[320,3584]{1,0:T(8,128)(2,1)} %get-tuple-element.27), channel_id=1, source_target_pairs={{0,4},{4,0},{1,5},{5,1},{2,6},{6,2},{3,7},{7,3},{8,12},{12,8},{9,1... | collective-permute-start | bytes 6881288 | tf_op jit(solution)/shard_map/ppermute | solution.py:430
  7.8 13.1 %all_to_all.40.squares = f32[32,8,128]{2,1,0:T(8,128)S(1)} all-to-all(f32[32,8,128]{2,1,0:T(8,128)} %get-tuple-element.28), channel_id=1, replica_groups=mesh['z'=8,'x'=4,'c'=2,'y'=4] {'x','c','y'}, dimensions={0} | all-to-all | bytes 262144 | tf_op jit(solution)/shard_map/all_to_all | solution.py:434
  20.8 0.0 collective-permute-done.got
  20.8 0.0 copy-done
  20.8 0.0 copy-done.1
  20.8 0.3 shard_map.58
  21.1 0.5 collective-permute-start.1
  21.6 1.7 %collective-permute-start.2 = (f32[96,896]{1,0:T(8,128)S(1)}, f32[96,896]{1,0:T(8,128)S(1)}, u32[]{:S(2)}, u32[]{:S(2)}) collective-permute-start(f32[96,896]{1,0:T(8,128)S(1)} %get-tuple-element.31), channel_id=1, source_target_pairs={{0,16},{8,24},{16,0},{24,8},{1,17},{9,25},{17,1},{25,9},{2,18},{10... | collective-permute-start | bytes 1032200 | tf_op jit(solution)/shard_map/ppermute | solution.py:426
  23.3 1.0 collective-permute-start.3
  24.3 14.9 %all_to_all.41.squares = f32[8,8,128]{2,1,0:T(8,128)S(1)} all-to-all(f32[8,8,128]{2,1,0:T(8,128)S(1)} %get-tuple-element.33), channel_id=1, replica_groups=mesh['z'=8,'x'=4,'c'=2,'y'=4] {'z'}, dimensions={0} | all-to-all | bytes 65536 | tf_op jit(solution)/shard_map/all_to_all | solution.py:434
  39.2 1.8 %shard_map.59 = (f32[112,896]{1,0:T(8,128)S(1)}, f32[112,896]{1,0:T(8,128)}, f32[112,896]{1,0:T(8,128)}, f32[112,896]{1,0:T(8,128)}, f32[8,128]{1,0:T(8,128)S(1)}) custom-call(bf16[1,160,7168]{2,1,0:T(8,128)(2,1)S(1)} %copy-done, bf16[1,160,7168]{2,1,0:T(8,128)(2,1)S(1)} %copy-done.1, bf16[320,3584]{1,0:T(8,128)(2,1)S(1)} %collective-permute-done.got, ...), custom_call_target="tpu_custom_call" | custom-call | flops 1000000000 | bytes 1048576 | tf_op jit(solution)/shard_map/pallas_call | solution.py:169
  41.0 0.4 collective-permute-start.4
  41.4 1.6 %collective-permute-start.5 = (f32[112,896]{1,0:T(8,128)}, f32[112,896]{1,0:T(8,128)}, u32[]{:S(2)}, u32[]{:S(2)}) collective-permute-start(f32[112,896]{1,0:T(8,128)} %get-tuple-element.37), channel_id=1, source_target_pairs={{0,16},{8,24},{16,0},{24,8},{1,17},{9,25},{17,1},{25,9},{2,18},{10... | collective-permute-start | bytes 1204232 | tf_op jit(solution)/shard_map/ppermute | solution.py:426
  43.0 0.0 collective-permute-done.1.b
  43.0 2.1 %collective-permute-start.6 = (f32[112,896]{1,0:T(8,128)}, f32[112,896]{1,0:T(8,128)}, u32[]{:S(2)}, u32[]{:S(2)}) collective-permute-start(f32[112,896]{1,0:T(8,128)} %get-tuple-element.38), channel_id=1, source_target_pairs={{0,24},{8,0},{16,8},{24,16},{1,25},{9,1},{17,9},{25,17},{2,26},{10... | collective-permute-start | bytes 1204232 | tf_op jit(solution)/shard_map/ppermute | solution.py:426
  45.0 0.0 collective-permute-done.2.c
  45.0 0.0 collective-permute-done.3.d
  45.0 0.0 copy-start.3
  45.0 0.8 shard_map.60
  45.8 3.4 %all-to-all-start.2 = ((f32[8,48,128]{2,1,0:T(8,128)}), f32[8,48,128]{2,1,0:T(8,128)S(1)}, u32[]{:S(2)}, u32[]{:S(2)}) async-start(f32[8,48,128]{2,1,0:T(8,128)} %shard_map.60), calls=%async_computation.2 | async-start | bytes 393216 | tf_op jit(solution)/shard_map/all_to_all | solution.py:434
  49.2 1.9 %collective-permute-done.4.b = f32[112,896]{1,0:T(8,128)S(1)} collective-permute-done((f32[112,896]{1,0:T(8,128)}, f32[112,896]{1,0:T(8,128)S(1)}, u32[]{:S(2)}, u32[]{:S(2)}) %collective-permute-start.4) | collective-permute-done | bytes 401440 | tf_op jit(solution)/shard_map/ppermute | solution.py:426
  51.1 7.8 %collective-permute-done.5.c = f32[112,896]{1,0:T(8,128)} collective-permute-done((f32[112,896]{1,0:T(8,128)}, f32[112,896]{1,0:T(8,128)}, u32[]{:S(2)}, u32[]{:S(2)}) %collective-permute-start.5) | collective-permute-done | bytes 401440 | tf_op jit(solution)/shard_map/ppermute | solution.py:426
  58.9 3.0 %collective-permute-done.6.d = f32[112,896]{1,0:T(8,128)} collective-permute-done((f32[112,896]{1,0:T(8,128)}, f32[112,896]{1,0:T(8,128)}, u32[]{:S(2)}, u32[]{:S(2)}) %collective-permute-start.6) | collective-permute-done | bytes 401440 | tf_op jit(solution)/shard_map/ppermute | solution.py:426
  61.9 0.0 all-to-all-done.2.after.early
  61.9 0.0 copy-start.2
  61.9 1.4 shard_map.61
  63.3 16.4 %all_to_all.42.late = f32[8,112,128]{2,1,0:T(8,128)S(1)} all-to-all(f32[8,112,128]{2,1,0:T(8,128)S(1)} %shard_map.61), channel_id=1, replica_groups=mesh['z'=8,'x'=4,'c'=2,'y'=4] {'z'}, dimensions={0} | all-to-all | bytes 917504 | tf_op jit(solution)/shard_map/all_to_all | solution.py:434
  79.7 0.0 copy-done.3
  79.7 0.5 terms.1
  80.2 16.2 %all_to_all.43.blocks = f32[32,8,128]{2,1,0:T(8,128)S(1)} all-to-all(f32[32,8,128]{2,1,0:T(8,128)S(1)} %get-tuple-element.40), channel_id=1, replica_groups=mesh['z'=8,'x'=4,'c'=2,'y'=4] {'x','c','y'}, dimensions={0} | all-to-all | bytes 262144 | tf_op jit(solution)/shard_map/all_to_all | solution.py:434
  96.5 9.2 %all_to_all.44.blocks = f32[8,8,128]{2,1,0:T(8,128)S(1)} all-to-all(f32[8,8,128]{2,1,0:T(8,128)S(1)} %respread.2), channel_id=1, replica_groups=mesh['z'=8,'x'=4,'c'=2,'y'=4] {'z'}, dimensions={0} | all-to-all | bytes 65536 | tf_op jit(solution)/shard_map/all_to_all | solution.py:434
  105.7 12.5 %all_to_all.45.pack = f32[32,8,128]{2,1,0:T(8,128)S(1)} all-to-all(f32[32,8,128]{2,1,0:T(8,128)S(1)} %respread.3), channel_id=1, replica_groups=mesh['z'=8,'x'=4,'c'=2,'y'=4] {'x','c','y'}, dimensions={0} | all-to-all | bytes 262144 | tf_op jit(solution)/shard_map/all_to_all | solution.py:434
  118.3 8.6 %factor.1 = (f32[64,160]{1,0:T(8,128)}, bf16[160,64]{1,0:T(8,128)(2,1)S(1)}, bf16[8,64,128]{2,1,0:T(8,128)(2,1)S(1)}) custom-call(f32[32,8,128]{2,1,0:T(8,128)S(1)} %all_to_all.45.pack, f32[160,128]{1,0:T(8,128)S(1)} %get-tuple-element.41.s), custom_call_target="tpu_custom_call" | custom-call | flops 100000000 | bytes 1048576 | tf_op jit(solution)/shard_map/factor/pallas_call | solution.py:339
  126.9 10.5 %all_to_all.46.refs_0_ = bf16[8,64,128]{2,1,0:T(8,128)(2,1)S(1)} all-to-all(bf16[8,64,128]{2,1,0:T(8,128)(2,1)S(1)} %get-tuple-element.44), channel_id=1, replica_groups=mesh['z'=8,'x'=4,'c'=2,'y'=4] {'z'}, dimensions={0} | all-to-all | bytes 262144 | tf_op jit(solution)/shard_map/all_to_all | solution.py:434
  137.4 1.1 collective-permute-start.9
  138.5 0.6 collective-permute-start.11
  139.1 2.1 %collective-permute-start.7 = (bf16[8,64,128]{2,1,0:T(8,128)(2,1)S(1)}, bf16[8,64,128]{2,1,0:T(8,128)(2,1)S(1)}, u32[]{:S(2)}, u32[]{:S(2)}) collective-permute-start(bf16[8,64,128]{2,1,0:T(8,128)(2,1)S(1)} %all_to_all.46.refs_0_), channel_id=1, source_target_pairs={{0,24},{8,0},{16,8},{24,16},{1,25},{9,1},{17,9},{25,17},{2,26},{10... | collective-permute-start | bytes 393224 | tf_op jit(solution)/shard_map/ppermute | solution.py:426
  141.2 2.6 %collective-permute-start.13 = (bf16[8,64,128]{2,1,0:T(8,128)(2,1)S(1)}, bf16[8,64,128]{2,1,0:T(8,128)(2,1)S(1)}, u32[]{:S(2)}, u32[]{:S(2)}) collective-permute-start(bf16[8,64,128]{2,1,0:T(8,128)(2,1)S(1)} %all_to_all.46.refs_0_), channel_id=1, source_target_pairs={{0,4},{4,0},{1,5},{5,1},{2,6},{6,2},{3,7},{7,3},{8,12},{12,8},{9,1... | collective-permute-start | bytes 393224 | tf_op jit(solution)/shard_map/ppermute | solution.py:430
  143.8 0.0 collective-permute-done.9.refs_1_
  143.8 2.4 %collective-permute-start.10 = (bf16[8,64,128]{2,1,0:T(8,128)(2,1)S(1)}, bf16[8,64,128]{2,1,0:T(8,128)(2,1)S(1)}, u32[]{:S(2)}, u32[]{:S(2)}) collective-permute-start(bf16[8,64,128]{2,1,0:T(8,128)(2,1)S(1)} %collective-permute-done.9.refs_1_), channel_id=1, source_target_pairs={{0,4},{4,0},{1,5},{5,1},{2,6},{6,2},{3,7},{7,3},{8,12},{12,8},{9,1... | collective-permute-start | bytes 393224 | tf_op jit(solution)/shard_map/ppermute | solution.py:430
  146.2 0.0 collective-permute-done.11.refs_2_
  146.3 1.4 collective-permute-start.12
  147.7 0.0 collective-permute-done.7.refs_0_
  147.7 0.0 collective-permute-start.8
  147.7 0.0 collective-permute-done.13.refs_1_
  147.7 0.0 copy-done.2
  147.7 1.5 finish.3
  149.2 1.8 %finish.4 = (f32[1,160,7168]{2,1,0:T(8,128)}, f32[64,7168]{1,0:T(8,128)}) custom-call(bf16[1,160,7168]{2,1,0:T(8,128)(2,1)S(1)} %copy-done, bf16[1,160,7168]{2,1,0:T(8,128)(2,1)S(1)} %copy-done.2, f32[8,128]{1,0:T(8,128)S(1)} %get-tuple-element.34.shrink, ...), custom_call_target="tpu_custom_call", output_to_operand_aliasing={{0}: (7, {}), {1}: (8, {})} | custom-call | flops 1000000000 | bytes 1048576 | tf_op jit(solution)/shard_map/finish/pallas_call | solution.py:386
  151.1 0.0 collective-permute-done.10.refs_1_
  151.1 0.0 collective-permute-done.12.refs_2_
  151.1 0.0 collective-permute-done.8.refs_0_
  151.1 1.8 %finish.5 = (f32[1,160,7168]{2,1,0:T(8,128)}, f32[64,7168]{1,0:T(8,128)}) custom-call(bf16[1,160,7168]{2,1,0:T(8,128)(2,1)S(1)} %copy-done, bf16[1,160,7168]{2,1,0:T(8,128)(2,1)S(1)} %copy-done.2, f32[8,128]{1,0:T(8,128)S(1)} %get-tuple-element.34.shrink, ...), custom_call_target="tpu_custom_call", output_to_operand_aliasing={{0}: (7, {}), {1}: (8, {})} | custom-call | flops 1000000000 | bytes 1048576 | tf_op jit(solution)/shard_map/finish/pallas_call | solution.py:386
  (2 shorter events, 0.1 us)
Async XLA Ops:
  0.6 20.2 %copy-start = (bf16[1,160,7168]{2,1,0:T(8,128)(2,1)S(1)}, bf16[1,160,7168]{2,1,0:T(8,128)(2,1)}, u32[]{:S(2)}) copy-start(bf16[1,160,7168]{2,1,0:T(8,128)(2,1)} %g.11) | copy-start | bytes 6881284
  0.6 20.2 %copy-start.1 = (bf16[1,160,7168]{2,1,0:T(8,128)(2,1)S(1)}, bf16[1,160,7168]{2,1,0:T(8,128)(2,1)}, u32[]{:S(2)}) copy-start(bf16[1,160,7168]{2,1,0:T(8,128)(2,1)} %e.11) | copy-start | bytes 6881284
  4.5 16.3 %collective-permute-start = (bf16[320,3584]{1,0:T(8,128)(2,1)}, bf16[320,3584]{1,0:T(8,128)(2,1)S(1)}, u32[]{:S(2)}, u32[]{:S(2)}) collective-permute-start(bf16[320,3584]{1,0:T(8,128)(2,1)} %get-tuple-element.27), channel_id=1, source_target_pairs={{0,4},{4,0},{1,5},{5,1},{2,6},{6,2},{3,7},{7,3},{8,12},{12,8},{9,1... | collective-permute-start | bytes 6881288 | tf_op jit(solution)/shard_map/ppermute | solution.py:430
  21.1 21.8 %collective-permute-start.1 = (f32[96,896]{1,0:T(8,128)S(1)}, f32[96,896]{1,0:T(8,128)S(1)}, u32[]{:S(2)}, u32[]{:S(2)}) collective-permute-start(f32[96,896]{1,0:T(8,128)S(1)} %get-tuple-element.30), channel_id=1, source_target_pairs={{0,8},{8,16},{16,24},{24,0},{1,9},{9,17},{17,25},{25,1},{2,10},{10... | collective-permute-start | bytes 1032200 | tf_op jit(solution)/shard_map/ppermute | solution.py:426
  21.6 23.4 %collective-permute-start.2 = (f32[96,896]{1,0:T(8,128)S(1)}, f32[96,896]{1,0:T(8,128)S(1)}, u32[]{:S(2)}, u32[]{:S(2)}) collective-permute-start(f32[96,896]{1,0:T(8,128)S(1)} %get-tuple-element.31), channel_id=1, source_target_pairs={{0,16},{8,24},{16,0},{24,8},{1,17},{9,25},{17,1},{25,9},{2,18},{10... | collective-permute-start | bytes 1032200 | tf_op jit(solution)/shard_map/ppermute | solution.py:426
  23.3 21.7 %collective-permute-start.3 = (f32[96,896]{1,0:T(8,128)S(1)}, f32[96,896]{1,0:T(8,128)S(1)}, u32[]{:S(2)}, u32[]{:S(2)}) collective-permute-start(f32[96,896]{1,0:T(8,128)S(1)} %get-tuple-element.32), channel_id=1, source_target_pairs={{0,24},{8,0},{16,8},{24,16},{1,25},{9,1},{17,9},{25,17},{2,26},{10... | collective-permute-start | bytes 1032200 | tf_op jit(solution)/shard_map/ppermute | solution.py:426
  41.0 10.1 %collective-permute-start.4 = (f32[112,896]{1,0:T(8,128)}, f32[112,896]{1,0:T(8,128)S(1)}, u32[]{:S(2)}, u32[]{:S(2)}) collective-permute-start(f32[112,896]{1,0:T(8,128)} %get-tuple-element.36), channel_id=1, source_target_pairs={{0,8},{8,16},{16,24},{24,0},{1,9},{9,17},{17,25},{25,1},{2,10},{10... | collective-permute-start | bytes 1204232 | tf_op jit(solution)/shard_map/ppermute | solution.py:426
  41.4 17.5 %collective-permute-start.5 = (f32[112,896]{1,0:T(8,128)}, f32[112,896]{1,0:T(8,128)}, u32[]{:S(2)}, u32[]{:S(2)}) collective-permute-start(f32[112,896]{1,0:T(8,128)} %get-tuple-element.37), channel_id=1, source_target_pairs={{0,16},{8,24},{16,0},{24,8},{1,17},{9,25},{17,1},{25,9},{2,18},{10... | collective-permute-start | bytes 1204232 | tf_op jit(solution)/shard_map/ppermute | solution.py:426
  43.0 18.9 %collective-permute-start.6 = (f32[112,896]{1,0:T(8,128)}, f32[112,896]{1,0:T(8,128)}, u32[]{:S(2)}, u32[]{:S(2)}) collective-permute-start(f32[112,896]{1,0:T(8,128)} %get-tuple-element.38), channel_id=1, source_target_pairs={{0,24},{8,0},{16,8},{24,16},{1,25},{9,1},{17,9},{25,17},{2,26},{10... | collective-permute-start | bytes 1204232 | tf_op jit(solution)/shard_map/ppermute | solution.py:426
  45.0 34.7 %copy-start.3 = (f32[64,128]{1,0:T(8,128)S(1)}, f32[64,128]{1,0:T(8,128)}, u32[]{:S(2)}) copy-start(f32[64,128]{1,0:T(8,128)} %get-tuple-element.39.q) | copy-start | bytes 98308
  45.8 16.1 %all-to-all-start.2 = ((f32[8,48,128]{2,1,0:T(8,128)}), f32[8,48,128]{2,1,0:T(8,128)S(1)}, u32[]{:S(2)}, u32[]{:S(2)}) async-start(f32[8,48,128]{2,1,0:T(8,128)} %shard_map.60), calls=%async_computation.2 | async-start | bytes 393216 | tf_op jit(solution)/shard_map/all_to_all | solution.py:434
  61.9 85.8 %copy-start.2 = (bf16[1,160,7168]{2,1,0:T(8,128)(2,1)S(1)}, bf16[1,160,7168]{2,1,0:T(8,128)(2,1)}, u32[]{:S(2)}) copy-start(bf16[1,160,7168]{2,1,0:T(8,128)(2,1)} %e.11) | copy-start | bytes 6881284
  137.4 6.4 %collective-permute-start.9 = (bf16[8,64,128]{2,1,0:T(8,128)(2,1)S(1)}, bf16[8,64,128]{2,1,0:T(8,128)(2,1)S(1)}, u32[]{:S(2)}, u32[]{:S(2)}) collective-permute-start(bf16[8,64,128]{2,1,0:T(8,128)(2,1)S(1)} %all_to_all.46.refs_0_), channel_id=1, source_target_pairs={{0,16},{8,24},{16,0},{24,8},{1,17},{9,25},{17,1},{25,9},{2,18},{10... | collective-permute-start | bytes 393224 | tf_op jit(solution)/shard_map/ppermute | solution.py:426
  138.5 7.7 %collective-permute-start.11 = (bf16[8,64,128]{2,1,0:T(8,128)(2,1)S(1)}, bf16[8,64,128]{2,1,0:T(8,128)(2,1)S(1)}, u32[]{:S(2)}, u32[]{:S(2)}) collective-permute-start(bf16[8,64,128]{2,1,0:T(8,128)(2,1)S(1)} %all_to_all.46.refs_0_), channel_id=1, source_target_pairs={{0,8},{8,16},{16,24},{24,0},{1,9},{9,17},{17,25},{25,1},{2,10},{10... | collective-permute-start | bytes 393224 | tf_op jit(solution)/shard_map/ppermute | solution.py:426
  139.1 8.6 %collective-permute-start.7 = (bf16[8,64,128]{2,1,0:T(8,128)(2,1)S(1)}, bf16[8,64,128]{2,1,0:T(8,128)(2,1)S(1)}, u32[]{:S(2)}, u32[]{:S(2)}) collective-permute-start(bf16[8,64,128]{2,1,0:T(8,128)(2,1)S(1)} %all_to_all.46.refs_0_), channel_id=1, source_target_pairs={{0,24},{8,0},{16,8},{24,16},{1,25},{9,1},{17,9},{25,17},{2,26},{10... | collective-permute-start | bytes 393224 | tf_op jit(solution)/shard_map/ppermute | solution.py:426
  141.2 6.5 %collective-permute-start.13 = (bf16[8,64,128]{2,1,0:T(8,128)(2,1)S(1)}, bf16[8,64,128]{2,1,0:T(8,128)(2,1)S(1)}, u32[]{:S(2)}, u32[]{:S(2)}) collective-permute-start(bf16[8,64,128]{2,1,0:T(8,128)(2,1)S(1)} %all_to_all.46.refs_0_), channel_id=1, source_target_pairs={{0,4},{4,0},{1,5},{5,1},{2,6},{6,2},{3,7},{7,3},{8,12},{12,8},{9,1... | collective-permute-start | bytes 393224 | tf_op jit(solution)/shard_map/ppermute | solution.py:430
  143.8 7.2 %collective-permute-start.10 = (bf16[8,64,128]{2,1,0:T(8,128)(2,1)S(1)}, bf16[8,64,128]{2,1,0:T(8,128)(2,1)S(1)}, u32[]{:S(2)}, u32[]{:S(2)}) collective-permute-start(bf16[8,64,128]{2,1,0:T(8,128)(2,1)S(1)} %collective-permute-done.9.refs_1_), channel_id=1, source_target_pairs={{0,4},{4,0},{1,5},{5,1},{2,6},{6,2},{3,7},{7,3},{8,12},{12,8},{9,1... | collective-permute-start | bytes 393224 | tf_op jit(solution)/shard_map/ppermute | solution.py:430
  146.3 4.8 %collective-permute-start.12 = (bf16[8,64,128]{2,1,0:T(8,128)(2,1)S(1)}, bf16[8,64,128]{2,1,0:T(8,128)(2,1)S(1)}, u32[]{:S(2)}, u32[]{:S(2)}) collective-permute-start(bf16[8,64,128]{2,1,0:T(8,128)(2,1)S(1)} %collective-permute-done.11.refs_2_), channel_id=1, source_target_pairs={{0,4},{4,0},{1,5},{5,1},{2,6},{6,2},{3,7},{7,3},{8,12},{12,8},{9,1... | collective-permute-start | bytes 393224 | tf_op jit(solution)/shard_map/ppermute | solution.py:430
  147.7 3.4 %collective-permute-start.8 = (bf16[8,64,128]{2,1,0:T(8,128)(2,1)S(1)}, bf16[8,64,128]{2,1,0:T(8,128)(2,1)S(1)}, u32[]{:S(2)}, u32[]{:S(2)}) collective-permute-start(bf16[8,64,128]{2,1,0:T(8,128)(2,1)S(1)} %collective-permute-done.7.refs_0_), channel_id=1, source_target_pairs={{0,4},{4,0},{1,5},{5,1},{2,6},{6,2},{3,7},{7,3},{8,12},{12,8},{9,1... | collective-permute-start | bytes 393224 | tf_op jit(solution)/shard_map/ppermute | solution.py:430

commit v5 on v4

--- a/solution.py
+++ b/solution.py
@@ -327,8 +327,8 @@
     p_t[:, LANES:ROWS] = b[:, 0:TAIL]
     a = a.astype(bf16).astype(f32)
     b = b.astype(bf16).astype(f32)
-    p_half[0:LANES, :] = a.T.astype(bf16)
-    p_half[LANES:ROWS, :] = b.T[0:TAIL].astype(bf16)
+    p_half[:, 0:LANES] = a.astype(bf16)
+    p_half[:, LANES:ROWS] = b[:, 0:TAIL].astype(bf16)
     tail_full = jnp.concatenate([s[LANES:ROWS], empty], axis=0)
     columns = ((dot(a, s[0:LANES]) + dot(b, tail_full)) * (1.0 / REPLICAS)).astype(q.dtype)
     for k in range(8):
@@ -342,7 +342,7 @@
         out_specs=[whole()] * 3,
         out_shape=[
             jax.ShapeDtypeStruct((RANK, ROWS), f32),
-            jax.ShapeDtypeStruct((ROWS, RANK), bf16),
+            jax.ShapeDtypeStruct((RANK, ROWS), bf16),
             jax.ShapeDtypeStruct((8, RANK, LANES), bf16),
         ],
         name="factor",
@@ -356,6 +356,7 @@
     out, q_t, new, right_part, sems = refs[-5:]
     shrink = shrink[0:1, 0:1]
     core, x = lax.axis_index("c"), lax.axis_index("x")
+    left = p_half[...].astype(f32).T.astype(bf16)
     copies = []
     for k, (other, ahead) in enumerate(which):
         place = (1 - core if other else core) * 4 + lax.rem(x + ahead, 4)
@@ -364,7 +365,7 @@
             cols = slice(block * LANES, (block + 1) * LANES)
             here = pl.ds(pl.multiple_of(first + block * LANES, LANES), LANES)
             q = parts[k][block]
-            approx = jnp.dot(p_half[...], q, preferred_element_type=f32)
+            approx = jnp.dot(left, q, preferred_element_type=f32)
             merged = shrink * g[0, :, here].astype(f32) + e[0, :, here].astype(f32)
             new[k, :, cols] = merged - approx
             right_part[k, :, cols] = q.astype(f32)

time: 154 us -> 154 us (level)
  no operation moved by 1% of the time
where the time goes in v5:
time: 154 us; the launch traced here: 153 us
  blocking collectives  92.9 us (60%)
  starting transfers between devices  24.1 us (16%)
  Pallas kernels  22.7 us (15%)
  waiting for transfers between devices  12.7 us (8%)
    all_to_all x7, blocking collectives, exchange(): return lax.all_to_all(blocks, axis, 0, 0, tiled=True)  92.9 us
    ppermute x9, waiting for transfers between devices, shifted(): return lax.ppermute(value, axis, [(i, (i - by) % n) for i in range(n)])  12.7 us
    ppermute x9, starting transfers between devices, shifted(): return lax.ppermute(value, axis, [(i, (i - by) % n) for i in range(n)])  11 us
    ppermute x5, starting transfers between devices, swap(): return lax.ppermute(value, axis, [(0, 1), (1, 0)])  9.76 us
    pallas_call x1, Pallas kernels, factor(): pl.pallas_call(factor_kernel, in_specs=[whole()] * 2, out_specs=[whole()]...  8.62 us
    pallas_call x3, Pallas kernels, finish(): pl.pallas_call(functools.partial(finish_kernel, which), in_specs=[whole()...  5.45 us
    pallas_call x1, Pallas kernels, prep(): pl.pallas_call(prep_kernel, in_specs=[hbm, hbm, hbm], out_specs=[hbm, who...  3.83 us
    all_to_all x1, starting transfers between devices, exchange(): return lax.all_to_all(blocks, axis, 0, 0, tiled=True)  3.39 us
  transfers between devices with their start and end apart: 15, of which 3 were waited for; matrix products, arithmetic and copies ran while one was open for 0% of the time, Pallas kernels for 4%

profile of v5, /device:TPU:1, one launch (start us, length us, event | category | flops | bytes accessed | tf_op | source)
XLA Modules:
  0.0 153.3 jit_solution(2364865114804801523)
XLA Ops:
  0.6 0.0 copy-start
  0.6 0.0 copy-start.1
  0.7 3.8 %prep.1 = (bf16[320,3584]{1,0:T(8,128)(2,1)}, f32[32,8,128]{2,1,0:T(8,128)}, f32[64,128]{1,0:T(8,128)}) custom-call(bf16[1,160,7168]{2,1,0:T(8,128)(2,1)} %g.11, bf16[1,160,7168]{2,1,0:T(8,128)(2,1)} %e.11, f32[64,7168]{1,0:T(8,128)} %bitcast.4), custom_call_target="tpu_custom_call" | custom-call | flops 100000000 | bytes 1048576 | tf_op jit(solution)/shard_map/prep/pallas_call | solution.py:105
  4.5 3.3 %collective-permute-start = (bf16[320,3584]{1,0:T(8,128)(2,1)}, bf16[320,3584]{1,0:T(8,128)(2,1)S(1)}, u32[]{:S(2)}, u32[]{:S(2)}) collective-permute-start(bf16[320,3584]{1,0:T(8,128)(2,1)} %get-tuple-element.27), channel_id=1, source_target_pairs={{0,4},{4,0},{1,5},{5,1},{2,6},{6,2},{3,7},{7,3},{8,12},{12,8},{9,1... | collective-permute-start | bytes 6881288 | tf_op jit(solution)/shard_map/ppermute | solution.py:431
  7.8 13.1 %all_to_all.40.squares = f32[32,8,128]{2,1,0:T(8,128)S(1)} all-to-all(f32[32,8,128]{2,1,0:T(8,128)} %get-tuple-element.28), channel_id=1, replica_groups=mesh['z'=8,'x'=4,'c'=2,'y'=4] {'x','c','y'}, dimensions={0} | all-to-all | bytes 262144 | tf_op jit(solution)/shard_map/all_to_all | solution.py:435
  20.8 0.0 collective-permute-done.got
  20.8 0.0 copy-done
  20.8 0.0 copy-done.1
  20.8 0.3 shard_map.58
  21.1 0.5 collective-permute-start.1
  21.6 1.7 %collective-permute-start.2 = (f32[96,896]{1,0:T(8,128)S(1)}, f32[96,896]{1,0:T(8,128)S(1)}, u32[]{:S(2)}, u32[]{:S(2)}) collective-permute-start(f32[96,896]{1,0:T(8,128)S(1)} %get-tuple-element.31), channel_id=1, source_target_pairs={{0,16},{8,24},{16,0},{24,8},{1,17},{9,25},{17,1},{25,9},{2,18},{10... | collective-permute-start | bytes 1032200 | tf_op jit(solution)/shard_map/ppermute | solution.py:427
  23.3 1.0 collective-permute-start.3
  24.3 14.9 %all_to_all.41.squares = f32[8,8,128]{2,1,0:T(8,128)S(1)} all-to-all(f32[8,8,128]{2,1,0:T(8,128)S(1)} %get-tuple-element.33), channel_id=1, replica_groups=mesh['z'=8,'x'=4,'c'=2,'y'=4] {'z'}, dimensions={0} | all-to-all | bytes 65536 | tf_op jit(solution)/shard_map/all_to_all | solution.py:435
  39.2 1.8 %shard_map.59 = (f32[112,896]{1,0:T(8,128)S(1)}, f32[112,896]{1,0:T(8,128)}, f32[112,896]{1,0:T(8,128)}, f32[112,896]{1,0:T(8,128)}, f32[8,128]{1,0:T(8,128)S(1)}) custom-call(bf16[1,160,7168]{2,1,0:T(8,128)(2,1)S(1)} %copy-done, bf16[1,160,7168]{2,1,0:T(8,128)(2,1)S(1)} %copy-done.1, bf16[320,3584]{1,0:T(8,128)(2,1)S(1)} %collective-permute-done.got, ...), custom_call_target="tpu_custom_call" | custom-call | flops 1000000000 | bytes 1048576 | tf_op jit(solution)/shard_map/pallas_call | solution.py:169
  41.0 0.4 collective-permute-start.4
  41.4 1.6 %collective-permute-start.5 = (f32[112,896]{1,0:T(8,128)}, f32[112,896]{1,0:T(8,128)}, u32[]{:S(2)}, u32[]{:S(2)}) collective-permute-start(f32[112,896]{1,0:T(8,128)} %get-tuple-element.37), channel_id=1, source_target_pairs={{0,16},{8,24},{16,0},{24,8},{1,17},{9,25},{17,1},{25,9},{2,18},{10... | collective-permute-start | bytes 1204232 | tf_op jit(solution)/shard_map/ppermute | solution.py:427
  43.0 0.0 collective-permute-done.1.b
  43.0 2.1 %collective-permute-start.6 = (f32[112,896]{1,0:T(8,128)}, f32[112,896]{1,0:T(8,128)}, u32[]{:S(2)}, u32[]{:S(2)}) collective-permute-start(f32[112,896]{1,0:T(8,128)} %get-tuple-element.38), channel_id=1, source_target_pairs={{0,24},{8,0},{16,8},{24,16},{1,25},{9,1},{17,9},{25,17},{2,26},{10... | collective-permute-start | bytes 1204232 | tf_op jit(solution)/shard_map/ppermute | solution.py:427
  45.0 0.0 collective-permute-done.2.c
  45.0 0.0 collective-permute-done.3.d
  45.0 0.0 copy-start.3
  45.0 0.8 shard_map.60
  45.8 3.4 %all-to-all-start.2 = ((f32[8,48,128]{2,1,0:T(8,128)}), f32[8,48,128]{2,1,0:T(8,128)S(1)}, u32[]{:S(2)}, u32[]{:S(2)}) async-start(f32[8,48,128]{2,1,0:T(8,128)} %shard_map.60), calls=%async_computation.2 | async-start | bytes 393216 | tf_op jit(solution)/shard_map/all_to_all | solution.py:435
  49.2 1.9 %collective-permute-done.4.b = f32[112,896]{1,0:T(8,128)S(1)} collective-permute-done((f32[112,896]{1,0:T(8,128)}, f32[112,896]{1,0:T(8,128)S(1)}, u32[]{:S(2)}, u32[]{:S(2)}) %collective-permute-start.4) | collective-permute-done | bytes 401440 | tf_op jit(solution)/shard_map/ppermute | solution.py:427
  51.1 7.8 %collective-permute-done.5.c = f32[112,896]{1,0:T(8,128)} collective-permute-done((f32[112,896]{1,0:T(8,128)}, f32[112,896]{1,0:T(8,128)}, u32[]{:S(2)}, u32[]{:S(2)}) %collective-permute-start.5) | collective-permute-done | bytes 401440 | tf_op jit(solution)/shard_map/ppermute | solution.py:427
  58.9 3.0 %collective-permute-done.6.d = f32[112,896]{1,0:T(8,128)} collective-permute-done((f32[112,896]{1,0:T(8,128)}, f32[112,896]{1,0:T(8,128)}, u32[]{:S(2)}, u32[]{:S(2)}) %collective-permute-start.6) | collective-permute-done | bytes 401440 | tf_op jit(solution)/shard_map/ppermute | solution.py:427
  61.9 0.0 all-to-all-done.2.after.early
  61.9 0.0 copy-start.2
  61.9 1.4 shard_map.61
  63.3 16.4 %all_to_all.42.late = f32[8,112,128]{2,1,0:T(8,128)S(1)} all-to-all(f32[8,112,128]{2,1,0:T(8,128)S(1)} %shard_map.61), channel_id=1, replica_groups=mesh['z'=8,'x'=4,'c'=2,'y'=4] {'z'}, dimensions={0} | all-to-all | bytes 917504 | tf_op jit(solution)/shard_map/all_to_all | solution.py:435
  79.7 0.0 copy-done.3
  79.7 0.5 terms.1
  80.2 16.2 %all_to_all.43.blocks = f32[32,8,128]{2,1,0:T(8,128)S(1)} all-to-all(f32[32,8,128]{2,1,0:T(8,128)S(1)} %get-tuple-element.40), channel_id=1, replica_groups=mesh['z'=8,'x'=4,'c'=2,'y'=4] {'x','c','y'}, dimensions={0} | all-to-all | bytes 262144 | tf_op jit(solution)/shard_map/all_to_all | solution.py:435
  96.5 9.2 %all_to_all.44.blocks = f32[8,8,128]{2,1,0:T(8,128)S(1)} all-to-all(f32[8,8,128]{2,1,0:T(8,128)S(1)} %respread.2), channel_id=1, replica_groups=mesh['z'=8,'x'=4,'c'=2,'y'=4] {'z'}, dimensions={0} | all-to-all | bytes 65536 | tf_op jit(solution)/shard_map/all_to_all | solution.py:435
  105.7 12.5 %all_to_all.45.pack = f32[32,8,128]{2,1,0:T(8,128)S(1)} all-to-all(f32[32,8,128]{2,1,0:T(8,128)S(1)} %respread.3), channel_id=1, replica_groups=mesh['z'=8,'x'=4,'c'=2,'y'=4] {'x','c','y'}, dimensions={0} | all-to-all | bytes 262144 | tf_op jit(solution)/shard_map/all_to_all | solution.py:435
  118.3 8.6 %factor.1 = (f32[64,160]{1,0:T(8,128)}, bf16[64,160]{1,0:T(8,128)(2,1)S(1)}, bf16[8,64,128]{2,1,0:T(8,128)(2,1)S(1)}) custom-call(f32[32,8,128]{2,1,0:T(8,128)S(1)} %all_to_all.45.pack, f32[160,128]{1,0:T(8,128)S(1)} %get-tuple-element.41.s), custom_call_target="tpu_custom_call" | custom-call | flops 100000000 | bytes 1048576 | tf_op jit(solution)/shard_map/factor/pallas_call | solution.py:339
  126.9 10.5 %all_to_all.46.refs_0_ = bf16[8,64,128]{2,1,0:T(8,128)(2,1)S(1)} all-to-all(bf16[8,64,128]{2,1,0:T(8,128)(2,1)S(1)} %get-tuple-element.44), channel_id=1, replica_groups=mesh['z'=8,'x'=4,'c'=2,'y'=4] {'z'}, dimensions={0} | all-to-all | bytes 262144 | tf_op jit(solution)/shard_map/all_to_all | solution.py:435
  137.4 1.1 collective-permute-start.9
  138.5 0.6 collective-permute-start.11
  139.1 2.1 %collective-permute-start.7 = (bf16[8,64,128]{2,1,0:T(8,128)(2,1)S(1)}, bf16[8,64,128]{2,1,0:T(8,128)(2,1)S(1)}, u32[]{:S(2)}, u32[]{:S(2)}) collective-permute-start(bf16[8,64,128]{2,1,0:T(8,128)(2,1)S(1)} %all_to_all.46.refs_0_), channel_id=1, source_target_pairs={{0,24},{8,0},{16,8},{24,16},{1,25},{9,1},{17,9},{25,17},{2,26},{10... | collective-permute-start | bytes 393224 | tf_op jit(solution)/shard_map/ppermute | solution.py:427
  141.2 2.6 %collective-permute-start.13 = (bf16[8,64,128]{2,1,0:T(8,128)(2,1)S(1)}, bf16[8,64,128]{2,1,0:T(8,128)(2,1)S(1)}, u32[]{:S(2)}, u32[]{:S(2)}) collective-permute-start(bf16[8,64,128]{2,1,0:T(8,128)(2,1)S(1)} %all_to_all.46.refs_0_), channel_id=1, source_target_pairs={{0,4},{4,0},{1,5},{5,1},{2,6},{6,2},{3,7},{7,3},{8,12},{12,8},{9,1... | collective-permute-start | bytes 393224 | tf_op jit(solution)/shard_map/ppermute | solution.py:431
  143.8 0.0 collective-permute-done.9.refs_1_
  143.8 2.4 %collective-permute-start.10 = (bf16[8,64,128]{2,1,0:T(8,128)(2,1)S(1)}, bf16[8,64,128]{2,1,0:T(8,128)(2,1)S(1)}, u32[]{:S(2)}, u32[]{:S(2)}) collective-permute-start(bf16[8,64,128]{2,1,0:T(8,128)(2,1)S(1)} %collective-permute-done.9.refs_1_), channel_id=1, source_target_pairs={{0,4},{4,0},{1,5},{5,1},{2,6},{6,2},{3,7},{7,3},{8,12},{12,8},{9,1... | collective-permute-start | bytes 393224 | tf_op jit(solution)/shard_map/ppermute | solution.py:431
  146.3 0.0 collective-permute-done.11.refs_2_
  146.3 1.4 collective-permute-start.12
  147.7 0.0 collective-permute-done.7.refs_0_
  147.7 0.0 collective-permute-start.8
  147.7 0.0 collective-permute-done.13.refs_1_
  147.7 0.0 copy-done.2
  147.7 1.6 %finish.3 = (f32[1,160,7168]{2,1,0:T(8,128)}, f32[64,7168]{1,0:T(8,128)}) custom-call(bf16[1,160,7168]{2,1,0:T(8,128)(2,1)S(1)} %copy-done, bf16[1,160,7168]{2,1,0:T(8,128)(2,1)S(1)} %copy-done.2, f32[8,128]{1,0:T(8,128)S(1)} %get-tuple-element.34.shrink, bf16[64,160]{1,0:T(8,128)(2,1)S(1)} %get-tuple-element.43.p_half, ...), custom_call_target="tpu_custom_call" | custom-call | flops 1000000000 | bytes 1048576 | tf_op jit(solution)/shard_map/finish/pallas_call | solution.py:387
  149.3 1.9 %finish.4 = (f32[1,160,7168]{2,1,0:T(8,128)}, f32[64,7168]{1,0:T(8,128)}) custom-call(bf16[1,160,7168]{2,1,0:T(8,128)(2,1)S(1)} %copy-done, bf16[1,160,7168]{2,1,0:T(8,128)(2,1)S(1)} %copy-done.2, f32[8,128]{1,0:T(8,128)S(1)} %get-tuple-element.34.shrink, ...), custom_call_target="tpu_custom_call", output_to_operand_aliasing={{0}: (7, {}), {1}: (8, {})} | custom-call | flops 1000000000 | bytes 1048576 | tf_op jit(solution)/shard_map/finish/pallas_call | solution.py:387
  151.2 0.0 collective-permute-done.10.refs_1_
  151.2 0.0 collective-permute-done.12.refs_2_
  151.3 0.0 collective-permute-done.8.refs_0_
  151.3 1.9 %finish.5 = (f32[1,160,7168]{2,1,0:T(8,128)}, f32[64,7168]{1,0:T(8,128)}) custom-call(bf16[1,160,7168]{2,1,0:T(8,128)(2,1)S(1)} %copy-done, bf16[1,160,7168]{2,1,0:T(8,128)(2,1)S(1)} %copy-done.2, f32[8,128]{1,0:T(8,128)S(1)} %get-tuple-element.34.shrink, ...), custom_call_target="tpu_custom_call", output_to_operand_aliasing={{0}: (7, {}), {1}: (8, {})} | custom-call | flops 1000000000 | bytes 1048576 | tf_op jit(solution)/shard_map/finish/pallas_call | solution.py:387
  (2 shorter events, 0.1 us)
Async XLA Ops:
  0.6 20.2 %copy-start = (bf16[1,160,7168]{2,1,0:T(8,128)(2,1)S(1)}, bf16[1,160,7168]{2,1,0:T(8,128)(2,1)}, u32[]{:S(2)}) copy-start(bf16[1,160,7168]{2,1,0:T(8,128)(2,1)} %g.11) | copy-start | bytes 6881284
  0.6 20.2 %copy-start.1 = (bf16[1,160,7168]{2,1,0:T(8,128)(2,1)S(1)}, bf16[1,160,7168]{2,1,0:T(8,128)(2,1)}, u32[]{:S(2)}) copy-start(bf16[1,160,7168]{2,1,0:T(8,128)(2,1)} %e.11) | copy-start | bytes 6881284
  4.5 16.3 %collective-permute-start = (bf16[320,3584]{1,0:T(8,128)(2,1)}, bf16[320,3584]{1,0:T(8,128)(2,1)S(1)}, u32[]{:S(2)}, u32[]{:S(2)}) collective-permute-start(bf16[320,3584]{1,0:T(8,128)(2,1)} %get-tuple-element.27), channel_id=1, source_target_pairs={{0,4},{4,0},{1,5},{5,1},{2,6},{6,2},{3,7},{7,3},{8,12},{12,8},{9,1... | collective-permute-start | bytes 6881288 | tf_op jit(solution)/shard_map/ppermute | solution.py:431
  21.1 21.8 %collective-permute-start.1 = (f32[96,896]{1,0:T(8,128)S(1)}, f32[96,896]{1,0:T(8,128)S(1)}, u32[]{:S(2)}, u32[]{:S(2)}) collective-permute-start(f32[96,896]{1,0:T(8,128)S(1)} %get-tuple-element.30), channel_id=1, source_target_pairs={{0,8},{8,16},{16,24},{24,0},{1,9},{9,17},{17,25},{25,1},{2,10},{10... | collective-permute-start | bytes 1032200 | tf_op jit(solution)/shard_map/ppermute | solution.py:427
  21.6 23.4 %collective-permute-start.2 = (f32[96,896]{1,0:T(8,128)S(1)}, f32[96,896]{1,0:T(8,128)S(1)}, u32[]{:S(2)}, u32[]{:S(2)}) collective-permute-start(f32[96,896]{1,0:T(8,128)S(1)} %get-tuple-element.31), channel_id=1, source_target_pairs={{0,16},{8,24},{16,0},{24,8},{1,17},{9,25},{17,1},{25,9},{2,18},{10... | collective-permute-start | bytes 1032200 | tf_op jit(solution)/shard_map/ppermute | solution.py:427
  23.3 21.7 %collective-permute-start.3 = (f32[96,896]{1,0:T(8,128)S(1)}, f32[96,896]{1,0:T(8,128)S(1)}, u32[]{:S(2)}, u32[]{:S(2)}) collective-permute-start(f32[96,896]{1,0:T(8,128)S(1)} %get-tuple-element.32), channel_id=1, source_target_pairs={{0,24},{8,0},{16,8},{24,16},{1,25},{9,1},{17,9},{25,17},{2,26},{10... | collective-permute-start | bytes 1032200 | tf_op jit(solution)/shard_map/ppermute | solution.py:427
  41.0 10.1 %collective-permute-start.4 = (f32[112,896]{1,0:T(8,128)}, f32[112,896]{1,0:T(8,128)S(1)}, u32[]{:S(2)}, u32[]{:S(2)}) collective-permute-start(f32[112,896]{1,0:T(8,128)} %get-tuple-element.36), channel_id=1, source_target_pairs={{0,8},{8,16},{16,24},{24,0},{1,9},{9,17},{17,25},{25,1},{2,10},{10... | collective-permute-start | bytes 1204232 | tf_op jit(solution)/shard_map/ppermute | solution.py:427
  41.4 17.5 %collective-permute-start.5 = (f32[112,896]{1,0:T(8,128)}, f32[112,896]{1,0:T(8,128)}, u32[]{:S(2)}, u32[]{:S(2)}) collective-permute-start(f32[112,896]{1,0:T(8,128)} %get-tuple-element.37), channel_id=1, source_target_pairs={{0,16},{8,24},{16,0},{24,8},{1,17},{9,25},{17,1},{25,9},{2,18},{10... | collective-permute-start | bytes 1204232 | tf_op jit(solution)/shard_map/ppermute | solution.py:427
  43.0 18.9 %collective-permute-start.6 = (f32[112,896]{1,0:T(8,128)}, f32[112,896]{1,0:T(8,128)}, u32[]{:S(2)}, u32[]{:S(2)}) collective-permute-start(f32[112,896]{1,0:T(8,128)} %get-tuple-element.38), channel_id=1, source_target_pairs={{0,24},{8,0},{16,8},{24,16},{1,25},{9,1},{17,9},{25,17},{2,26},{10... | collective-permute-start | bytes 1204232 | tf_op jit(solution)/shard_map/ppermute | solution.py:427
  45.0 34.7 %copy-start.3 = (f32[64,128]{1,0:T(8,128)S(1)}, f32[64,128]{1,0:T(8,128)}, u32[]{:S(2)}) copy-start(f32[64,128]{1,0:T(8,128)} %get-tuple-element.39.q) | copy-start | bytes 98308
  45.8 16.1 %all-to-all-start.2 = ((f32[8,48,128]{2,1,0:T(8,128)}), f32[8,48,128]{2,1,0:T(8,128)S(1)}, u32[]{:S(2)}, u32[]{:S(2)}) async-start(f32[8,48,128]{2,1,0:T(8,128)} %shard_map.60), calls=%async_computation.2 | async-start | bytes 393216 | tf_op jit(solution)/shard_map/all_to_all | solution.py:435
  61.9 85.8 %copy-start.2 = (bf16[1,160,7168]{2,1,0:T(8,128)(2,1)S(1)}, bf16[1,160,7168]{2,1,0:T(8,128)(2,1)}, u32[]{:S(2)}) copy-start(bf16[1,160,7168]{2,1,0:T(8,128)(2,1)} %e.11) | copy-start | bytes 6881284
  137.4 6.4 %collective-permute-start.9 = (bf16[8,64,128]{2,1,0:T(8,128)(2,1)S(1)}, bf16[8,64,128]{2,1,0:T(8,128)(2,1)S(1)}, u32[]{:S(2)}, u32[]{:S(2)}) collective-permute-start(bf16[8,64,128]{2,1,0:T(8,128)(2,1)S(1)} %all_to_all.46.refs_0_), channel_id=1, source_target_pairs={{0,16},{8,24},{16,0},{24,8},{1,17},{9,25},{17,1},{25,9},{2,18},{10... | collective-permute-start | bytes 393224 | tf_op jit(solution)/shard_map/ppermute | solution.py:427
  138.5 7.7 %collective-permute-start.11 = (bf16[8,64,128]{2,1,0:T(8,128)(2,1)S(1)}, bf16[8,64,128]{2,1,0:T(8,128)(2,1)S(1)}, u32[]{:S(2)}, u32[]{:S(2)}) collective-permute-start(bf16[8,64,128]{2,1,0:T(8,128)(2,1)S(1)} %all_to_all.46.refs_0_), channel_id=1, source_target_pairs={{0,8},{8,16},{16,24},{24,0},{1,9},{9,17},{17,25},{25,1},{2,10},{10... | collective-permute-start | bytes 393224 | tf_op jit(solution)/shard_map/ppermute | solution.py:427
  139.1 8.6 %collective-permute-start.7 = (bf16[8,64,128]{2,1,0:T(8,128)(2,1)S(1)}, bf16[8,64,128]{2,1,0:T(8,128)(2,1)S(1)}, u32[]{:S(2)}, u32[]{:S(2)}) collective-permute-start(bf16[8,64,128]{2,1,0:T(8,128)(2,1)S(1)} %all_to_all.46.refs_0_), channel_id=1, source_target_pairs={{0,24},{8,0},{16,8},{24,16},{1,25},{9,1},{17,9},{25,17},{2,26},{10... | collective-permute-start | bytes 393224 | tf_op jit(solution)/shard_map/ppermute | solution.py:427
  141.2 6.5 %collective-permute-start.13 = (bf16[8,64,128]{2,1,0:T(8,128)(2,1)S(1)}, bf16[8,64,128]{2,1,0:T(8,128)(2,1)S(1)}, u32[]{:S(2)}, u32[]{:S(2)}) collective-permute-start(bf16[8,64,128]{2,1,0:T(8,128)(2,1)S(1)} %all_to_all.46.refs_0_), channel_id=1, source_target_pairs={{0,4},{4,0},{1,5},{5,1},{2,6},{6,2},{3,7},{7,3},{8,12},{12,8},{9,1... | collective-permute-start | bytes 393224 | tf_op jit(solution)/shard_map/ppermute | solution.py:431
  143.8 7.4 %collective-permute-start.10 = (bf16[8,64,128]{2,1,0:T(8,128)(2,1)S(1)}, bf16[8,64,128]{2,1,0:T(8,128)(2,1)S(1)}, u32[]{:S(2)}, u32[]{:S(2)}) collective-permute-start(bf16[8,64,128]{2,1,0:T(8,128)(2,1)S(1)} %collective-permute-done.9.refs_1_), channel_id=1, source_target_pairs={{0,4},{4,0},{1,5},{5,1},{2,6},{6,2},{3,7},{7,3},{8,12},{12,8},{9,1... | collective-permute-start | bytes 393224 | tf_op jit(solution)/shard_map/ppermute | solution.py:431
  146.3 5.0 %collective-permute-start.12 = (bf16[8,64,128]{2,1,0:T(8,128)(2,1)S(1)}, bf16[8,64,128]{2,1,0:T(8,128)(2,1)S(1)}, u32[]{:S(2)}, u32[]{:S(2)}) collective-permute-start(bf16[8,64,128]{2,1,0:T(8,128)(2,1)S(1)} %collective-permute-done.11.refs_2_), channel_id=1, source_target_pairs={{0,4},{4,0},{1,5},{5,1},{2,6},{6,2},{3,7},{7,3},{8,12},{12,8},{9,1... | collective-permute-start | bytes 393224 | tf_op jit(solution)/shard_map/ppermute | solution.py:431
  147.7 3.6 %collective-permute-start.8 = (bf16[8,64,128]{2,1,0:T(8,128)(2,1)S(1)}, bf16[8,64,128]{2,1,0:T(8,128)(2,1)S(1)}, u32[]{:S(2)}, u32[]{:S(2)}) collective-permute-start(bf16[8,64,128]{2,1,0:T(8,128)(2,1)S(1)} %collective-permute-done.7.refs_0_), channel_id=1, source_target_pairs={{0,4},{4,0},{1,5},{5,1},{2,6},{6,2},{3,7},{7,3},{8,12},{12,8},{9,1... | collective-permute-start | bytes 393224 | tf_op jit(solution)/shard_map/ppermute | solution.py:431
